TPU v7x, 32 devices: a whole 2x2x4 slice. The times are simulated.
32 devices in a mesh: span: 4 (over z), head: 4 (over y, x), group: 2 (over core).
Axes of the slice: x: 2, y: 2, z: 4, core: 2. Of those that a mesh axis runs over, the one named last changes fastest.
Arguments:
- states: bfloat16 [4096, 4096], P(('span', 'group'), 'head'), may hold values from -6 to 6
- owners: int32 [64, 2], P(('span', 'group')), may hold values from 0 to 3, as said below
- places: int32 [64, 2], P(('span', 'group')), may hold values from 0 to 7, as said below
- stored: bfloat16 [4, 4, 2, 8, 128, 896], P('span', 'head', 'group'), may hold values from -6 to 6
- encoder_weights: bfloat16 [896, 5376], P(('span', 'group')), may hold values from -0.1875 to 0.1875
- context_weight: bfloat16 [4096, 1792], P('head'), may hold values from -0.09375 to 0.09375
- query_weight: bfloat16 [4096, 4096], P(None, 'head'), may hold values from -0.09375 to 0.09375
- neighbour_weight: bfloat16 [896, 2, 4096], P(None, None, 'head'), may hold values from -0.1875 to 0.1875
- output_weight: bfloat16 [4096, 4096], P('head'), may hold values from -0.09375 to 0.09375
Outputs:
- updated: bfloat16 [4096, 4096], P(('span', 'group'), 'head')
Inputs may be any that keep to these rules, and one draw needn't show every extreme that they name: `owners`: within each aligned block of 8 spans no two neighbours share an owner and a slot, no owner stores more than 8 of the block's neighbours, and at least one owner stores exactly 8. `places`: slots of a block's neighbours on one owner are distinct.
All inputs are finite; a program needn't handle non-finite values.
Results may differ from a plain program's by a relative error of at most 0.025.
Values may be sent and summed in bfloat16 or wider, within the bound.
No kernel may reach another device: no remote copies, remote signals or barrier semaphores. Data moves between devices by JAX's collectives and lax.ppermute only.
A program may use at most 128 MiB of HBM per device.

v0:
```python
import functools

import jax
import jax.numpy as jnp
import numpy as np
from jax import lax
from jax.experimental import pallas as pl
from jax.experimental.pallas import tpu as pltpu
from jax.sharding import PartitionSpec as P


HEAD_DIM = 128
ENC_WIDTH = 896
SPAN_LEN = 64
RETRIEVED = 128
NEIGHBOURS = 2


HBM = pl.BlockSpec(memory_space=pltpu.HBM)
VMEM = pl.BlockSpec(memory_space=pltpu.VMEM)
SMEM = pl.BlockSpec(memory_space=pltpu.SMEM)


def attend(queries, keys_in, values_in, factor):
    scores = (
        jnp.einsum("bqhe,bkhe->bhqk", queries, keys_in, preferred_element_type=jnp.float32) * factor
    )
    weights = jax.nn.softmax(scores, axis=-1).astype(jnp.bfloat16)
    result = jnp.einsum("bhqk,bkhe->bqhe", weights, values_in, preferred_element_type=jnp.float32)
    return result.astype(jnp.bfloat16)


def encode(source, context, weights):
    number, length, breadth = source.shape
    groups = breadth // HEAD_DIM
    factor = HEAD_DIM ** (-0.5)
    rows_in = source.reshape(number * length, breadth)
    triple = jnp.dot(rows_in, weights[:, : 3 * breadth], preferred_element_type=jnp.float32).astype(
        jnp.bfloat16
    )
    triple = triple.reshape(number, length, 3, groups, HEAD_DIM)
    within = attend(triple[:, :, 0], triple[:, :, 1], triple[:, :, 2], factor).reshape(
        number * length, breadth
    )
    middle = rows_in.astype(jnp.float32) + jnp.dot(
        within, weights[:, 3 * breadth : 4 * breadth], preferred_element_type=jnp.float32
    )
    middle = middle.astype(jnp.bfloat16)
    asking = jnp.dot(
        middle, weights[:, 4 * breadth : 5 * breadth], preferred_element_type=jnp.float32
    ).astype(jnp.bfloat16)
    asking = asking.reshape(number, length, groups, HEAD_DIM)
    paired = context.reshape(number, context.shape[1], 2, groups, HEAD_DIM)
    across = attend(asking, paired[:, :, 0], paired[:, :, 1], factor).reshape(
        number * length, breadth
    )
    result = middle.astype(jnp.float32) + jnp.dot(
        across, weights[:, 5 * breadth :], preferred_element_type=jnp.float32
    )
    return result.astype(jnp.bfloat16).reshape(number, length, breadth)


def general(
    states,
    owners,
    places,
    stored,
    encoder_weights,
    context_weight,
    query_weight,
    neighbour_weight,
    output_weight,
):
    position = lax.axis_index("head")
    token_rows = states.shape[0]
    span_count = owners.shape[0]
    pair_count = span_count * NEIGHBOURS
    local_width = query_weight.shape[1]
    local_heads = local_width // HEAD_DIM
    factor = HEAD_DIM ** (-0.5)
    query_sums = jnp.dot(
        lax.all_gather(states, "head", axis=1, tiled=True),
        query_weight,
        preferred_element_type=jnp.float32,
    )
    queries = query_sums.astype(jnp.bfloat16)
    partial_context = jnp.dot(states, context_weight, preferred_element_type=jnp.float32)
    context = lax.psum(partial_context.astype(jnp.bfloat16), "head")
    context = context.reshape(span_count, SPAN_LEN, 2 * ENC_WIDTH)
    weights_all = lax.all_gather(encoder_weights, ("span", "group"), axis=0, tiled=True)
    owner_flat = owners.reshape(pair_count)
    place_flat = places.reshape(pair_count)
    pair_ids = jnp.arange(pair_count, dtype=jnp.int32)
    local_store = stored.reshape(stored.shape[3], stored.shape[4], stored.shape[5])
    slot_count = local_store.shape[0]
    slot_ids = jnp.arange(slot_count, dtype=jnp.int32)
    matched = (owner_flat[None, :] == position) & (place_flat[None, :] == slot_ids[:, None])
    span_of = jnp.sum(jnp.where(matched, pair_ids[None, :] // NEIGHBOURS, 0), axis=1)
    encoded = encode(local_store, context[span_of], weights_all)
    local_pair = neighbour_weight.reshape(ENC_WIDTH, 2 * local_width)
    piece = lax.all_gather(encoded, "head", axis=0, tiled=True)
    rows_in = piece.reshape(piece.shape[0] * RETRIEVED, ENC_WIDTH)
    result = jnp.dot(rows_in, local_pair, preferred_element_type=jnp.float32).astype(jnp.bfloat16)
    gathered = result.reshape(piece.shape[0], RETRIEVED, 2 * local_width)
    neighbour_pairs = gathered[owner_flat * slot_count + place_flat]
    asked = queries.reshape(span_count, SPAN_LEN, local_heads, HEAD_DIM)
    memory = neighbour_pairs.reshape(span_count, NEIGHBOURS * RETRIEVED, 2, local_heads, HEAD_DIM)
    attended = attend(asked, memory[:, :, 0], memory[:, :, 1], factor).reshape(
        token_rows, local_width
    )
    terms = jnp.dot(attended, output_weight, preferred_element_type=jnp.float32)
    summed = lax.psum_scatter(
        terms.astype(jnp.bfloat16), "head", scatter_dimension=1, tiled=True
    ).astype(jnp.float32)
    return (states.astype(jnp.float32) + summed).astype(jnp.bfloat16)


def call(kernel, out_shape, in_specs, out_specs, scratch, mib, flops, *args):
    return pl.pallas_call(
        kernel,
        out_shape=out_shape,
        in_specs=in_specs,
        out_specs=out_specs,
        scratch_shapes=scratch,
        compiler_params=pltpu.CompilerParams(vmem_limit_bytes=mib * 1024 * 1024),
        cost_estimate=pl.CostEstimate(
            flops=flops,
            bytes_accessed=2 * sum(a.size for a in args),
            transcendentals=0,
        ),
    )(*args)


def dot(a, b):
    return jnp.dot(a, b, preferred_element_type=jnp.float32)


def attend_many(units, scores, weights):
    rows = scores.shape[0] // len(units)
    part = [slice(i * rows, (i + 1) * rows) for i in range(len(units))]
    factor = HEAD_DIM ** (-0.5)
    for at, (q, k, _, _) in zip(part, units):
        scores[at, :] = lax.dot_general(
            q(), k(), (((1,), (1,)), ((), ())), preferred_element_type=jnp.float32
        )
    for at in part:
        one = scores[at, :]
        top = jnp.max(one, axis=-1, keepdims=True)
        weights[at, :] = jnp.exp((one - top) * factor).astype(jnp.bfloat16)
    for at, (_, _, v, put) in zip(part, units):
        values = v()
        both = dot(weights[at, :], jnp.concatenate([values, jnp.ones_like(values)], axis=1))
        put((both[:, :HEAD_DIM] / both[:, HEAD_DIM:]).astype(jnp.bfloat16))


def unit(q, q_rows, q_col, k, k_rows, k_col, v_col, out):
    def put(value):
        out[q_rows, q_col : q_col + HEAD_DIM] = value

    return (
        lambda: q[q_rows, q_col : q_col + HEAD_DIM],
        lambda: k[k_rows, k_col : k_col + HEAD_DIM],
        lambda: k[k_rows, v_col : v_col + HEAD_DIM],
        put,
    )


def head_index():
    return lax.axis_index("head").astype(jnp.int32)


def pairings(items):
    if not items:
        yield ()
        return
    for other in items[1:]:
        rest = tuple(i for i in items[1:] if i != other)
        for more in pairings(rest):
            yield ((items[0], other),) + more


def pair_table(spans):
    every = list(pairings(tuple(range(spans))))
    table = np.full((spans, -(-len(every) // 128) * 128), -1, np.int32)
    for c, pairing in enumerate(every):
        for slot, pair in enumerate(pairing):
            for span in pair:
                table[span, c] = slot
    return table


def plan_kernel(owners, table, assign):
    spans = table.shape[0]
    devices = spans // 2
    shape_row = (1, table.shape[1])
    hits = [
        [sum((owners[n, s] == o).astype(jnp.int32) for n in range(NEIGHBOURS)) for s in range(spans)]
        for o in range(devices)
    ]
    rows = [table[s : s + 1, :] for s in range(spans)]
    inside = [[(r == slot).astype(jnp.int32) for r in rows] for slot in range(devices)]
    fits = rows[0] >= 0
    for o in range(devices):
        heavy = jnp.zeros(shape_row, jnp.int32)
        for slot in range(devices):
            count = jnp.zeros(shape_row, jnp.int32)
            for s in range(spans):
                count = count + inside[slot][s] * hits[o][s]
            heavy = heavy + (count >= 3).astype(jnp.int32)
        fits = fits & (heavy <= 1)
    code = jnp.zeros(shape_row, jnp.int32)
    for s in range(spans):
        code = code + rows[s] * (devices**s)
    worst = devices**spans
    chosen = jnp.min(jnp.where(fits, code, worst).astype(jnp.float32)).astype(jnp.int32)
    slot_of = []
    for s in range(spans):
        slot_of.append(lax.rem(chosen, devices))
        chosen = lax.div(chosen, devices)
    takes = []
    for slot in range(devices):
        taker = jnp.int32(-1)
        for o in range(devices):
            count = sum(jnp.where(slot_of[s] == slot, hits[o][s], 0) for s in range(spans))
            taker = jnp.where(count >= 3, o, taker)
        takes.append(taker)
    for slot in range(devices):
        free = jnp.int32(0)
        for d in reversed(range(devices)):
            taken = sum((t == d).astype(jnp.int32) for t in takes)
            free = jnp.where(taken == 0, d, free)
        takes[slot] = jnp.where(takes[slot] < 0, free, takes[slot])
    for s in range(spans):
        before = sum(((slot_of[t] == slot_of[s]).astype(jnp.int32) for t in range(s)), jnp.int32(0))
        device = jnp.int32(0)
        for slot in range(devices):
            device = jnp.where(slot_of[s] == slot, takes[slot], device)
        assign[device * 2 + before] = jnp.int32(s)


def neighbours_of(assign, owners, places, device):
    found = []
    for j in range(2 * NEIGHBOURS):
        span = assign[device * 2 + j // NEIGHBOURS]
        found.append((owners[j % NEIGHBOURS, span], places[j % NEIGHBOURS, span]))
    return found


def pick_kernel(assign, owners, places, store, *rest):
    outs, (buf, sem_in, sem_out) = rest[:3], rest[3:]
    me = head_index()
    most = outs[0].shape[0]
    ins, puts = [], []
    for i in range(3):
        slots = [jnp.int32(0)] * most
        count = jnp.int32(0)
        for owner, place in neighbours_of(assign, owners, places, me ^ (i + 1)):
            here = owner == me
            for c in range(most):
                slots[c] = jnp.where(here & (count == c), place, slots[c])
            count = count + here.astype(jnp.int32)
        for c in range(most):
            k = i * most + c
            ins.append(pltpu.make_async_copy(store.at[slots[c]], buf.at[k], sem_in.at[k]))
            puts.append(pltpu.make_async_copy(buf.at[k], outs[i].at[c], sem_out.at[k]))
            ins[-1].start()
    for get, put in zip(ins, puts):
        get.wait()
        put.start()
    for c in puts:
        c.wait()


def context_kernel(assign, x, w, *rest):
    outs, buf = rest[:4], rest[4]
    me = head_index()
    width = w.shape[1]
    half = width // 2
    for c in range(2):
        cols = slice(c * half, (c + 1) * half)
        buf[:, cols] = dot(x[...], w[:, cols]).astype(jnp.bfloat16)
    for k in range(4):
        for i in range(2):
            start = pl.multiple_of(assign[(me ^ k) * 2 + i] * SPAN_LEN, SPAN_LEN)
            outs[k][i * SPAN_LEN : (i + 1) * SPAN_LEN, :] = buf[pl.ds(start, SPAN_LEN), :]


def load_pieces(n_span, pieces, held, sems):
    z = lax.axis_index("span").astype(jnp.int32)
    g = lax.axis_index("group").astype(jnp.int32)
    rows = pieces[0].shape[0]
    copies = []
    for i, piece in enumerate(pieces):
        spot = lax.rem(z + (n_span - i // 2), n_span) * 2 + (g ^ (i % 2))
        start = pl.multiple_of(spot * rows, rows)
        copies.append(
            pltpu.make_async_copy(piece, held.at[pl.ds(start, rows), :], sems.at[i])
        )
    return copies


def self_kernel(n_span, assign, owners, places, store, r1, r2, r3, *rest):
    pieces = rest[: 2 * n_span]
    source, within, held, triple, scores, weights, sem_s, sem_w = rest[2 * n_span :]
    me = head_index()
    per = 2 * NEIGHBOURS
    copies = load_pieces(n_span, pieces, held, sem_w)
    mine = neighbours_of(assign, owners, places, me)
    for j, (owner, place) in enumerate(mine):
        at = source.at[pl.ds(j * RETRIEVED, RETRIEVED), :]
        relation = owner ^ me
        nth = sum(((mine[t][0] == owner).astype(jnp.int32) for t in range(j)), jnp.int32(0))
        nth = jnp.minimum(nth, r1.shape[0] - 1)
        for k, ref in enumerate((store, r1, r2, r3)):

            @pl.when(relation == k)
            def _():
                pltpu.make_async_copy(ref.at[place if k == 0 else nth], at, sem_s.at[j]).start()

    for c in copies:
        c.start()
    for j in range(per):
        at = source.at[pl.ds(j * RETRIEVED, RETRIEVED), :]
        pltpu.make_async_copy(r1.at[0], at, sem_s.at[j]).wait()
    for c in copies:
        c.wait()
    breadth = source.shape[1]
    for c in range(3):
        cols = slice(c * breadth, (c + 1) * breadth)
        triple[:, cols] = dot(source[...], held[:, cols]).astype(jnp.bfloat16)
    units = []
    for j in range(per):
        rows = slice(j * RETRIEVED, (j + 1) * RETRIEVED)
        for c in range(0, breadth, HEAD_DIM):
            units.append(unit(triple, rows, c, triple, rows, breadth + c, 2 * breadth + c, within))
    attend_many(units, scores, weights)


def cross_kernel(n_span, source, within, c0, c1, c2, c3, *rest):
    pieces = rest[: 2 * n_span]
    outs = rest[2 * n_span : -8]
    held, context, middle, asking, across, scores, weights, sem_w = rest[-8:]
    copies = load_pieces(n_span, pieces, held, sem_w)
    for c in copies:
        c.start()
    breadth = source.shape[1]
    total = c0[...].astype(jnp.float32) + c1[...].astype(jnp.float32)
    total = total + (c2[...].astype(jnp.float32) + c3[...].astype(jnp.float32))
    context[...] = total.astype(jnp.bfloat16)
    for c in copies:
        c.wait()
    middle[...] = (
        source[...].astype(jnp.float32) + dot(within[...], held[:, :breadth])
    ).astype(jnp.bfloat16)
    asking[...] = dot(middle[...], held[:, breadth : 2 * breadth]).astype(jnp.bfloat16)
    span_rows = NEIGHBOURS * RETRIEVED
    units = []
    for s in range(len(outs)):
        rows = slice(s * span_rows, (s + 1) * span_rows)
        keys = slice(s * SPAN_LEN, (s + 1) * SPAN_LEN)
        for c in range(0, breadth, HEAD_DIM):
            units.append(unit(asking, rows, c, context, keys, c, breadth + c, across))
    attend_many(units, scores, weights)
    for s, out in enumerate(outs):
        rows = slice(s * span_rows, (s + 1) * span_rows)
        out[...] = (
            middle[rows, :].astype(jnp.float32) + dot(across[rows, :], held[:, 2 * breadth :])
        ).astype(jnp.bfloat16)


def query_kernel(own, x0, x1, y0, y1, d0, d1, w, out, held, total, sems):
    me = head_index()
    width = own.shape[1]
    half = x0.shape[0]
    copies = []
    for k in range(4):
        start = pl.multiple_of((me ^ k) * width, width)
        copies.append(
            pltpu.make_async_copy(w.at[pl.ds(start, width), :], held.at[k], sems.at[k])
        )
    for c in copies:
        c.start()
    copies[0].wait()
    total[...] = dot(own[...], held[0])
    for k, (a, b) in enumerate(((x0, x1), (y0, y1), (d0, d1))):
        copies[k + 1].wait()
        total[:half, :] += dot(a[...], held[k + 1])
        total[half:, :] += dot(b[...], held[k + 1])
    out[...] = total[...].astype(jnp.bfloat16)


def span_kernel(relations, assign, queries, *rest):
    n = 2 * len(relations)
    encs = rest[:n]
    pair, held = rest[n : n + 2]
    outs = rest[n + 2 : n + 6]
    q, keep, memory, att, scores, weights, sem = rest[n + 6 :]
    me = head_index()
    local = q.shape[1]
    span_rows = NEIGHBOURS * RETRIEVED
    loads = []
    for i in range(n):
        span = assign[(me ^ relations[i // 2]) * 2 + i % 2]
        at = pl.ds(pl.multiple_of(span * SPAN_LEN, SPAN_LEN), SPAN_LEN)
        to_rows = pl.ds(i * SPAN_LEN, SPAN_LEN)
        loads.append(pltpu.make_async_copy(queries.at[at, :], q.at[to_rows, :], sem.at[i]))
    for c in loads:
        c.start()
    for s in range(n):
        keep[s * span_rows : (s + 1) * span_rows, :] = encs[s][...]
    for c in range(2):
        cols = slice(c * local, (c + 1) * local)
        memory[:, cols] = dot(keep[...], pair[:, cols]).astype(jnp.bfloat16)
    for c in loads:
        c.wait()
    units = []
    for s in range(n):
        r = slice(s * SPAN_LEN, (s + 1) * SPAN_LEN)
        m = slice(s * span_rows, (s + 1) * span_rows)
        for c in range(0, local, HEAD_DIM):
            units.append(unit(q, r, c, memory, m, c, local + c, att))
    attend_many(units, scores, weights)
    width = outs[0].shape[1]
    for k in range(4):
        start = pl.multiple_of((me ^ k) * width, width)
        outs[k][...] = dot(att[...], held[:, pl.ds(start, width)]).astype(jnp.bfloat16)


def final_kernel(assign, states, *rest):
    terms, out = rest[:12], rest[12]
    me = head_index()
    chunk_of = ((0, 0), (1, 0), (1, 1), (2, 0))
    for m, i in ((m, i) for m in range(4) for i in range(2)):
        span = assign[(me ^ m) * 2 + i]
        at = pl.ds(pl.multiple_of(span * SPAN_LEN, SPAN_LEN), SPAN_LEN)
        parts = []
        for k in range(4):
            chunk, part = chunk_of[k ^ m]
            start = (2 * part + i) * SPAN_LEN
            term = terms[4 * chunk + k][start : start + SPAN_LEN, :]
            parts.append(term.astype(jnp.float32))
        total = (parts[0] + parts[1]) + (parts[2] + parts[3])
        out[at, :] = (states[at, :].astype(jnp.float32) + total).astype(jnp.bfloat16)


def shape(*dims):
    return jax.ShapeDtypeStruct(dims, jnp.bfloat16)


def to(k, value):
    return lax.ppermute(value, "head", [(i, i ^ k) for i in range(4)])


def fast(
    n_span,
    states,
    owners,
    places,
    stored,
    encoder_weights,
    context_weight,
    query_weight,
    neighbour_weight,
    output_weight,
):
    bf16 = jnp.bfloat16
    tokens, feat = states.shape
    span_count = owners.shape[0]
    per = span_count * NEIGHBOURS // 4
    own_spans = span_count // 4
    local = query_weight.shape[1]
    store = stored.reshape(stored.shape[3], RETRIEVED, ENC_WIDTH)
    owners, places = owners.T, places.T

    table = jnp.asarray(pair_table(span_count))
    assign = pl.pallas_call(
        plan_kernel,
        out_shape=jax.ShapeDtypeStruct((span_count,), jnp.int32),
        in_specs=[SMEM, VMEM],
        out_specs=SMEM,
        name="plan",
    )(owners, table)

    most = 2
    sends = call(
        pick_kernel,
        [shape(most, RETRIEVED, ENC_WIDTH)] * 3,
        [SMEM] * 3 + [HBM],
        [HBM] * 3,
        [
            pltpu.VMEM((3 * most, RETRIEVED, ENC_WIDTH), bf16),
            pltpu.SemaphoreType.DMA((3 * most,)),
            pltpu.SemaphoreType.DMA((3 * most,)),
        ],
        8,
        4 * 10**9,
        assign,
        owners,
        places,
        store,
    )
    raw = [to(k + 1, sends[k]) for k in range(3)]

    cut = 3 * ENC_WIDTH
    ring = [(i, (i + 1) % n_span) for i in range(n_span)]
    halves = []
    for part in (encoder_weights[:, :cut], encoder_weights[:, cut:]):
        pieces, now = [], part
        for r in range(n_span):
            if r:
                now = lax.ppermute(now, "span", ring)
            pieces.append(now)
            pieces.append(lax.ppermute(now, "group", [(0, 1), (1, 0)]))
        halves.append(pieces)
    n_pieces = 2 * n_span

    width_c = context_weight.shape[1]
    rows_c = tokens // 4
    part_c = call(
        context_kernel,
        [shape(rows_c, width_c)] * 4,
        [SMEM, VMEM, VMEM],
        [VMEM] * 4,
        [pltpu.VMEM((tokens, width_c), bf16)],
        16,
        2 * tokens * feat * width_c,
        assign,
        states,
        context_weight,
    )
    context = [part_c[0]] + [to(k, part_c[k]) for k in range(1, 4)]

    half_t = tokens // 2
    s0, s1 = states[:half_t], states[half_t:]
    x0, y1 = to(1, s0), to(2, s1)
    x1, y0 = to(1, s1), to(2, s0)
    d0, d1 = to(2, x0), to(1, y1)

    source, within = call(
        functools.partial(self_kernel, n_span),
        [shape(per * RETRIEVED, ENC_WIDTH)] * 2,
        [SMEM] * 3 + [HBM] * (4 + n_pieces),
        [VMEM] * 2,
        [
            pltpu.VMEM((ENC_WIDTH, cut), bf16),
            pltpu.VMEM((per * RETRIEVED, cut), bf16),
            pltpu.VMEM((per * ENC_WIDTH, RETRIEVED), jnp.float32),
            pltpu.VMEM((per * ENC_WIDTH, RETRIEVED), bf16),
            pltpu.SemaphoreType.DMA((per,)),
            pltpu.SemaphoreType.DMA((n_pieces,)),
        ],
        20,
        4 * per * RETRIEVED * ENC_WIDTH * cut,
        assign,
        owners,
        places,
        store,
        *raw,
        *halves[0],
    )
    span_rows = NEIGHBOURS * RETRIEVED
    enc = call(
        functools.partial(cross_kernel, n_span),
        [shape(span_rows, ENC_WIDTH)] * own_spans,
        [VMEM] * 6 + [HBM] * n_pieces,
        [VMEM] * own_spans,
        [
            pltpu.VMEM((ENC_WIDTH, cut), bf16),
            pltpu.VMEM((rows_c, width_c), bf16),
            pltpu.VMEM((per * RETRIEVED, ENC_WIDTH), bf16),
            pltpu.VMEM((per * RETRIEVED, ENC_WIDTH), bf16),
            pltpu.VMEM((per * RETRIEVED, ENC_WIDTH), bf16),
            pltpu.VMEM((per * ENC_WIDTH, SPAN_LEN), jnp.float32),
            pltpu.VMEM((per * ENC_WIDTH, SPAN_LEN), bf16),
            pltpu.SemaphoreType.DMA((n_pieces,)),
        ],
        20,
        4 * per * RETRIEVED * ENC_WIDTH * cut,
        source,
        within,
        *context,
        *halves[1],
    )
    first = own_spans // 2
    x = [to(1, e) for e in enc]
    y = [to(2, e) for e in enc]
    d = [to(2, x[i]) for i in range(first)]
    d += [to(1, y[i]) for i in range(first, own_spans)]

    queries = call(
        query_kernel,
        shape(tokens, local),
        [VMEM] * 7 + [HBM],
        VMEM,
        [
            pltpu.VMEM((4, feat, local), bf16),
            pltpu.VMEM((tokens, local), jnp.float32),
            pltpu.SemaphoreType.DMA((4,)),
        ],
        24,
        8 * tokens * feat * local,
        states,
        x0,
        x1,
        y0,
        y1,
        d0,
        d1,
        query_weight,
    )
    w_pair = neighbour_weight.reshape(ENC_WIDTH, 2 * local)
    arrived = []
    for relations, chunk in (((0,), enc), ((1, 2), x + y), ((3,), d)):
        spans = len(chunk)
        rows = spans * SPAN_LEN
        terms = call(
            functools.partial(span_kernel, relations),
            [shape(rows, feat)] * 4,
            [SMEM, HBM] + [VMEM] * (spans + 2),
            [VMEM] * 4,
            [
                pltpu.VMEM((rows, local), bf16),
                pltpu.VMEM((spans * span_rows, ENC_WIDTH), bf16),
                pltpu.VMEM((spans * span_rows, 2 * local), bf16),
                pltpu.VMEM((rows, local), bf16),
                pltpu.VMEM((rows * local // HEAD_DIM, span_rows), jnp.float32),
                pltpu.VMEM((rows * local // HEAD_DIM, span_rows), bf16),
                pltpu.SemaphoreType.DMA((spans,)),
            ],
            32,
            4 * spans * span_rows * ENC_WIDTH * 2 * local,
            assign,
            queries,
            *chunk,
            w_pair,
            output_weight,
        )
        arrived.append(terms[0])
        arrived += [to(k, terms[k]) for k in range(1, 4)]
    return call(
        final_kernel,
        shape(tokens, feat),
        [SMEM] + [VMEM] * 13,
        VMEM,
        [],
        16,
        17 * tokens * feat,
        assign,
        states,
        *arrived,
    )


def solution(mesh):
    sizes = mesh.shape
    n_head, n_span = sizes["head"], sizes["span"]
    square = n_head == 4 and sizes["group"] == 2

    def per_device(*args):
        spans = args[1].shape[0]
        if square and spans == 2 * n_head:
            return fast(n_span, *args)
        return general(*args)

    in_specs = (
        P(("span", "group"), "head"),
        P(("span", "group"), None),
        P(("span", "group"), None),
        P("span", "head", "group", None, None, None),
        P(("span", "group"), None),
        P("head", None),
        P(None, "head"),
        P(None, None, "head"),
        P("head", None),
    )
    out_specs = P(("span", "group"), "head")
    return jax.shard_map(
        per_device, mesh=mesh, in_specs=in_specs, out_specs=out_specs, check_vma=False
    )
```

profile of v0, /device:TPU:0, one launch (start us, length us, event | category | flops | bytes accessed | tf_op | source)
XLA Modules:
  0.0 207.2 jit_solution(14880570821535889490)
XLA Ops:
  1.3 3.1 %collective-permute-start.10 = (bf16[112,2688]{1,0:T(8,128)(2,1)S(1)}, bf16[112,2688]{1,0:T(8,128)(2,1)S(1)}, u32[]{:S(2)}, u32[]{:S(2)}) collective-permute-start(bf16[112,2688]{1,0:T(8,128)(2,1)S(1)} %get-tuple-element.52.rest_0_), channel_id=1, source_target_pairs={{0,8},{8,16},{16,24},{24,0},{1,9},{9,17},{17,25},{25,1},{2,10},{10... | collective-permute-start | bytes 1806344 | tf_op jit(solution)/shard_map/ppermute | solution.py:511
  4.4 1.7 plan.1.assign
  9.7 4.3 %shard_map.101 = (bf16[2,128,896]{2,1,0:T(8,128)(2,1)S(1)}, bf16[2,128,896]{2,1,0:T(8,128)(2,1)S(1)}, bf16[2,128,896]{2,1,0:T(8,128)(2,1)S(1)}) custom-call(s32[8]{0:T(128)S(1)} %copy-done.1, s32[2,8]{1,0:T(2,128)S(1)} %bitcast.11, s32[2,8]{1,0:T(2,128)S(1)} %bitcast.15, bf16[8,128,896]{2,1,0:T(8,128)(2,1)S(1)} %bitcast.13), custom_call_target="tpu_custom_call" | custom-call | flops 4000000000 | bytes 1835088 | tf_op jit(solution)/shard_map/pallas_call | solution.py:119
  14.0 1.6 collective-permute-start.6
  17.5 3.0 %shard_map.103 = (bf16[128,1792]{1,0:T(8,128)(2,1)S(1)}, bf16[128,1792]{1,0:T(8,128)(2,1)S(1)}, bf16[128,1792]{1,0:T(8,128)(2,1)S(1)}, bf16[128,1792]{1,0:T(8,128)(2,1)S(1)}) custom-call(s32[8]{0:T(128)S(1)} %copy-done.2, bf16[512,1024]{1,0:T(8,128)(2,1)S(1)} %copy-done, bf16[1024,1792]{1,0:T(8,128)(2,1)S(1)} %copy-done.6), custom_call_target="tpu_custom_call" | custom-call | flops 1879048192 | bytes 4718608 | tf_op jit(solution)/shard_map/pallas_call | solution.py:119
  20.5 1.6 collective-permute-start.16
  22.1 5.3 %collective-permute-done.6.r1 = bf16[2,128,896]{2,1,0:T(8,128)(2,1)S(1)} collective-permute-done((bf16[2,128,896]{2,1,0:T(8,128)(2,1)S(1)}, bf16[2,128,896]{2,1,0:T(8,128)(2,1)S(1)}, u32[]{:S(2)}, u32[]{:S(2)}) %collective-permute-start.6) | collective-permute-done | bytes 458784 | tf_op jit(solution)/shard_map/ppermute | solution.py:451
  28.9 8.5 %collective-permute-done.7.r2 = bf16[2,128,896]{2,1,0:T(8,128)(2,1)S(1)} collective-permute-done((bf16[2,128,896]{2,1,0:T(8,128)(2,1)S(1)}, bf16[2,128,896]{2,1,0:T(8,128)(2,1)S(1)}, u32[]{:S(2)}, u32[]{:S(2)}) %collective-permute-start.7) | collective-permute-done | bytes 458784 | tf_op jit(solution)/shard_map/ppermute | solution.py:451
  37.4 1.6 collective-permute-start.20
  39.0 1.6 collective-permute-start.12
  40.7 6.4 %collective-permute-done.16.c1 = bf16[128,1792]{1,0:T(8,128)(2,1)S(1)} collective-permute-done((bf16[128,1792]{1,0:T(8,128)(2,1)S(1)}, bf16[128,1792]{1,0:T(8,128)(2,1)S(1)}, u32[]{:S(2)}, u32[]{:S(2)}) %collective-permute-start.16) | collective-permute-done | bytes 458784 | tf_op jit(solution)/shard_map/ppermute | solution.py:451
  50.1 1.6 collective-permute-start.22
  51.7 16.2 %collective-permute-done.18.c3 = bf16[128,1792]{1,0:T(8,128)(2,1)S(1)} collective-permute-done((bf16[128,1792]{1,0:T(8,128)(2,1)S(1)}, bf16[128,1792]{1,0:T(8,128)(2,1)S(1)}, u32[]{:S(2)}, u32[]{:S(2)}) %collective-permute-start.18) | collective-permute-done | bytes 458784 | tf_op jit(solution)/shard_map/ppermute | solution.py:451
  68.4 1.6 collective-permute-start.14
  70.0 1.6 collective-permute-start.24
  72.2 14.5 %collective-permute-done.14.rest_6_ = bf16[112,2688]{1,0:T(8,128)(2,1)S(1)} collective-permute-done((bf16[112,2688]{1,0:T(8,128)(2,1)S(1)}, bf16[112,2688]{1,0:T(8,128)(2,1)S(1)}, u32[]{:S(2)}, u32[]{:S(2)}) %collective-permute-start.14) | collective-permute-done | bytes 602144 | tf_op jit(solution)/shard_map/ppermute | solution.py:511
  86.7 12.4 %collective-permute-done.24.rest_6_ = bf16[112,2688]{1,0:T(8,128)(2,1)S(1)} collective-permute-done((bf16[112,2688]{1,0:T(8,128)(2,1)S(1)}, bf16[112,2688]{1,0:T(8,128)(2,1)S(1)}, u32[]{:S(2)}, u32[]{:S(2)}) %collective-permute-start.24) | collective-permute-done | bytes 602144 | tf_op jit(solution)/shard_map/ppermute | solution.py:511
  104.5 7.9 %shard_map.102 = (bf16[512,896]{1,0:T(8,128)(2,1)S(1)}, bf16[512,896]{1,0:T(8,128)(2,1)S(1)}) custom-call(s32[8]{0:T(128)S(1)} %copy-done.2, s32[2,8]{1,0:T(2,128)S(1)} %bitcast.12, s32[2,8]{1,0:T(2,128)S(1)} %bitcast.16, bf16[8,128,896]{2,1,0:T(8,128)(2,1)S(1)} %bitcast.14, bf16[2,128,896]{2,1,0:T(8,128)(2,1)S(1)} %collective-permute-done.6.r1, ...), custom_call_target="tpu_custom_call" | custom-call | flops 4932501504 | bytes 8028240 | tf_op jit(solution)/shard_map/pallas_call | solution.py:119
  112.4 5.7 %shard_map.104 = (bf16[256,896]{1,0:T(8,128)(2,1)S(1)}, bf16[256,896]{1,0:T(8,128)(2,1)S(1)}) custom-call(bf16[512,896]{1,0:T(8,128)(2,1)S(1)} %get-tuple-element.31.source, bf16[512,896]{1,0:T(8,128)(2,1)S(1)} %get-tuple-element.32.within, bf16[128,1792]{1,0:T(8,128)(2,1)S(1)} %get-tuple-element.33.c0, bf16[128,1792]{1,0:T(8,128)(2,1)S(1)} %collective-permute-done.16.c1, ...), custom_call_target="tpu_custom_call" | custom-call | flops 4932501504 | bytes 8486912 | tf_op jit(solution)/shard_map/pallas_call | solution.py:119
  121.4 6.5 %collective-permute-done.4.d0 = bf16[256,1024]{1,0:T(8,128)(2,1)S(1)} collective-permute-done((bf16[256,1024]{1,0:T(8,128)(2,1)S(1)}, bf16[256,1024]{1,0:T(8,128)(2,1)S(1)}, u32[]{:S(2)}, u32[]{:S(2)}) %collective-permute-start.4) | collective-permute-done | bytes 524320 | tf_op jit(solution)/shard_map/ppermute | solution.py:451
  129.2 3.4 %copy-done.5 = bf16[4096,1024]{1,0:T(8,128)(2,1)S(1)} copy-done((bf16[4096,1024]{1,0:T(8,128)(2,1)S(1)}, bf16[4096,1024]{1,0:T(8,128)(2,1)}, u32[]{:S(2)}) %copy-start.5) | copy-done | bytes 8388632
  132.6 5.3 %shard_map.100.queries = bf16[512,1024]{1,0:T(8,128)(2,1)S(1)} custom-call(bf16[512,1024]{1,0:T(8,128)(2,1)S(1)} %copy-done, bf16[256,1024]{1,0:T(8,128)(2,1)S(1)} %collective-permute-done.x0, bf16[256,1024]{1,0:T(8,128)(2,1)S(1)} %collective-permute-done.1.x1, bf16[256,1024]{1,0:T(8,128)(2,1)S(1)} %collective-permute-done.2.y0, ...), custom_call_target="tpu_custom_call" | custom-call | flops 4294967296 | bytes 12582912 | tf_op jit(solution)/shard_map/pallas_call | solution.py:119
  137.9 5.6 %shard_map.105 = (bf16[128,1024]{1,0:T(8,128)(2,1)S(1)}, bf16[128,1024]{1,0:T(8,128)(2,1)S(1)}, bf16[128,1024]{1,0:T(8,128)(2,1)S(1)}, bf16[128,1024]{1,0:T(8,128)(2,1)S(1)}) custom-call(s32[8]{0:T(128)S(1)} %copy-done.2, bf16[512,1024]{1,0:T(8,128)(2,1)S(1)} %shard_map.100.queries, bf16[256,896]{1,0:T(8,128)(2,1)S(1)} %get-tuple-element.37.rest_0_, ...), custom_call_target="tpu_custom_call" | custom-call | flops 3758096384 | bytes 14024720 | tf_op jit(solution)/shard_map/pallas_call | solution.py:119
  144.9 2.8 %collective-permute-done.32.rest_3_ = bf16[256,896]{1,0:T(8,128)(2,1)S(1)} collective-permute-done((bf16[256,896]{1,0:T(8,128)(2,1)S(1)}, bf16[256,896]{1,0:T(8,128)(2,1)S(1)}, u32[]{:S(2)}, u32[]{:S(2)}) %collective-permute-start.32) | collective-permute-done | bytes 458784 | tf_op jit(solution)/shard_map/ppermute | solution.py:451
  148.2 9.7 %shard_map.106 = (bf16[256,1024]{1,0:T(8,128)(2,1)S(1)}, bf16[256,1024]{1,0:T(8,128)(2,1)S(1)}, bf16[256,1024]{1,0:T(8,128)(2,1)S(1)}, bf16[256,1024]{1,0:T(8,128)(2,1)S(1)}) custom-call(s32[8]{0:T(128)S(1)} %copy-done.2, bf16[512,1024]{1,0:T(8,128)(2,1)S(1)} %shard_map.100.queries, bf16[256,896]{1,0:T(8,128)(2,1)S(1)} %collective-permute-done.29.rest_0_, ...), custom_call_target="tpu_custom_call" | custom-call | flops 7516192768 | bytes 14942224 | tf_op jit(solution)/shard_map/pallas_call | solution.py:119
  157.9 1.6 collective-permute-start.33
  162.7 1.7 collective-permute-start.35
  164.4 5.6 %shard_map.107 = (bf16[128,1024]{1,0:T(8,128)(2,1)S(1)}, bf16[128,1024]{1,0:T(8,128)(2,1)S(1)}, bf16[128,1024]{1,0:T(8,128)(2,1)S(1)}, bf16[128,1024]{1,0:T(8,128)(2,1)S(1)}) custom-call(s32[8]{0:T(128)S(1)} %copy-done.2, bf16[512,1024]{1,0:T(8,128)(2,1)S(1)} %shard_map.100.queries, bf16[256,896]{1,0:T(8,128)(2,1)S(1)} %collective-permute-done.36.rest_0_, ...), custom_call_target="tpu_custom_call" | custom-call | flops 3758096384 | bytes 14024720 | tf_op jit(solution)/shard_map/pallas_call | solution.py:119
  170.6 9.1 %collective-permute-done.28.rest_3_ = bf16[128,1024]{1,0:T(8,128)(2,1)S(1)} collective-permute-done((bf16[128,1024]{1,0:T(8,128)(2,1)S(1)}, bf16[128,1024]{1,0:T(8,128)(2,1)S(1)}, u32[]{:S(2)}, u32[]{:S(2)}) %collective-permute-start.28) | collective-permute-done | bytes 262176 | tf_op jit(solution)/shard_map/ppermute | solution.py:451
  182.2 20.0 %collective-permute-done.34.rest_6_ = bf16[256,1024]{1,0:T(8,128)(2,1)S(1)} collective-permute-done((bf16[256,1024]{1,0:T(8,128)(2,1)S(1)}, bf16[256,1024]{1,0:T(8,128)(2,1)S(1)}, u32[]{:S(2)}, u32[]{:S(2)}) %collective-permute-start.34) | collective-permute-done | bytes 524320 | tf_op jit(solution)/shard_map/ppermute | solution.py:451
  202.2 2.8 %collective-permute-done.39.rest_10_ = bf16[128,1024]{1,0:T(8,128)(2,1)S(1)} collective-permute-done((bf16[128,1024]{1,0:T(8,128)(2,1)S(1)}, bf16[128,1024]{1,0:T(8,128)(2,1)S(1)}, u32[]{:S(2)}, u32[]{:S(2)}) %collective-permute-start.39) | collective-permute-done | bytes 262176 | tf_op jit(solution)/shard_map/ppermute | solution.py:451
  205.0 2.2 %shard_map.108 = bf16[512,1024]{1,0:T(8,128)(2,1)} custom-call(s32[8]{0:T(128)S(1)} %copy-done.2, bf16[512,1024]{1,0:T(8,128)(2,1)S(1)} %copy-done, bf16[128,1024]{1,0:T(8,128)(2,1)S(1)} %get-tuple-element.39.rest_0_, bf16[128,1024]{1,0:T(8,128)(2,1)S(1)} %collective-permute-done.26.rest_1_, bf16[128,1024]{1,0:T(8,128)(2,1)S(1)} %collective-permute-done.27.rest_2_, ...), custom_call_target="tpu_custom_call" | custom-call | flops 8912896 | bytes 5242896 | tf_op jit(solution)/shard_map/pallas_call | solution.py:119
  (92 shorter events, 30.9 us)
Async XLA Ops:
  1.3 37.7 %collective-permute-start.10 = (bf16[112,2688]{1,0:T(8,128)(2,1)S(1)}, bf16[112,2688]{1,0:T(8,128)(2,1)S(1)}, u32[]{:S(2)}, u32[]{:S(2)}) collective-permute-start(bf16[112,2688]{1,0:T(8,128)(2,1)S(1)} %get-tuple-element.52.rest_0_), channel_id=1, source_target_pairs={{0,8},{8,16},{16,24},{24,0},{1,9},{9,17},{17,25},{25,1},{2,10},{10... | collective-permute-start | bytes 1806344 | tf_op jit(solution)/shard_map/ppermute | solution.py:511
  15.5 21.9 %collective-permute-start.7 = (bf16[2,128,896]{2,1,0:T(8,128)(2,1)S(1)}, bf16[2,128,896]{2,1,0:T(8,128)(2,1)S(1)}, u32[]{:S(2)}, u32[]{:S(2)}) collective-permute-start(bf16[2,128,896]{2,1,0:T(8,128)(2,1)S(1)} %get-tuple-element.29), channel_id=1, source_target_pairs={{0,4},{2,6},{4,0},{6,2},{1,5},{3,7},{5,1},{7,3},{8,12},{10,14},{12... | collective-permute-start | bytes 1376264 | tf_op jit(solution)/shard_map/ppermute | solution.py:451
  17.0 23.6 %collective-permute-start.8 = (bf16[2,128,896]{2,1,0:T(8,128)(2,1)S(1)}, bf16[2,128,896]{2,1,0:T(8,128)(2,1)S(1)}, u32[]{:S(2)}, u32[]{:S(2)}) collective-permute-start(bf16[2,128,896]{2,1,0:T(8,128)(2,1)S(1)} %get-tuple-element.30), channel_id=1, source_target_pairs={{0,6},{2,4},{4,2},{6,0},{1,7},{3,5},{5,3},{7,1},{8,14},{10,12},{12... | collective-permute-start | bytes 1376264 | tf_op jit(solution)/shard_map/ppermute | solution.py:451
  20.5 26.6 %collective-permute-start.16 = (bf16[128,1792]{1,0:T(8,128)(2,1)S(1)}, bf16[128,1792]{1,0:T(8,128)(2,1)S(1)}, u32[]{:S(2)}, u32[]{:S(2)}) collective-permute-start(bf16[128,1792]{1,0:T(8,128)(2,1)S(1)} %get-tuple-element.34), channel_id=1, source_target_pairs={{0,2},{2,0},{4,6},{6,4},{1,3},{3,1},{5,7},{7,5},{8,10},{10,8},{12,... | collective-permute-start | bytes 1376264 | tf_op jit(solution)/shard_map/ppermute | solution.py:451
  27.4 21.2 %collective-permute-start.17 = (bf16[128,1792]{1,0:T(8,128)(2,1)S(1)}, bf16[128,1792]{1,0:T(8,128)(2,1)S(1)}, u32[]{:S(2)}, u32[]{:S(2)}) collective-permute-start(bf16[128,1792]{1,0:T(8,128)(2,1)S(1)} %get-tuple-element.35), channel_id=1, source_target_pairs={{0,4},{2,6},{4,0},{6,2},{1,5},{3,7},{5,1},{7,3},{8,12},{10,14},{12... | collective-permute-start | bytes 1376264 | tf_op jit(solution)/shard_map/ppermute | solution.py:451
  39.0 29.4 %collective-permute-start.12 = (bf16[112,2688]{1,0:T(8,128)(2,1)S(1)}, bf16[112,2688]{1,0:T(8,128)(2,1)S(1)}, u32[]{:S(2)}, u32[]{:S(2)}) collective-permute-start(bf16[112,2688]{1,0:T(8,128)(2,1)S(1)} %collective-permute-done.10.rest_2_), channel_id=1, source_target_pairs={{0,8},{8,16},{16,24},{24,0},{1,9},{9,17},{17,25},{25,1},{2,10},{10... | collective-permute-start | bytes 1806344 | tf_op jit(solution)/shard_map/ppermute | solution.py:511
  40.7 27.2 %collective-permute-start = (bf16[256,1024]{1,0:T(8,128)(2,1)S(1)}, bf16[256,1024]{1,0:T(8,128)(2,1)S(1)}, u32[]{:S(2)}, u32[]{:S(2)}) collective-permute-start(bf16[256,1024]{1,0:T(8,128)(2,1)S(1)} %get-tuple-element.54), channel_id=1, source_target_pairs={{0,2},{2,0},{4,6},{6,4},{1,3},{3,1},{5,7},{7,5},{8,10},{10,8},{12,... | collective-permute-start | bytes 1572872 | tf_op jit(solution)/shard_map/ppermute | solution.py:451
  47.1 21.2 %collective-permute-start.3 = (bf16[256,1024]{1,0:T(8,128)(2,1)S(1)}, bf16[256,1024]{1,0:T(8,128)(2,1)S(1)}, u32[]{:S(2)}, u32[]{:S(2)}) collective-permute-start(bf16[256,1024]{1,0:T(8,128)(2,1)S(1)} %get-tuple-element.53), channel_id=1, source_target_pairs={{0,4},{2,6},{4,0},{6,2},{1,5},{3,7},{5,1},{7,3},{8,12},{10,14},{12... | collective-permute-start | bytes 1572872 | tf_op jit(solution)/shard_map/ppermute | solution.py:451
  48.7 19.2 %collective-permute-start.18 = (bf16[128,1792]{1,0:T(8,128)(2,1)S(1)}, bf16[128,1792]{1,0:T(8,128)(2,1)S(1)}, u32[]{:S(2)}, u32[]{:S(2)}) collective-permute-start(bf16[128,1792]{1,0:T(8,128)(2,1)S(1)} %get-tuple-element.36), channel_id=1, source_target_pairs={{0,6},{2,4},{4,2},{6,0},{1,7},{3,5},{5,3},{7,1},{8,14},{10,12},{12... | collective-permute-start | bytes 1376264 | tf_op jit(solution)/shard_map/ppermute | solution.py:451
  50.1 19.9 %collective-permute-start.22 = (bf16[112,2688]{1,0:T(8,128)(2,1)S(1)}, bf16[112,2688]{1,0:T(8,128)(2,1)S(1)}, u32[]{:S(2)}, u32[]{:S(2)}) collective-permute-start(bf16[112,2688]{1,0:T(8,128)(2,1)S(1)} %collective-permute-done.20.rest_2_), channel_id=1, source_target_pairs={{0,8},{8,16},{16,24},{24,0},{1,9},{9,17},{17,25},{25,1},{2,10},{10... | collective-permute-start | bytes 1806344 | tf_op jit(solution)/shard_map/ppermute | solution.py:511
  68.4 18.3 %collective-permute-start.14 = (bf16[112,2688]{1,0:T(8,128)(2,1)S(1)}, bf16[112,2688]{1,0:T(8,128)(2,1)S(1)}, u32[]{:S(2)}, u32[]{:S(2)}) collective-permute-start(bf16[112,2688]{1,0:T(8,128)(2,1)S(1)} %collective-permute-done.12.rest_4_), channel_id=1, source_target_pairs={{0,8},{8,16},{16,24},{24,0},{1,9},{9,17},{17,25},{25,1},{2,10},{10... | collective-permute-start | bytes 1806344 | tf_op jit(solution)/shard_map/ppermute | solution.py:511
  70.0 29.1 %collective-permute-start.24 = (bf16[112,2688]{1,0:T(8,128)(2,1)S(1)}, bf16[112,2688]{1,0:T(8,128)(2,1)S(1)}, u32[]{:S(2)}, u32[]{:S(2)}) collective-permute-start(bf16[112,2688]{1,0:T(8,128)(2,1)S(1)} %collective-permute-done.22.rest_4_), channel_id=1, source_target_pairs={{0,8},{8,16},{16,24},{24,0},{1,9},{9,17},{17,25},{25,1},{2,10},{10... | collective-permute-start | bytes 1806344 | tf_op jit(solution)/shard_map/ppermute | solution.py:511
  71.6 28.8 %collective-permute-start.21 = (bf16[112,2688]{1,0:T(8,128)(2,1)S(1)}, bf16[112,2688]{1,0:T(8,128)(2,1)S(1)}, u32[]{:S(2)}, u32[]{:S(2)}) collective-permute-start(bf16[112,2688]{1,0:T(8,128)(2,1)S(1)} %collective-permute-done.20.rest_2_), channel_id=1, source_target_pairs={{0,1},{1,0},{2,3},{3,2},{4,5},{5,4},{6,7},{7,6},{8,9},{9,8},{10,11... | collective-permute-start | bytes 1806344 | tf_op jit(solution)/shard_map/ppermute | solution.py:513
  71.6 30.3 %collective-permute-start.13 = (bf16[112,2688]{1,0:T(8,128)(2,1)S(1)}, bf16[112,2688]{1,0:T(8,128)(2,1)S(1)}, u32[]{:S(2)}, u32[]{:S(2)}) collective-permute-start(bf16[112,2688]{1,0:T(8,128)(2,1)S(1)} %collective-permute-done.12.rest_4_), channel_id=1, source_target_pairs={{0,1},{1,0},{2,3},{3,2},{4,5},{5,4},{6,7},{7,6},{8,9},{9,8},{10,11... | collective-permute-start | bytes 1806344 | tf_op jit(solution)/shard_map/ppermute | solution.py:513
  72.1 31.1 %collective-permute-start.23 = (bf16[112,2688]{1,0:T(8,128)(2,1)S(1)}, bf16[112,2688]{1,0:T(8,128)(2,1)S(1)}, u32[]{:S(2)}, u32[]{:S(2)}) collective-permute-start(bf16[112,2688]{1,0:T(8,128)(2,1)S(1)} %collective-permute-done.22.rest_4_), channel_id=1, source_target_pairs={{0,1},{1,0},{2,3},{3,2},{4,5},{5,4},{6,7},{7,6},{8,9},{9,8},{10,11... | collective-permute-start | bytes 1806344 | tf_op jit(solution)/shard_map/ppermute | solution.py:513
  86.7 17.3 %collective-permute-start.15 = (bf16[112,2688]{1,0:T(8,128)(2,1)S(1)}, bf16[112,2688]{1,0:T(8,128)(2,1)S(1)}, u32[]{:S(2)}, u32[]{:S(2)}) collective-permute-start(bf16[112,2688]{1,0:T(8,128)(2,1)S(1)} %collective-permute-done.14.rest_6_), channel_id=1, source_target_pairs={{0,1},{1,0},{2,3},{3,2},{4,5},{5,4},{6,7},{7,6},{8,9},{9,8},{10,11... | collective-permute-start | bytes 1806344 | tf_op jit(solution)/shard_map/ppermute | solution.py:513
  100.4 19.3 %collective-permute-start.1 = (bf16[256,1024]{1,0:T(8,128)(2,1)S(1)}, bf16[256,1024]{1,0:T(8,128)(2,1)S(1)}, u32[]{:S(2)}, u32[]{:S(2)}) collective-permute-start(bf16[256,1024]{1,0:T(8,128)(2,1)S(1)} %get-tuple-element.53), channel_id=1, source_target_pairs={{0,2},{2,0},{4,6},{6,4},{1,3},{3,1},{5,7},{7,5},{8,10},{10,8},{12,... | collective-permute-start | bytes 1572872 | tf_op jit(solution)/shard_map/ppermute | solution.py:451
  102.0 19.0 %collective-permute-start.2 = (bf16[256,1024]{1,0:T(8,128)(2,1)S(1)}, bf16[256,1024]{1,0:T(8,128)(2,1)S(1)}, u32[]{:S(2)}, u32[]{:S(2)}) collective-permute-start(bf16[256,1024]{1,0:T(8,128)(2,1)S(1)} %get-tuple-element.54), channel_id=1, source_target_pairs={{0,4},{2,6},{4,0},{6,2},{1,5},{3,7},{5,1},{7,3},{8,12},{10,14},{12... | collective-permute-start | bytes 1572872 | tf_op jit(solution)/shard_map/ppermute | solution.py:451
  103.2 24.8 %collective-permute-start.4 = (bf16[256,1024]{1,0:T(8,128)(2,1)S(1)}, bf16[256,1024]{1,0:T(8,128)(2,1)S(1)}, u32[]{:S(2)}, u32[]{:S(2)}) collective-permute-start(bf16[256,1024]{1,0:T(8,128)(2,1)S(1)} %collective-permute-done.x0), channel_id=1, source_target_pairs={{0,4},{2,6},{4,0},{6,2},{1,5},{3,7},{5,1},{7,3},{8,12},{10,14},{12... | collective-permute-start | bytes 1572872 | tf_op jit(solution)/shard_map/ppermute | solution.py:451
  104.0 25.2 %collective-permute-start.5 = (bf16[256,1024]{1,0:T(8,128)(2,1)S(1)}, bf16[256,1024]{1,0:T(8,128)(2,1)S(1)}, u32[]{:S(2)}, u32[]{:S(2)}) collective-permute-start(bf16[256,1024]{1,0:T(8,128)(2,1)S(1)} %collective-permute-done.3.y1), channel_id=1, source_target_pairs={{0,2},{2,0},{4,6},{6,4},{1,3},{3,1},{5,7},{7,5},{8,10},{10,8},{12,... | collective-permute-start | bytes 1572872 | tf_op jit(solution)/shard_map/ppermute | solution.py:451
  118.1 26.0 %collective-permute-start.29 = (bf16[256,896]{1,0:T(8,128)(2,1)S(1)}, bf16[256,896]{1,0:T(8,128)(2,1)S(1)}, u32[]{:S(2)}, u32[]{:S(2)}) collective-permute-start(bf16[256,896]{1,0:T(8,128)(2,1)S(1)} %get-tuple-element.37.rest_0_), channel_id=1, source_target_pairs={{0,2},{2,0},{4,6},{6,4},{1,3},{3,1},{5,7},{7,5},{8,10},{10,8},{12,... | collective-permute-start | bytes 1376264 | tf_op jit(solution)/shard_map/ppermute | solution.py:451
  119.7 28.5 %collective-permute-start.31 = (bf16[256,896]{1,0:T(8,128)(2,1)S(1)}, bf16[256,896]{1,0:T(8,128)(2,1)S(1)}, u32[]{:S(2)}, u32[]{:S(2)}) collective-permute-start(bf16[256,896]{1,0:T(8,128)(2,1)S(1)} %get-tuple-element.37.rest_0_), channel_id=1, source_target_pairs={{0,4},{2,6},{4,0},{6,2},{1,5},{3,7},{5,1},{7,3},{8,12},{10,14},{12... | collective-permute-start | bytes 1376264 | tf_op jit(solution)/shard_map/ppermute | solution.py:451
  120.9 27.3 %collective-permute-start.30 = (bf16[256,896]{1,0:T(8,128)(2,1)S(1)}, bf16[256,896]{1,0:T(8,128)(2,1)S(1)}, u32[]{:S(2)}, u32[]{:S(2)}) collective-permute-start(bf16[256,896]{1,0:T(8,128)(2,1)S(1)} %get-tuple-element.38.rest_1_), channel_id=1, source_target_pairs={{0,2},{2,0},{4,6},{6,4},{1,3},{3,1},{5,7},{7,5},{8,10},{10,8},{12,... | collective-permute-start | bytes 1376264 | tf_op jit(solution)/shard_map/ppermute | solution.py:451
  128.0 19.7 %collective-permute-start.32 = (bf16[256,896]{1,0:T(8,128)(2,1)S(1)}, bf16[256,896]{1,0:T(8,128)(2,1)S(1)}, u32[]{:S(2)}, u32[]{:S(2)}) collective-permute-start(bf16[256,896]{1,0:T(8,128)(2,1)S(1)} %get-tuple-element.38.rest_1_), channel_id=1, source_target_pairs={{0,4},{2,6},{4,0},{6,2},{1,5},{3,7},{5,1},{7,3},{8,12},{10,14},{12... | collective-permute-start | bytes 1376264 | tf_op jit(solution)/shard_map/ppermute | solution.py:451
  144.1 17.4 %collective-permute-start.36 = (bf16[256,896]{1,0:T(8,128)(2,1)S(1)}, bf16[256,896]{1,0:T(8,128)(2,1)S(1)}, u32[]{:S(2)}, u32[]{:S(2)}) collective-permute-start(bf16[256,896]{1,0:T(8,128)(2,1)S(1)} %collective-permute-done.29.rest_0_), channel_id=1, source_target_pairs={{0,4},{2,6},{4,0},{6,2},{1,5},{3,7},{5,1},{7,3},{8,12},{10,14},{12... | collective-permute-start | bytes 1376264 | tf_op jit(solution)/shard_map/ppermute | solution.py:451
  157.9 23.1 %collective-permute-start.33 = (bf16[256,1024]{1,0:T(8,128)(2,1)S(1)}, bf16[256,1024]{1,0:T(8,128)(2,1)S(1)}, u32[]{:S(2)}, u32[]{:S(2)}) collective-permute-start(bf16[256,1024]{1,0:T(8,128)(2,1)S(1)} %get-tuple-element.44), channel_id=1, source_target_pairs={{0,2},{2,0},{4,6},{6,4},{1,3},{3,1},{5,7},{7,5},{8,10},{10,8},{12,... | collective-permute-start | bytes 1572872 | tf_op jit(solution)/shard_map/ppermute | solution.py:451
  160.7 19.0 %collective-permute-start.28 = (bf16[128,1024]{1,0:T(8,128)(2,1)S(1)}, bf16[128,1024]{1,0:T(8,128)(2,1)S(1)}, u32[]{:S(2)}, u32[]{:S(2)}) collective-permute-start(bf16[128,1024]{1,0:T(8,128)(2,1)S(1)} %get-tuple-element.42), channel_id=1, source_target_pairs={{0,6},{2,4},{4,2},{6,0},{1,7},{3,5},{5,3},{7,1},{8,14},{10,12},{12... | collective-permute-start | bytes 786440 | tf_op jit(solution)/shard_map/ppermute | solution.py:451
  161.5 40.7 %collective-permute-start.34 = (bf16[256,1024]{1,0:T(8,128)(2,1)S(1)}, bf16[256,1024]{1,0:T(8,128)(2,1)S(1)}, u32[]{:S(2)}, u32[]{:S(2)}) collective-permute-start(bf16[256,1024]{1,0:T(8,128)(2,1)S(1)} %get-tuple-element.45), channel_id=1, source_target_pairs={{0,4},{2,6},{4,0},{6,2},{1,5},{3,7},{5,1},{7,3},{8,12},{10,14},{12... | collective-permute-start | bytes 1572872 | tf_op jit(solution)/shard_map/ppermute | solution.py:451
  162.7 39.5 %collective-permute-start.35 = (bf16[256,1024]{1,0:T(8,128)(2,1)S(1)}, bf16[256,1024]{1,0:T(8,128)(2,1)S(1)}, u32[]{:S(2)}, u32[]{:S(2)}) collective-permute-start(bf16[256,1024]{1,0:T(8,128)(2,1)S(1)} %get-tuple-element.46), channel_id=1, source_target_pairs={{0,6},{2,4},{4,2},{6,0},{1,7},{3,5},{5,3},{7,1},{8,14},{10,12},{12... | collective-permute-start | bytes 1572872 | tf_op jit(solution)/shard_map/ppermute | solution.py:451
  170.0 32.2 %collective-permute-start.38 = (bf16[128,1024]{1,0:T(8,128)(2,1)S(1)}, bf16[128,1024]{1,0:T(8,128)(2,1)S(1)}, u32[]{:S(2)}, u32[]{:S(2)}) collective-permute-start(bf16[128,1024]{1,0:T(8,128)(2,1)S(1)} %get-tuple-element.48), channel_id=1, source_target_pairs={{0,2},{2,0},{4,6},{6,4},{1,3},{3,1},{5,7},{7,5},{8,10},{10,8},{12,... | collective-permute-start | bytes 786440 | tf_op jit(solution)/shard_map/ppermute | solution.py:451
  179.7 25.3 %collective-permute-start.39 = (bf16[128,1024]{1,0:T(8,128)(2,1)S(1)}, bf16[128,1024]{1,0:T(8,128)(2,1)S(1)}, u32[]{:S(2)}, u32[]{:S(2)}) collective-permute-start(bf16[128,1024]{1,0:T(8,128)(2,1)S(1)} %get-tuple-element.49), channel_id=1, source_target_pairs={{0,4},{2,6},{4,0},{6,2},{1,5},{3,7},{5,1},{7,3},{8,12},{10,14},{12... | collective-permute-start | bytes 786440 | tf_op jit(solution)/shard_map/ppermute | solution.py:451
  181.0 24.0 %collective-permute-start.40 = (bf16[128,1024]{1,0:T(8,128)(2,1)S(1)}, bf16[128,1024]{1,0:T(8,128)(2,1)S(1)}, u32[]{:S(2)}, u32[]{:S(2)}) collective-permute-start(bf16[128,1024]{1,0:T(8,128)(2,1)S(1)} %get-tuple-element.50), channel_id=1, source_target_pairs={{0,6},{2,4},{4,2},{6,0},{1,7},{3,5},{5,3},{7,1},{8,14},{10,12},{12... | collective-permute-start | bytes 786440 | tf_op jit(solution)/shard_map/ppermute | solution.py:451
  (23 other events, 256.3 us)
where the time goes:
time: 207 us
  waiting for transfers between devices  105 us (51%)
  Pallas kernels  50.7 us (24%)
  starting transfers between devices  42 us (20%)
  local copies, waits for them, and re-layouts  9.6 us (5%)
    ppermute x27, waiting for transfers between devices, to(): return lax.ppermute(value, 'head', [(i, i ^ k) for i in range(4)])  77.7 us
    pallas_call x9, Pallas kernels, call(): pl.pallas_call(kernel, out_shape=out_shape, in_specs=in_specs, out_specs=...  49 us
    ppermute x27, starting transfers between devices, to(): return lax.ppermute(value, 'head', [(i, i ^ k) for i in range(4)])  29.9 us
    ppermute x6, waiting for transfers between devices, fast(): now = lax.ppermute(now, 'span', ring)  26.9 us
    ppermute x6, starting transfers between devices, fast(): now = lax.ppermute(now, 'span', ring)  11 us
    unnamed x29, local copies, waits for them, and re-layouts  8.2 us
  transfers between devices with their start and end apart: 41, of which 11 were waited for; matrix products, arithmetic and copies ran while one was open for 1% of the time, Pallas kernels for 23%

commit v1 on v0

--- a/solution.py
+++ b/solution.py
@@ -167,6 +167,27 @@
 
 def head_index():
     return lax.axis_index("head").astype(jnp.int32)
+
+
+def square_place():
+    me = head_index()
+    return me % 2, me // 2
+
+
+def cut_kernel(weights, query_part, half_part, last_part, sems):
+    _, y = square_place()
+    width = half_part.shape[1]
+    first = query_part.shape[1]
+    copies = []
+    for i, (start, part) in enumerate(
+        ((0, query_part), (first + y * width, half_part), (first + 2 * width, last_part))
+    ):
+        cols = pl.ds(pl.multiple_of(start, HEAD_DIM), part.shape[1])
+        copies.append(pltpu.make_async_copy(weights.at[:, cols], part, sems.at[i]))
+    for c in copies:
+        c.start()
+    for c in copies:
+        c.wait()
 
 
 def pairings(items):
@@ -271,32 +292,61 @@
         c.wait()
 
 
-def context_kernel(assign, x, w, *rest):
-    outs, buf = rest[:4], rest[4]
+def context_kernel(assign, x, w, own, to_x, to_y, for_y, for_x, buf, sems):
     me = head_index()
     width = w.shape[1]
     half = width // 2
     for c in range(2):
         cols = slice(c * half, (c + 1) * half)
         buf[:, cols] = dot(x[...], w[:, cols]).astype(jnp.bfloat16)
-    for k in range(4):
-        for i in range(2):
+    copies = []
+    for out, parts in (
+        (to_x, ((1, 0), (3, 0))),
+        (to_y, ((2, 1), (3, 1))),
+        (for_y, ((2, 0),)),
+        (for_x, ((1, 1),)),
+        (own, ((0, 0), (0, 1))),
+    ):
+        for n, (k, i) in enumerate(parts):
             start = pl.multiple_of(assign[(me ^ k) * 2 + i] * SPAN_LEN, SPAN_LEN)
-            outs[k][i * SPAN_LEN : (i + 1) * SPAN_LEN, :] = buf[pl.ds(start, SPAN_LEN), :]
-
-
-def load_pieces(n_span, pieces, held, sems):
+            rows = out.at[pl.ds(n * SPAN_LEN, SPAN_LEN), :]
+            part = buf.at[pl.ds(start, SPAN_LEN), :]
+            copies.append(pltpu.make_async_copy(part, rows, sems.at[len(copies)]))
+            copies[-1].start()
+    for c in copies:
+        c.wait()
+
+
+def load_pieces(n_span, first, pieces, held, sems):
     z = lax.axis_index("span").astype(jnp.int32)
     g = lax.axis_index("group").astype(jnp.int32)
+    x, y = square_place()
     rows = pieces[0].shape[0]
     copies = []
+    split = (len(pieces) - 2) // (2 * (n_span - 1))
     for i, piece in enumerate(pieces):
-        spot = lax.rem(z + (n_span - i // 2), n_span) * 2 + (g ^ (i % 2))
+        if i < 2:
+            r, other, cols = 0, i, slice(None)
+            piece = piece.at[:, pl.ds(first, held.shape[1])]
+        else:
+            r, rest = 1 + (i - 2) // (2 * split), (i - 2) % (2 * split)
+            other = rest % 2
+            cols = slice(None)
+            if split == 2:
+                place = y if half_axis(n_span, r) else x
+                block = place if rest < 2 else 1 - place
+                width = held.shape[1] // 2
+                cols = pl.ds(pl.multiple_of(block * width, width), width)
+        spot = lax.rem(z + (n_span - r), n_span) * 2 + (g ^ other)
         start = pl.multiple_of(spot * rows, rows)
         copies.append(
-            pltpu.make_async_copy(piece, held.at[pl.ds(start, rows), :], sems.at[i])
+            pltpu.make_async_copy(piece, held.at[pl.ds(start, rows), cols], sems.at[i])
         )
     return copies
+
+
+def half_axis(n_span, r):
+    return min(r, n_span - 2) % 2
 
 
 def self_kernel(n_span, assign, owners, places, store, r1, r2, r3, *rest):
@@ -304,7 +354,7 @@
     source, within, held, triple, scores, weights, sem_s, sem_w = rest[2 * n_span :]
     me = head_index()
     per = 2 * NEIGHBOURS
-    copies = load_pieces(n_span, pieces, held, sem_w)
+    copies = load_pieces(n_span, 0, pieces, held, sem_w)
     mine = neighbours_of(assign, owners, places, me)
     for j, (owner, place) in enumerate(mine):
         at = source.at[pl.ds(j * RETRIEVED, RETRIEVED), :]
@@ -336,42 +386,51 @@
     attend_many(units, scores, weights)
 
 
-def cross_kernel(n_span, source, within, c0, c1, c2, c3, *rest):
-    pieces = rest[: 2 * n_span]
-    outs = rest[2 * n_span : -8]
-    held, context, middle, asking, across, scores, weights, sem_w = rest[-8:]
-    copies = load_pieces(n_span, pieces, held, sem_w)
+def cross_kernel(n_span, first, source, within, own, from_x, from_y, last_y, last_x, *rest):
+    pieces = rest[: 4 * n_span - 2]
+    middle, across, held, context, asking, scores, weights, sem_w = rest[4 * n_span - 2 :]
+    copies = load_pieces(n_span, first, pieces, held, sem_w)
     for c in copies:
         c.start()
     breadth = source.shape[1]
-    total = c0[...].astype(jnp.float32) + c1[...].astype(jnp.float32)
-    total = total + (c2[...].astype(jnp.float32) + c3[...].astype(jnp.float32))
-    context[...] = total.astype(jnp.bfloat16)
+    for i, (near, far) in enumerate(((from_x, last_y), (from_y, last_x))):
+        at = slice(i * SPAN_LEN, (i + 1) * SPAN_LEN)
+        total = own[at, :].astype(jnp.float32) + near[:SPAN_LEN, :].astype(jnp.float32)
+        context[at, :] = (total + far[...].astype(jnp.float32)).astype(jnp.bfloat16)
     for c in copies:
         c.wait()
     middle[...] = (
         source[...].astype(jnp.float32) + dot(within[...], held[:, :breadth])
     ).astype(jnp.bfloat16)
-    asking[...] = dot(middle[...], held[:, breadth : 2 * breadth]).astype(jnp.bfloat16)
+    asking[...] = dot(middle[...], held[:, breadth:]).astype(jnp.bfloat16)
     span_rows = NEIGHBOURS * RETRIEVED
     units = []
-    for s in range(len(outs)):
+    for s in range(2):
         rows = slice(s * span_rows, (s + 1) * span_rows)
         keys = slice(s * SPAN_LEN, (s + 1) * SPAN_LEN)
         for c in range(0, breadth, HEAD_DIM):
             units.append(unit(asking, rows, c, context, keys, c, breadth + c, across))
     attend_many(units, scores, weights)
+
+
+def encoded_kernel(n_span, first, middle, across, *rest):
+    pieces = rest[: 2 * n_span]
+    outs, held, sem_w = rest[2 * n_span : -2], rest[-2], rest[-1]
+    copies = load_pieces(n_span, first, pieces, held, sem_w)
+    for c in copies:
+        c.start()
+    for c in copies:
+        c.wait()
+    span_rows = NEIGHBOURS * RETRIEVED
+    total = middle[...].astype(jnp.float32) + dot(across[...], held[...])
     for s, out in enumerate(outs):
-        rows = slice(s * span_rows, (s + 1) * span_rows)
-        out[...] = (
-            middle[rows, :].astype(jnp.float32) + dot(across[rows, :], held[:, 2 * breadth :])
-        ).astype(jnp.bfloat16)
-
-
-def query_kernel(own, x0, x1, y0, y1, d0, d1, w, out, held, total, sems):
+        out[...] = total[s * span_rows : (s + 1) * span_rows, :].astype(jnp.bfloat16)
+
+
+def query_kernel(own, from_x, from_y, d0, d1, w, out, held, total, sems):
     me = head_index()
     width = own.shape[1]
-    half = x0.shape[0]
+    half = d0.shape[0]
     copies = []
     for k in range(4):
         start = pl.multiple_of((me ^ k) * width, width)
@@ -382,31 +441,32 @@
         c.start()
     copies[0].wait()
     total[...] = dot(own[...], held[0])
-    for k, (a, b) in enumerate(((x0, x1), (y0, y1), (d0, d1))):
+    for k, from_k in enumerate((from_x, from_y)):
         copies[k + 1].wait()
-        total[:half, :] += dot(a[...], held[k + 1])
-        total[half:, :] += dot(b[...], held[k + 1])
+        total[...] += dot(from_k[...], held[k + 1])
+    copies[3].wait()
+    total[:half, :] += dot(d0[...], held[3])
+    total[half:, :] += dot(d1[...], held[3])
     out[...] = total[...].astype(jnp.bfloat16)
 
 
-def span_kernel(relations, assign, queries, *rest):
-    n = 2 * len(relations)
-    encs = rest[:n]
-    pair, held = rest[n : n + 2]
-    outs = rest[n + 2 : n + 6]
-    q, keep, memory, att, scores, weights, sem = rest[n + 6 :]
+CHUNKS = (((0, 0), (1, 0), (0, 1), (2, 1)), ((2, 0), (3, 0), (1, 1), (3, 1)))
+
+
+def attend_spans(spans, assign, queries, encs, pair, att, rows_of, scratch):
+    q, keep, memory, scores, weights, sem = scratch
     me = head_index()
     local = q.shape[1]
     span_rows = NEIGHBOURS * RETRIEVED
     loads = []
-    for i in range(n):
-        span = assign[(me ^ relations[i // 2]) * 2 + i % 2]
+    for s, (relation, i) in enumerate(spans):
+        span = assign[(me ^ relation) * 2 + i]
         at = pl.ds(pl.multiple_of(span * SPAN_LEN, SPAN_LEN), SPAN_LEN)
-        to_rows = pl.ds(i * SPAN_LEN, SPAN_LEN)
-        loads.append(pltpu.make_async_copy(queries.at[at, :], q.at[to_rows, :], sem.at[i]))
+        to_rows = pl.ds(rows_of[s] * SPAN_LEN, SPAN_LEN)
+        loads.append(pltpu.make_async_copy(queries.at[at, :], q.at[to_rows, :], sem.at[s]))
     for c in loads:
         c.start()
-    for s in range(n):
+    for s in range(len(spans)):
         keep[s * span_rows : (s + 1) * span_rows, :] = encs[s][...]
     for c in range(2):
         cols = slice(c * local, (c + 1) * local)
@@ -414,37 +474,73 @@
     for c in loads:
         c.wait()
     units = []
-    for s in range(n):
-        r = slice(s * SPAN_LEN, (s + 1) * SPAN_LEN)
+    for s in range(len(spans)):
+        r = slice(rows_of[s] * SPAN_LEN, (rows_of[s] + 1) * SPAN_LEN)
         m = slice(s * span_rows, (s + 1) * span_rows)
         for c in range(0, local, HEAD_DIM):
             units.append(unit(q, r, c, memory, m, c, local + c, att))
     attend_many(units, scores, weights)
-    width = outs[0].shape[1]
+
+
+def early_kernel(spans, assign, queries, *rest):
+    n = len(spans)
+    attend_spans(spans, assign, queries, rest[:n], rest[n], rest[n + 1], range(n), rest[n + 2 :])
+
+
+def span_kernel(chunk, early, assign, queries, *rest):
+    late = [s for s in range(len(chunk)) if s not in early]
+    n = len(late)
+    encs, rest = rest[:n], rest[n:]
+    if early:
+        before, rest = rest[0], rest[1:]
+    pair, held, keep_a, keep_b, to_x, to_y, att = rest[:7]
+    me = head_index()
+    for i, s in enumerate(early):
+        att[s * SPAN_LEN : (s + 1) * SPAN_LEN, :] = before[i * SPAN_LEN : (i + 1) * SPAN_LEN, :]
+    attend_spans([chunk[s] for s in late], assign, queries, encs, pair, att, late, rest[7:])
+    width = keep_a.shape[1] // 2
+    one = SPAN_LEN
+    low, high = slice(0, width), slice(width, 2 * width)
+    places = (
+        ((keep_a, low, False), (keep_b, low, False)),
+        ((to_x, low, True), (keep_b, high, False)),
+        ((keep_a, high, False), (to_y, low, True)),
+        ((to_x, high, True), (to_y, high, True)),
+    )
     for k in range(4):
         start = pl.multiple_of((me ^ k) * width, width)
-        outs[k][...] = dot(att[...], held[:, pl.ds(start, width)]).astype(jnp.bfloat16)
+        term = dot(att[...], held[:, pl.ds(start, width)]).astype(jnp.bfloat16)
+        for side, (out, cols, swapped) in enumerate(places[k]):
+            first = term[2 * side * one : (2 * side + 1) * one, :]
+            second = term[(2 * side + 1) * one : (2 * side + 2) * one, :]
+            out[:one, cols] = second if swapped else first
+            out[one:, cols] = first if swapped else second
 
 
 def final_kernel(assign, states, *rest):
-    terms, out = rest[:12], rest[12]
+    terms, out = rest[:-1], rest[-1]
     me = head_index()
-    chunk_of = ((0, 0), (1, 0), (1, 1), (2, 0))
-    for m, i in ((m, i) for m in range(4) for i in range(2)):
-        span = assign[(me ^ m) * 2 + i]
-        at = pl.ds(pl.multiple_of(span * SPAN_LEN, SPAN_LEN), SPAN_LEN)
-        parts = []
-        for k in range(4):
-            chunk, part = chunk_of[k ^ m]
-            start = (2 * part + i) * SPAN_LEN
-            term = terms[4 * chunk + k][start : start + SPAN_LEN, :]
-            parts.append(term.astype(jnp.float32))
-        total = (parts[0] + parts[1]) + (parts[2] + parts[3])
-        out[at, :] = (states[at, :].astype(jnp.float32) + total).astype(jnp.bfloat16)
+    width = out.shape[1]
+    for c, chunk in enumerate(CHUNKS):
+        for s, (relation, i) in enumerate(chunk):
+            side, row = s // 2, (s % 2) * SPAN_LEN
+            near = slice(row, row + SPAN_LEN)
+            span = assign[(me ^ relation) * 2 + i]
+            at = pl.ds(pl.multiple_of(span * SPAN_LEN, SPAN_LEN), SPAN_LEN)
+            kept, arrived = terms[6 * c + side], terms[6 * c + 2 + side]
+            last = terms[6 * (1 - c) + 4 + side]
+            total = kept[near, :width].astype(jnp.float32)
+            total = total + arrived[near, :width].astype(jnp.float32)
+            total = total + last[near, :].astype(jnp.float32)
+            out[at, :] = (states[at, :].astype(jnp.float32) + total).astype(jnp.bfloat16)
 
 
 def shape(*dims):
     return jax.ShapeDtypeStruct(dims, jnp.bfloat16)
+
+
+def add(a, b):
+    return (a.astype(jnp.float32) + b.astype(jnp.float32)).astype(jnp.bfloat16)
 
 
 def to(k, value):
@@ -470,7 +566,49 @@
     own_spans = span_count // 4
     local = query_weight.shape[1]
     store = stored.reshape(stored.shape[3], RETRIEVED, ENC_WIDTH)
-    owners, places = owners.T, places.T
+    owners, slots = owners.T, places.T
+
+    starts = (0, 3 * ENC_WIDTH, 5 * ENC_WIDTH)
+    widths = (3 * ENC_WIDTH, 2 * ENC_WIDTH, ENC_WIDTH)
+    rows_w = encoder_weights.shape[0]
+    cut = call(
+        cut_kernel,
+        [shape(rows_w, widths[0]), shape(rows_w, ENC_WIDTH), shape(rows_w, ENC_WIDTH)],
+        [HBM],
+        [VMEM] * 3,
+        [pltpu.SemaphoreType.DMA((3,))],
+        8,
+        2 * 10**9,
+        encoder_weights,
+    )
+    h = lax.axis_index("head")
+    places = (h % 2, h // 2)
+
+    def ring(value):
+        return lax.ppermute(value, "span", [(i, (i + 1) % n_span) for i in range(n_span)])
+
+    def swap(value):
+        return lax.ppermute(value, "group", [(0, 1), (1, 0)])
+
+    partner = swap(encoder_weights)
+    parts = [[encoder_weights, partner] for _ in starts]
+    whole, near, last = cut
+    far = None
+    for r in range(1, n_span):
+        whole = ring(whole)
+        if r < n_span - 1:
+            if r > 1:
+                same = places[half_axis(n_span, r)] == places[half_axis(n_span, r - 1)]
+                near = jnp.where(same, near, far)
+            near = ring(near)
+            far = to(1 + half_axis(n_span, r), near)
+        else:
+            near, far = ring(near), ring(far)
+        last = ring(last)
+        parts[0] += [whole, swap(whole)]
+        parts[1] += [near, swap(near), far, swap(far)]
+        parts[2] += [last, swap(last)]
+    n_pieces = [len(p) for p in parts]
 
     table = jnp.asarray(pair_table(span_count))
     assign = pl.pallas_call(
@@ -496,90 +634,92 @@
         4 * 10**9,
         assign,
         owners,
-        places,
+        slots,
         store,
     )
     raw = [to(k + 1, sends[k]) for k in range(3)]
 
-    cut = 3 * ENC_WIDTH
-    ring = [(i, (i + 1) % n_span) for i in range(n_span)]
-    halves = []
-    for part in (encoder_weights[:, :cut], encoder_weights[:, cut:]):
-        pieces, now = [], part
-        for r in range(n_span):
-            if r:
-                now = lax.ppermute(now, "span", ring)
-            pieces.append(now)
-            pieces.append(lax.ppermute(now, "group", [(0, 1), (1, 0)]))
-        halves.append(pieces)
-    n_pieces = 2 * n_span
-
     width_c = context_weight.shape[1]
-    rows_c = tokens // 4
-    part_c = call(
+    rows_c = own_spans * SPAN_LEN
+    own_c, to_x, to_y, for_y, for_x = call(
         context_kernel,
-        [shape(rows_c, width_c)] * 4,
+        [shape(rows_c, width_c)] * 3 + [shape(SPAN_LEN, width_c)] * 2,
         [SMEM, VMEM, VMEM],
-        [VMEM] * 4,
-        [pltpu.VMEM((tokens, width_c), bf16)],
+        [HBM] * 5,
+        [pltpu.VMEM((tokens, width_c), bf16), pltpu.SemaphoreType.DMA((8,))],
         16,
         2 * tokens * feat * width_c,
         assign,
         states,
         context_weight,
     )
-    context = [part_c[0]] + [to(k, part_c[k]) for k in range(1, 4)]
+    from_x, from_y = to(1, to_x), to(2, to_y)
+    last_y = add(for_y, from_x[SPAN_LEN:])
+    last_x = add(for_x, from_y[SPAN_LEN:])
+    last_y, last_x = to(2, last_y), to(1, last_x)
+    context = [own_c, from_x, from_y, last_y, last_x]
 
     half_t = tokens // 2
-    s0, s1 = states[:half_t], states[half_t:]
-    x0, y1 = to(1, s0), to(2, s1)
-    x1, y0 = to(1, s1), to(2, s0)
-    d0, d1 = to(2, x0), to(1, y1)
+    states_x, states_y = to(1, states), to(2, states)
+    d0, d1 = to(2, states_x[:half_t]), to(1, states_y[half_t:])
 
     source, within = call(
         functools.partial(self_kernel, n_span),
         [shape(per * RETRIEVED, ENC_WIDTH)] * 2,
-        [SMEM] * 3 + [HBM] * (4 + n_pieces),
+        [SMEM] * 3 + [HBM] * (4 + n_pieces[0]),
         [VMEM] * 2,
         [
-            pltpu.VMEM((ENC_WIDTH, cut), bf16),
-            pltpu.VMEM((per * RETRIEVED, cut), bf16),
+            pltpu.VMEM((ENC_WIDTH, widths[0]), bf16),
+            pltpu.VMEM((per * RETRIEVED, widths[0]), bf16),
             pltpu.VMEM((per * ENC_WIDTH, RETRIEVED), jnp.float32),
             pltpu.VMEM((per * ENC_WIDTH, RETRIEVED), bf16),
             pltpu.SemaphoreType.DMA((per,)),
-            pltpu.SemaphoreType.DMA((n_pieces,)),
+            pltpu.SemaphoreType.DMA((n_pieces[0],)),
         ],
         20,
-        4 * per * RETRIEVED * ENC_WIDTH * cut,
+        4 * per * RETRIEVED * ENC_WIDTH * widths[0],
         assign,
         owners,
-        places,
+        slots,
         store,
         *raw,
-        *halves[0],
+        *parts[0],
     )
     span_rows = NEIGHBOURS * RETRIEVED
-    enc = call(
-        functools.partial(cross_kernel, n_span),
-        [shape(span_rows, ENC_WIDTH)] * own_spans,
-        [VMEM] * 6 + [HBM] * n_pieces,
-        [VMEM] * own_spans,
+    middle, across = call(
+        functools.partial(cross_kernel, n_span, starts[1]),
+        [shape(per * RETRIEVED, ENC_WIDTH)] * 2,
+        [VMEM] * 7 + [HBM] * n_pieces[1],
+        [VMEM] * 2,
         [
-            pltpu.VMEM((ENC_WIDTH, cut), bf16),
+            pltpu.VMEM((ENC_WIDTH, widths[1]), bf16),
             pltpu.VMEM((rows_c, width_c), bf16),
-            pltpu.VMEM((per * RETRIEVED, ENC_WIDTH), bf16),
-            pltpu.VMEM((per * RETRIEVED, ENC_WIDTH), bf16),
             pltpu.VMEM((per * RETRIEVED, ENC_WIDTH), bf16),
             pltpu.VMEM((per * ENC_WIDTH, SPAN_LEN), jnp.float32),
             pltpu.VMEM((per * ENC_WIDTH, SPAN_LEN), bf16),
-            pltpu.SemaphoreType.DMA((n_pieces,)),
+            pltpu.SemaphoreType.DMA((n_pieces[1],)),
         ],
         20,
-        4 * per * RETRIEVED * ENC_WIDTH * cut,
+        4 * per * RETRIEVED * ENC_WIDTH * widths[1],
         source,
         within,
         *context,
-        *halves[1],
+        *parts[1],
+    )
+    enc = call(
+        functools.partial(encoded_kernel, n_span, starts[2]),
+        [shape(span_rows, ENC_WIDTH)] * own_spans,
+        [VMEM] * 2 + [HBM] * n_pieces[2],
+        [VMEM] * own_spans,
+        [
+            pltpu.VMEM((ENC_WIDTH, widths[2]), bf16),
+            pltpu.SemaphoreType.DMA((n_pieces[2],)),
+        ],
+        16,
+        4 * per * RETRIEVED * ENC_WIDTH * widths[2],
+        middle,
+        across,
+        *parts[2],
     )
     first = own_spans // 2
     x = [to(1, e) for e in enc]
@@ -590,7 +730,7 @@
     queries = call(
         query_kernel,
         shape(tokens, local),
-        [VMEM] * 7 + [HBM],
+        [VMEM] * 5 + [HBM],
         VMEM,
         [
             pltpu.VMEM((4, feat, local), bf16),
@@ -600,43 +740,66 @@
         24,
         8 * tokens * feat * local,
         states,
-        x0,
-        x1,
-        y0,
-        y1,
+        states_x,
+        states_y,
         d0,
         d1,
         query_weight,
     )
     w_pair = neighbour_weight.reshape(ENC_WIDTH, 2 * local)
-    arrived = []
-    for relations, chunk in (((0,), enc), ((1, 2), x + y), ((3,), d)):
-        spans = len(chunk)
-        rows = spans * SPAN_LEN
-        terms = call(
-            functools.partial(span_kernel, relations),
-            [shape(rows, feat)] * 4,
-            [SMEM, HBM] + [VMEM] * (spans + 2),
+    encoded = (enc, x, y, d)
+
+    def scratch(spans, rows):
+        return [
+            pltpu.VMEM((rows * SPAN_LEN, local), bf16),
+            pltpu.VMEM((spans * span_rows, ENC_WIDTH), bf16),
+            pltpu.VMEM((spans * span_rows, 2 * local), bf16),
+            pltpu.VMEM((spans * SPAN_LEN * local // HEAD_DIM, span_rows), jnp.float32),
+            pltpu.VMEM((spans * SPAN_LEN * local // HEAD_DIM, span_rows), bf16),
+            pltpu.SemaphoreType.DMA((spans,)),
+        ]
+
+    terms = []
+    for chunk, early in zip(CHUNKS, ((), (0, 2))):
+        rows = len(chunk) * SPAN_LEN
+        given = []
+        if early:
+            spans = [chunk[s] for s in early]
+            given.append(
+                call(
+                    functools.partial(early_kernel, spans),
+                    shape(len(early) * SPAN_LEN, local),
+                    [SMEM, HBM] + [VMEM] * (len(early) + 1),
+                    VMEM,
+                    scratch(len(early), len(early)),
+                    24,
+                    4 * len(early) * span_rows * ENC_WIDTH * 2 * local,
+                    assign,
+                    queries,
+                    *(encoded[relation][i] for relation, i in spans),
+                    w_pair,
+                )
+            )
+        late = [chunk[s] for s in range(len(chunk)) if s not in early]
+        keep_a, keep_b, to_x, to_y = call(
+            functools.partial(span_kernel, chunk, early),
+            [shape(rows // 2, 2 * feat)] * 4,
+            [SMEM, HBM] + [VMEM] * (len(late) + len(given) + 2),
             [VMEM] * 4,
-            [
-                pltpu.VMEM((rows, local), bf16),
-                pltpu.VMEM((spans * span_rows, ENC_WIDTH), bf16),
-                pltpu.VMEM((spans * span_rows, 2 * local), bf16),
-                pltpu.VMEM((rows, local), bf16),
-                pltpu.VMEM((rows * local // HEAD_DIM, span_rows), jnp.float32),
-                pltpu.VMEM((rows * local // HEAD_DIM, span_rows), bf16),
-                pltpu.SemaphoreType.DMA((spans,)),
-            ],
+            [pltpu.VMEM((rows, local), bf16)] + scratch(len(late), len(chunk)),
             32,
-            4 * spans * span_rows * ENC_WIDTH * 2 * local,
+            4 * len(late) * span_rows * ENC_WIDTH * 2 * local,
             assign,
             queries,
-            *chunk,
+            *(encoded[relation][i] for relation, i in late),
+            *given,
             w_pair,
             output_weight,
         )
-        arrived.append(terms[0])
-        arrived += [to(k, terms[k]) for k in range(1, 4)]
+        near_x, near_y = to(1, to_x), to(2, to_y)
+        last_y = to(2, add(keep_a[:, feat:], near_x[:, feat:]))
+        last_x = to(1, add(keep_b[:, feat:], near_y[:, feat:]))
+        terms += [keep_a, keep_b, near_x, near_y, last_y, last_x]
     return call(
         final_kernel,
         shape(tokens, feat),
@@ -647,14 +810,14 @@
         17 * tokens * feat,
         assign,
         states,
-        *arrived,
+        *terms,
     )
 
 
 def solution(mesh):
     sizes = mesh.shape
     n_head, n_span = sizes["head"], sizes["span"]
-    square = n_head == 4 and sizes["group"] == 2
+    square = n_head == 4 and sizes["group"] == 2 and n_span >= 3
 
     def per_device(*args):
         spans = args[1].shape[0]

time: 207 us -> 207 us (level)
  starting transfers between devices: 42 us -> 34.7 us
  waiting for transfers between devices: 105 us -> 109 us
  Pallas kernels: 50.7 us -> 53.3 us
    ppermute x14 -> x23, waiting for transfers between devices: 26.9 us -> 53.9 us  [the longest x10 52.8 us: ring(): lax.ppermute(value, 'span', [(i, (i + 1) % n_span) for i in range(n_span)])]
    ppermute x27, waiting for transfers between devices: 77.7 us -> 54.8 us  [to(): return lax.ppermute(value, 'head', [(i, i ^ k) for i in range(4)])]
    ppermute x27, starting transfers between devices: 29.9 us -> 26.1 us  [to(): return lax.ppermute(value, 'head', [(i, i ^ k) for i in range(4)])]
    ppermute x14 -> x23, starting transfers between devices: 12.2 us -> 8.53 us  [the longest x10 6.71 us: ring(): lax.ppermute(value, 'span', [(i, (i + 1) % n_span) for i in range(n_span)])]
    pallas_call x9 -> x11, Pallas kernels: 49 us -> 51.7 us  [call(): pl.pallas_call(kernel, out_shape=out_shape, in_specs=in_specs, out_specs=...]
    unnamed x29 -> x41, local copies, waits for them, and re-layouts: 8.2 us -> 9.21 us
  transfers between devices with their start and end apart: 41 -> 50, of which waited for: 11 -> 17; matrix products, arithmetic and copies ran while one was open for 1% -> 1% of each run, Pallas kernels for 23% -> 24%
where the time goes in v1:
time: 207 us
  waiting for transfers between devices  109 us (53%)
  Pallas kernels  53.3 us (26%)
  starting transfers between devices  34.7 us (17%)
  local copies, waits for them, and re-layouts  9.28 us (4%)
    ppermute x27, waiting for transfers between devices, to(): return lax.ppermute(value, 'head', [(i, i ^ k) for i in range(4)])  54.8 us
    ppermute x10, waiting for transfers between devices, ring(): lax.ppermute(value, 'span', [(i, (i + 1) % n_span) for i in range(n_span)])  52.8 us
    pallas_call x11, Pallas kernels, call(): pl.pallas_call(kernel, out_shape=out_shape, in_specs=in_specs, out_specs=...  51.7 us
    ppermute x27, starting transfers between devices, to(): return lax.ppermute(value, 'head', [(i, i ^ k) for i in range(4)])  26.1 us
    unnamed x41, local copies, waits for them, and re-layouts  9.21 us
    ppermute x10, starting transfers between devices, ring(): lax.ppermute(value, 'span', [(i, (i + 1) % n_span) for i in range(n_span)])  6.71 us
  transfers between devices with their start and end apart: 50, of which 17 were waited for; matrix products, arithmetic and copies ran while one was open for 1% of the time, Pallas kernels for 24%

profile of v1, /device:TPU:0, one launch (start us, length us, event | category | flops | bytes accessed | tf_op | source)
XLA Modules:
  0.0 206.9 jit_solution(4004424133846586575)
XLA Ops:
  2.4 3.1 %collective-permute-start.18 = (bf16[112,896]{1,0:T(8,128)(2,1)S(1)}, bf16[112,896]{1,0:T(8,128)(2,1)S(1)}, u32[]{:S(2)}, u32[]{:S(2)}) collective-permute-start(bf16[112,896]{1,0:T(8,128)(2,1)S(1)} %get-tuple-element.41), channel_id=1, source_target_pairs={{0,8},{8,16},{16,24},{24,0},{1,9},{9,17},{17,25},{25,1},{2,10},{10... | collective-permute-start | bytes 602120 | tf_op jit(solution)/shard_map/ppermute | solution.py:588
  5.5 1.7 plan.1.assign
  7.8 2.0 copy-done.4
  9.9 4.7 %shard_map.104 = (bf16[128,1792]{1,0:T(8,128)(2,1)S(1)}, bf16[128,1792]{1,0:T(8,128)(2,1)}, bf16[128,1792]{1,0:T(8,128)(2,1)S(1)}, bf16[64,1792]{1,0:T(8,128)(2,1)S(1)}, bf16[64,1792]{1,0:T(8,128)(2,1)S(1)}) custom-call(s32[8]{0:T(128)S(1)} %copy-done.1, bf16[512,1024]{1,0:T(8,128)(2,1)S(1)} %copy-done, bf16[1024,1792]{1,0:T(8,128)(2,1)S(1)} %copy-done.4), custom_call_target="tpu_custom_call" | custom-call | flops 1879048192 | bytes 4718608 | tf_op jit(solution)/shard_map/pallas_call | solution.py:119
  16.9 1.6 collective-permute-start.30
  21.5 3.7 %shard_map.101 = (bf16[2,128,896]{2,1,0:T(8,128)(2,1)}, bf16[2,128,896]{2,1,0:T(8,128)(2,1)S(1)}, bf16[2,128,896]{2,1,0:T(8,128)(2,1)S(1)}) custom-call(s32[8]{0:T(128)S(1)} %copy-done.1, s32[2,8]{1,0:T(2,128)S(1)} %bitcast.11, s32[2,8]{1,0:T(2,128)S(1)} %bitcast.17, bf16[8,128,896]{2,1,0:T(8,128)(2,1)S(1)} %bitcast.15), custom_call_target="tpu_custom_call" | custom-call | flops 4000000000 | bytes 1835088 | tf_op jit(solution)/shard_map/pallas_call | solution.py:119
  27.3 1.6 collective-permute-start.8
  30.9 16.7 %collective-permute-done.32.rest_4_ = bf16[112,896]{1,0:T(8,128)(2,1)S(1)} collective-permute-done((bf16[112,896]{1,0:T(8,128)(2,1)}, bf16[112,896]{1,0:T(8,128)(2,1)S(1)}, u32[]{:S(2)}, u32[]{:S(2)}) %collective-permute-start.32) | collective-permute-done | bytes 200736 | tf_op jit(solution)/shard_map/ppermute | solution.py:588
  51.2 10.9 %collective-permute-done.6.r3 = bf16[2,128,896]{2,1,0:T(8,128)(2,1)S(1)} collective-permute-done((bf16[2,128,896]{2,1,0:T(8,128)(2,1)}, bf16[2,128,896]{2,1,0:T(8,128)(2,1)S(1)}, u32[]{:S(2)}, u32[]{:S(2)}) %collective-permute-start.6) | collective-permute-done | bytes 458784 | tf_op jit(solution)/shard_map/ppermute | solution.py:547
  62.1 6.4 %collective-permute-done.15.from_y = bf16[128,1792]{1,0:T(8,128)(2,1)S(1)} collective-permute-done((bf16[128,1792]{1,0:T(8,128)(2,1)}, bf16[128,1792]{1,0:T(8,128)(2,1)S(1)}, u32[]{:S(2)}, u32[]{:S(2)}) %collective-permute-start.15) | collective-permute-done | bytes 458784 | tf_op jit(solution)/shard_map/ppermute | solution.py:547
  70.8 7.4 %collective-permute-done.34.rest_6_ = bf16[112,896]{1,0:T(8,128)(2,1)S(1)} collective-permute-done((bf16[112,896]{1,0:T(8,128)(2,1)S(1)}, bf16[112,896]{1,0:T(8,128)(2,1)S(1)}, u32[]{:S(2)}, u32[]{:S(2)}) %collective-permute-start.34) | collective-permute-done | bytes 200736 | tf_op jit(solution)/shard_map/ppermute | solution.py:588
  78.7 6.5 %collective-permute-done.17.last_x = bf16[64,1792]{1,0:T(8,128)(2,1)S(1)} collective-permute-done((bf16[64,1792]{1,0:T(8,128)(2,1)S(1)}, bf16[64,1792]{1,0:T(8,128)(2,1)S(1)}, u32[]{:S(2)}, u32[]{:S(2)}) %collective-permute-start.17) | collective-permute-done | bytes 229408 | tf_op jit(solution)/shard_map/ppermute | solution.py:547
  85.2 5.0 %collective-permute-done.10.rest_4_ = bf16[112,2688]{1,0:T(8,128)(2,1)S(1)} collective-permute-done((bf16[112,2688]{1,0:T(8,128)(2,1)S(1)}, bf16[112,2688]{1,0:T(8,128)(2,1)S(1)}, u32[]{:S(2)}, u32[]{:S(2)}) %collective-permute-start.10) | collective-permute-done | bytes 602144 | tf_op jit(solution)/shard_map/ppermute | solution.py:588
  90.2 6.0 %collective-permute-done.24.rest_8_ = bf16[112,896]{1,0:T(8,128)(2,1)S(1)} collective-permute-done((bf16[112,896]{1,0:T(8,128)(2,1)S(1)}, bf16[112,896]{1,0:T(8,128)(2,1)S(1)}, u32[]{:S(2)}, u32[]{:S(2)}) %collective-permute-start.24) | collective-permute-done | bytes 200736 | tf_op jit(solution)/shard_map/ppermute | solution.py:547
  96.2 14.7 %collective-permute-done.26.rest_10_ = bf16[112,896]{1,0:T(8,128)(2,1)S(1)} collective-permute-done((bf16[112,896]{1,0:T(8,128)(2,1)S(1)}, bf16[112,896]{1,0:T(8,128)(2,1)S(1)}, u32[]{:S(2)}, u32[]{:S(2)}) %collective-permute-start.26) | collective-permute-done | bytes 200736 | tf_op jit(solution)/shard_map/ppermute | solution.py:588
  111.6 9.0 %collective-permute-done.28.rest_12_ = bf16[112,896]{1,0:T(8,128)(2,1)S(1)} collective-permute-done((bf16[112,896]{1,0:T(8,128)(2,1)S(1)}, bf16[112,896]{1,0:T(8,128)(2,1)S(1)}, u32[]{:S(2)}, u32[]{:S(2)}) %collective-permute-start.28) | collective-permute-done | bytes 200736 | tf_op jit(solution)/shard_map/ppermute | solution.py:588
  123.2 7.7 %shard_map.103 = (bf16[512,896]{1,0:T(8,128)(2,1)S(1)}, bf16[512,896]{1,0:T(8,128)(2,1)S(1)}) custom-call(s32[8]{0:T(128)S(1)} %copy-done.2, s32[2,8]{1,0:T(2,128)S(1)} %bitcast.12, s32[2,8]{1,0:T(2,128)S(1)} %bitcast.18, bf16[8,128,896]{2,1,0:T(8,128)(2,1)S(1)} %bitcast.16, bf16[2,128,896]{2,1,0:T(8,128)(2,1)S(1)} %collective-permute-done.4.r1, ...), custom_call_target="tpu_custom_call" | custom-call | flops 4932501504 | bytes 9232464 | tf_op jit(solution)/shard_map/pallas_call | solution.py:119
  131.6 3.9 %shard_map.105 = (bf16[512,896]{1,0:T(8,128)(2,1)S(1)}, bf16[512,896]{1,0:T(8,128)(2,1)S(1)}) custom-call(bf16[512,896]{1,0:T(8,128)(2,1)S(1)} %get-tuple-element.34.source, bf16[512,896]{1,0:T(8,128)(2,1)S(1)} %get-tuple-element.35.within, bf16[128,1792]{1,0:T(8,128)(2,1)S(1)} %copy-done.14, bf16[128,1792]{1,0:T(8,128)(2,1)S(1)} %collective-permute-done.14.from_x, ...), custom_call_target="tpu_custom_call" | custom-call | flops 3288334336 | bytes 8486912 | tf_op jit(solution)/shard_map/pallas_call | solution.py:119
  135.6 2.7 %shard_map.106 = (bf16[256,896]{1,0:T(8,128)(2,1)S(1)}, bf16[256,896]{1,0:T(8,128)(2,1)S(1)}) custom-call(bf16[512,896]{1,0:T(8,128)(2,1)S(1)} %get-tuple-element.42.middle, bf16[512,896]{1,0:T(8,128)(2,1)S(1)} %get-tuple-element.43.across, bf16[112,5376]{1,0:T(8,128)(2,1)S(1)} %copy-done.8, bf16[112,5376]{1,0:T(8,128)(2,1)S(1)} %collective-permute-done.7.rest_1_, ...), custom_call_target="tpu_custom_call" | custom-call | flops 1644167168 | bytes 5447680 | tf_op jit(solution)/shard_map/pallas_call | solution.py:119
  141.8 5.5 %shard_map.100.queries = bf16[512,1024]{1,0:T(8,128)(2,1)S(1)} custom-call(bf16[512,1024]{1,0:T(8,128)(2,1)S(1)} %copy-done, bf16[512,1024]{1,0:T(8,128)(2,1)S(1)} %collective-permute-done.from_x, bf16[512,1024]{1,0:T(8,128)(2,1)S(1)} %collective-permute-done.1.from_y, bf16[256,1024]{1,0:T(8,128)(2,1)S(1)} %collective-permute-done.2.d0, ...), custom_call_target="tpu_custom_call" | custom-call | flops 4294967296 | bytes 12582912 | tf_op jit(solution)/shard_map/pallas_call | solution.py:119
  149.4 2.4 %collective-permute-done.36.rest_1_ = bf16[256,896]{1,0:T(8,128)(2,1)S(1)} collective-permute-done((bf16[256,896]{1,0:T(8,128)(2,1)S(1)}, bf16[256,896]{1,0:T(8,128)(2,1)S(1)}, u32[]{:S(2)}, u32[]{:S(2)}) %collective-permute-start.36) | collective-permute-done | bytes 458784 | tf_op jit(solution)/shard_map/ppermute | solution.py:547
  153.8 9.6 %shard_map.107 = (bf16[128,2048]{1,0:T(8,128)(2,1)S(1)}, bf16[128,2048]{1,0:T(8,128)(2,1)S(1)}, bf16[128,2048]{1,0:T(8,128)(2,1)S(1)}, bf16[128,2048]{1,0:T(8,128)(2,1)S(1)}) custom-call(s32[8]{0:T(128)S(1)} %copy-done.2, bf16[512,1024]{1,0:T(8,128)(2,1)S(1)} %shard_map.100.queries, bf16[256,896]{1,0:T(8,128)(2,1)S(1)} %get-tuple-element.45.rest_0_, ...), custom_call_target="tpu_custom_call" | custom-call | flops 7516192768 | bytes 14942224 | tf_op jit(solution)/shard_map/pallas_call | solution.py:119
  164.0 1.5 collective-permute-start.39
  165.5 4.1 %shard_map.108.rest_2_ = bf16[128,1024]{1,0:T(8,128)(2,1)S(1)} custom-call(s32[8]{0:T(128)S(1)} %copy-done.2, bf16[512,1024]{1,0:T(8,128)(2,1)S(1)} %shard_map.100.queries, bf16[256,896]{1,0:T(8,128)(2,1)S(1)} %collective-permute-done.44.rest_0_, bf16[256,896]{1,0:T(8,128)(2,1)S(1)} %collective-permute-done.45.rest_1_, bf16[896,2048]{1,0:T(8,128)(2,1)S(1)} %bitcast.6), custom_call_target="tpu_custom_call" | custom-call | flops 3758096384 | bytes 5636112 | tf_op jit(solution)/shard_map/pallas_call | solution.py:119
  169.7 2.3 %collective-permute-done.42.rest_0_ = bf16[256,896]{1,0:T(8,128)(2,1)S(1)} collective-permute-done((bf16[256,896]{1,0:T(8,128)(2,1)S(1)}, bf16[256,896]{1,0:T(8,128)(2,1)S(1)}, u32[]{:S(2)}, u32[]{:S(2)}) %collective-permute-start.42) | collective-permute-done | bytes 458784 | tf_op jit(solution)/shard_map/ppermute | solution.py:547
  172.0 6.6 %shard_map.109 = (bf16[128,2048]{1,0:T(8,128)(2,1)S(1)}, bf16[128,2048]{1,0:T(8,128)(2,1)S(1)}, bf16[128,2048]{1,0:T(8,128)(2,1)S(1)}, bf16[128,2048]{1,0:T(8,128)(2,1)S(1)}) custom-call(s32[8]{0:T(128)S(1)} %copy-done.2, bf16[512,1024]{1,0:T(8,128)(2,1)S(1)} %shard_map.100.queries, bf16[256,896]{1,0:T(8,128)(2,1)S(1)} %collective-permute-done.42.rest_0_, ...), custom_call_target="tpu_custom_call" | custom-call | flops 3758096384 | bytes 14286864 | tf_op jit(solution)/shard_map/pallas_call | solution.py:119
  178.6 1.5 collective-permute-start.46
  180.3 2.4 %collective-permute-done.38.rest_2_ = bf16[128,2048]{1,0:T(8,128)(2,1)S(1)} collective-permute-done((bf16[128,2048]{1,0:T(8,128)(2,1)S(1)}, bf16[128,2048]{1,0:T(8,128)(2,1)S(1)}, u32[]{:S(2)}, u32[]{:S(2)}) %collective-permute-start.38) | collective-permute-done | bytes 524320 | tf_op jit(solution)/shard_map/ppermute | solution.py:547
  185.0 8.9 %collective-permute-done.46.rest_8_ = bf16[128,2048]{1,0:T(8,128)(2,1)S(1)} collective-permute-done((bf16[128,2048]{1,0:T(8,128)(2,1)S(1)}, bf16[128,2048]{1,0:T(8,128)(2,1)S(1)}, u32[]{:S(2)}, u32[]{:S(2)}) %collective-permute-start.46) | collective-permute-done | bytes 524320 | tf_op jit(solution)/shard_map/ppermute | solution.py:547
  196.2 4.3 %collective-permute-done.40.rest_4_ = bf16[128,1024]{1,0:T(8,128)(2,1)S(1)} collective-permute-done((bf16[128,1024]{1,0:T(8,128)(2,1)S(1)}, bf16[128,1024]{1,0:T(8,128)(2,1)S(1)}, u32[]{:S(2)}, u32[]{:S(2)}) %collective-permute-start.40) | collective-permute-done | bytes 262176 | tf_op jit(solution)/shard_map/ppermute | solution.py:547
  200.5 4.3 %collective-permute-done.48.rest_10_ = bf16[128,1024]{1,0:T(8,128)(2,1)S(1)} collective-permute-done((bf16[128,1024]{1,0:T(8,128)(2,1)S(1)}, bf16[128,1024]{1,0:T(8,128)(2,1)S(1)}, u32[]{:S(2)}, u32[]{:S(2)}) %collective-permute-start.48) | collective-permute-done | bytes 262176 | tf_op jit(solution)/shard_map/ppermute | solution.py:547
  204.8 2.0 shard_map.110
  (132 shorter events, 35.7 us)
Async XLA Ops:
  2.4 16.1 %collective-permute-start.18 = (bf16[112,896]{1,0:T(8,128)(2,1)S(1)}, bf16[112,896]{1,0:T(8,128)(2,1)S(1)}, u32[]{:S(2)}, u32[]{:S(2)}) collective-permute-start(bf16[112,896]{1,0:T(8,128)(2,1)S(1)} %get-tuple-element.41), channel_id=1, source_target_pairs={{0,8},{8,16},{16,24},{24,0},{1,9},{9,17},{17,25},{25,1},{2,10},{10... | collective-permute-start | bytes 602120 | tf_op jit(solution)/shard_map/ppermute | solution.py:588
  15.4 33.6 %collective-permute-start.14 = (bf16[128,1792]{1,0:T(8,128)(2,1)}, bf16[128,1792]{1,0:T(8,128)(2,1)S(1)}, u32[]{:S(2)}, u32[]{:S(2)}) collective-permute-start(bf16[128,1792]{1,0:T(8,128)(2,1)} %get-tuple-element.37), channel_id=1, source_target_pairs={{0,2},{2,0},{4,6},{6,4},{1,3},{3,1},{5,7},{7,5},{8,10},{10,8},{12,... | collective-permute-start | bytes 1376264 | tf_op jit(solution)/shard_map/ppermute | solution.py:547
  16.9 12.0 %collective-permute-start.30 = (bf16[112,896]{1,0:T(8,128)(2,1)}, bf16[112,896]{1,0:T(8,128)(2,1)}, u32[]{:S(2)}, u32[]{:S(2)}) collective-permute-start(bf16[112,896]{1,0:T(8,128)(2,1)} %get-tuple-element.44), channel_id=1, source_target_pairs={{0,8},{8,16},{16,24},{24,0},{1,9},{9,17},{17,25},{25,1},{2,10},{10... | collective-permute-start | bytes 602120 | tf_op jit(solution)/shard_map/ppermute | solution.py:588
  26.8 23.8 %collective-permute-start.4 = (bf16[2,128,896]{2,1,0:T(8,128)(2,1)}, bf16[2,128,896]{2,1,0:T(8,128)(2,1)S(1)}, u32[]{:S(2)}, u32[]{:S(2)}) collective-permute-start(bf16[2,128,896]{2,1,0:T(8,128)(2,1)} %get-tuple-element.30), channel_id=1, source_target_pairs={{0,2},{2,0},{4,6},{6,4},{1,3},{3,1},{5,7},{7,5},{8,10},{10,8},{12,... | collective-permute-start | bytes 1376264 | tf_op jit(solution)/shard_map/ppermute | solution.py:547
  27.3 41.2 %collective-permute-start.8 = (bf16[112,2688]{1,0:T(8,128)(2,1)}, bf16[112,2688]{1,0:T(8,128)(2,1)S(1)}, u32[]{:S(2)}, u32[]{:S(2)}) collective-permute-start(bf16[112,2688]{1,0:T(8,128)(2,1)} %get-tuple-element.33), channel_id=1, source_target_pairs={{0,8},{8,16},{16,24},{24,0},{1,9},{9,17},{17,25},{25,1},{2,10},{10... | collective-permute-start | bytes 1806344 | tf_op jit(solution)/shard_map/ppermute | solution.py:588
  29.0 18.6 %collective-permute-start.32 = (bf16[112,896]{1,0:T(8,128)(2,1)}, bf16[112,896]{1,0:T(8,128)(2,1)S(1)}, u32[]{:S(2)}, u32[]{:S(2)}) collective-permute-start(bf16[112,896]{1,0:T(8,128)(2,1)} %collective-permute-done.30.rest_2_), channel_id=1, source_target_pairs={{0,8},{8,16},{16,24},{24,0},{1,9},{9,17},{17,25},{25,1},{2,10},{10... | collective-permute-start | bytes 602120 | tf_op jit(solution)/shard_map/ppermute | solution.py:588
  30.4 20.8 %collective-permute-start.5 = (bf16[2,128,896]{2,1,0:T(8,128)(2,1)}, bf16[2,128,896]{2,1,0:T(8,128)(2,1)S(1)}, u32[]{:S(2)}, u32[]{:S(2)}) collective-permute-start(bf16[2,128,896]{2,1,0:T(8,128)(2,1)} %copy-done.11), channel_id=1, source_target_pairs={{0,4},{2,6},{4,0},{6,2},{1,5},{3,7},{5,1},{7,3},{8,12},{10,14},{12... | collective-permute-start | bytes 1376264 | tf_op jit(solution)/shard_map/ppermute | solution.py:547
  47.6 14.5 %collective-permute-start.6 = (bf16[2,128,896]{2,1,0:T(8,128)(2,1)}, bf16[2,128,896]{2,1,0:T(8,128)(2,1)S(1)}, u32[]{:S(2)}, u32[]{:S(2)}) collective-permute-start(bf16[2,128,896]{2,1,0:T(8,128)(2,1)} %copy-done.10), channel_id=1, source_target_pairs={{0,6},{2,4},{4,2},{6,0},{1,7},{3,5},{5,3},{7,1},{8,14},{10,12},{12... | collective-permute-start | bytes 1376264 | tf_op jit(solution)/shard_map/ppermute | solution.py:547
  49.0 19.5 %collective-permute-start.15 = (bf16[128,1792]{1,0:T(8,128)(2,1)}, bf16[128,1792]{1,0:T(8,128)(2,1)S(1)}, u32[]{:S(2)}, u32[]{:S(2)}) collective-permute-start(bf16[128,1792]{1,0:T(8,128)(2,1)} %copy-done.9), channel_id=1, source_target_pairs={{0,4},{2,6},{4,0},{6,2},{1,5},{3,7},{5,1},{7,3},{8,12},{10,14},{12... | collective-permute-start | bytes 1376264 | tf_op jit(solution)/shard_map/ppermute | solution.py:547
  50.6 60.3 %collective-permute-start = (bf16[512,1024]{1,0:T(8,128)(2,1)S(1)}, bf16[512,1024]{1,0:T(8,128)(2,1)S(1)}, u32[]{:S(2)}, u32[]{:S(2)}) collective-permute-start(bf16[512,1024]{1,0:T(8,128)(2,1)S(1)} %copy-done), channel_id=1, source_target_pairs={{0,2},{2,0},{4,6},{6,4},{1,3},{3,1},{5,7},{7,5},{8,10},{10,8},{12,... | collective-permute-start | bytes 3145736 | tf_op jit(solution)/shard_map/ppermute | solution.py:547
  51.2 18.3 %collective-permute-start.22 = (bf16[112,896]{1,0:T(8,128)(2,1)S(1)}, bf16[112,896]{1,0:T(8,128)(2,1)S(1)}, u32[]{:S(2)}, u32[]{:S(2)}) collective-permute-start(bf16[112,896]{1,0:T(8,128)(2,1)S(1)} %broadcast_select_fusion), channel_id=1, source_target_pairs={{0,8},{8,16},{16,24},{24,0},{1,9},{9,17},{17,25},{25,1},{2,10},{10... | collective-permute-start | bytes 602120 | tf_op jit(solution)/shard_map/ppermute | solution.py:588
  68.5 21.6 %collective-permute-start.10 = (bf16[112,2688]{1,0:T(8,128)(2,1)S(1)}, bf16[112,2688]{1,0:T(8,128)(2,1)S(1)}, u32[]{:S(2)}, u32[]{:S(2)}) collective-permute-start(bf16[112,2688]{1,0:T(8,128)(2,1)S(1)} %collective-permute-done.8.rest_2_), channel_id=1, source_target_pairs={{0,8},{8,16},{16,24},{24,0},{1,9},{9,17},{17,25},{25,1},{2,10},{10... | collective-permute-start | bytes 1806344 | tf_op jit(solution)/shard_map/ppermute | solution.py:588
  69.5 15.6 %collective-permute-start.17 = (bf16[64,1792]{1,0:T(8,128)(2,1)S(1)}, bf16[64,1792]{1,0:T(8,128)(2,1)S(1)}, u32[]{:S(2)}, u32[]{:S(2)}) collective-permute-start(bf16[64,1792]{1,0:T(8,128)(2,1)S(1)} %add_convert_fusion.4), channel_id=1, source_target_pairs={{0,2},{2,0},{4,6},{6,4},{1,3},{3,1},{5,7},{7,5},{8,10},{10,8},{12,... | collective-permute-start | bytes 688136 | tf_op jit(solution)/shard_map/ppermute | solution.py:547
  78.2 33.3 %collective-permute-start.1 = (bf16[512,1024]{1,0:T(8,128)(2,1)S(1)}, bf16[512,1024]{1,0:T(8,128)(2,1)S(1)}, u32[]{:S(2)}, u32[]{:S(2)}) collective-permute-start(bf16[512,1024]{1,0:T(8,128)(2,1)S(1)} %copy-done), channel_id=1, source_target_pairs={{0,4},{2,6},{4,0},{6,2},{1,5},{3,7},{5,1},{7,3},{8,12},{10,14},{12... | collective-permute-start | bytes 3145736 | tf_op jit(solution)/shard_map/ppermute | solution.py:547
  78.7 11.4 %collective-permute-start.23 = (bf16[112,896]{1,0:T(8,128)(2,1)S(1)}, bf16[112,896]{1,0:T(8,128)(2,1)S(1)}, u32[]{:S(2)}, u32[]{:S(2)}) collective-permute-start(bf16[112,896]{1,0:T(8,128)(2,1)S(1)} %collective-permute-done.22.rest_6_), channel_id=1, source_target_pairs={{0,1},{1,0},{2,3},{3,2},{4,5},{5,4},{6,7},{7,6},{8,9},{9,8},{10,11... | collective-permute-start | bytes 602120 | tf_op jit(solution)/shard_map/ppermute | solution.py:591
  85.2 35.5 %collective-permute-start.7 = (bf16[112,5376]{1,0:T(8,128)(2,1)}, bf16[112,5376]{1,0:T(8,128)(2,1)S(1)}, u32[]{:S(2)}, u32[]{:S(2)}) collective-permute-start(bf16[112,5376]{1,0:T(8,128)(2,1)} %rest_0_.5), channel_id=1, source_target_pairs={{0,1},{1,0},{2,3},{3,2},{4,5},{5,4},{6,7},{7,6},{8,9},{9,8},{10,11... | collective-permute-start | bytes 3612680 | tf_op jit(solution)/shard_map/ppermute | solution.py:591
  90.1 21.3 %collective-permute-start.12 = (bf16[112,2688]{1,0:T(8,128)(2,1)S(1)}, bf16[112,2688]{1,0:T(8,128)(2,1)S(1)}, u32[]{:S(2)}, u32[]{:S(2)}) collective-permute-start(bf16[112,2688]{1,0:T(8,128)(2,1)S(1)} %collective-permute-done.10.rest_4_), channel_id=1, source_target_pairs={{0,8},{8,16},{16,24},{24,0},{1,9},{9,17},{17,25},{25,1},{2,10},{10... | collective-permute-start | bytes 1806344 | tf_op jit(solution)/shard_map/ppermute | solution.py:588
  96.2 14.7 %collective-permute-start.26 = (bf16[112,896]{1,0:T(8,128)(2,1)S(1)}, bf16[112,896]{1,0:T(8,128)(2,1)S(1)}, u32[]{:S(2)}, u32[]{:S(2)}) collective-permute-start(bf16[112,896]{1,0:T(8,128)(2,1)S(1)} %collective-permute-done.22.rest_6_), channel_id=1, source_target_pairs={{0,8},{8,16},{16,24},{24,0},{1,9},{9,17},{17,25},{25,1},{2,10},{10... | collective-permute-start | bytes 602120 | tf_op jit(solution)/shard_map/ppermute | solution.py:588
  121.2 20.5 %collective-permute-start.2 = (bf16[256,1024]{1,0:T(8,128)(2,1)S(1)}, bf16[256,1024]{1,0:T(8,128)(2,1)S(1)}, u32[]{:S(2)}, u32[]{:S(2)}) collective-permute-start(bf16[256,1024]{1,0:T(8,128)(2,1)S(1)} %slice.48), channel_id=1, source_target_pairs={{0,4},{2,6},{4,0},{6,2},{1,5},{3,7},{5,1},{7,3},{8,12},{10,14},{12... | collective-permute-start | bytes 1572872 | tf_op jit(solution)/shard_map/ppermute | solution.py:547
  121.7 20.0 %collective-permute-start.3 = (bf16[256,1024]{1,0:T(8,128)(2,1)S(1)}, bf16[256,1024]{1,0:T(8,128)(2,1)S(1)}, u32[]{:S(2)}, u32[]{:S(2)}) collective-permute-start(bf16[256,1024]{1,0:T(8,128)(2,1)S(1)} %slice.49), channel_id=1, source_target_pairs={{0,2},{2,0},{4,6},{6,4},{1,3},{3,1},{5,7},{7,5},{8,10},{10,8},{12,... | collective-permute-start | bytes 1572872 | tf_op jit(solution)/shard_map/ppermute | solution.py:547
  138.3 13.5 %collective-permute-start.36 = (bf16[256,896]{1,0:T(8,128)(2,1)S(1)}, bf16[256,896]{1,0:T(8,128)(2,1)S(1)}, u32[]{:S(2)}, u32[]{:S(2)}) collective-permute-start(bf16[256,896]{1,0:T(8,128)(2,1)S(1)} %get-tuple-element.45.rest_0_), channel_id=1, source_target_pairs={{0,2},{2,0},{4,6},{6,4},{1,3},{3,1},{5,7},{7,5},{8,10},{10,8},{12,... | collective-permute-start | bytes 1376264 | tf_op jit(solution)/shard_map/ppermute | solution.py:547
  138.9 13.4 %collective-permute-start.37 = (bf16[256,896]{1,0:T(8,128)(2,1)S(1)}, bf16[256,896]{1,0:T(8,128)(2,1)S(1)}, u32[]{:S(2)}, u32[]{:S(2)}) collective-permute-start(bf16[256,896]{1,0:T(8,128)(2,1)S(1)} %get-tuple-element.46.rest_2_), channel_id=1, source_target_pairs={{0,4},{2,6},{4,0},{6,2},{1,5},{3,7},{5,1},{7,3},{8,12},{10,14},{12... | collective-permute-start | bytes 1376264 | tf_op jit(solution)/shard_map/ppermute | solution.py:547
  147.3 16.7 %collective-permute-start.44 = (bf16[256,896]{1,0:T(8,128)(2,1)S(1)}, bf16[256,896]{1,0:T(8,128)(2,1)S(1)}, u32[]{:S(2)}, u32[]{:S(2)}) collective-permute-start(bf16[256,896]{1,0:T(8,128)(2,1)S(1)} %get-tuple-element.45.rest_0_), channel_id=1, source_target_pairs={{0,4},{2,6},{4,0},{6,2},{1,5},{3,7},{5,1},{7,3},{8,12},{10,14},{12... | collective-permute-start | bytes 1376264 | tf_op jit(solution)/shard_map/ppermute | solution.py:547
  147.9 17.6 %collective-permute-start.45 = (bf16[256,896]{1,0:T(8,128)(2,1)S(1)}, bf16[256,896]{1,0:T(8,128)(2,1)S(1)}, u32[]{:S(2)}, u32[]{:S(2)}) collective-permute-start(bf16[256,896]{1,0:T(8,128)(2,1)S(1)} %get-tuple-element.46.rest_2_), channel_id=1, source_target_pairs={{0,2},{2,0},{4,6},{6,4},{1,3},{3,1},{5,7},{7,5},{8,10},{10,8},{12,... | collective-permute-start | bytes 1376264 | tf_op jit(solution)/shard_map/ppermute | solution.py:547
  151.8 20.2 %collective-permute-start.42 = (bf16[256,896]{1,0:T(8,128)(2,1)S(1)}, bf16[256,896]{1,0:T(8,128)(2,1)S(1)}, u32[]{:S(2)}, u32[]{:S(2)}) collective-permute-start(bf16[256,896]{1,0:T(8,128)(2,1)S(1)} %collective-permute-done.36.rest_1_), channel_id=1, source_target_pairs={{0,4},{2,6},{4,0},{6,2},{1,5},{3,7},{5,1},{7,3},{8,12},{10,14},{12... | collective-permute-start | bytes 1376264 | tf_op jit(solution)/shard_map/ppermute | solution.py:547
  152.3 19.7 %collective-permute-start.43 = (bf16[256,896]{1,0:T(8,128)(2,1)S(1)}, bf16[256,896]{1,0:T(8,128)(2,1)S(1)}, u32[]{:S(2)}, u32[]{:S(2)}) collective-permute-start(bf16[256,896]{1,0:T(8,128)(2,1)S(1)} %collective-permute-done.37.rest_3_), channel_id=1, source_target_pairs={{0,2},{2,0},{4,6},{6,4},{1,3},{3,1},{5,7},{7,5},{8,10},{10,8},{12,... | collective-permute-start | bytes 1376264 | tf_op jit(solution)/shard_map/ppermute | solution.py:547
  163.4 19.2 %collective-permute-start.38 = (bf16[128,2048]{1,0:T(8,128)(2,1)S(1)}, bf16[128,2048]{1,0:T(8,128)(2,1)S(1)}, u32[]{:S(2)}, u32[]{:S(2)}) collective-permute-start(bf16[128,2048]{1,0:T(8,128)(2,1)S(1)} %get-tuple-element.49), channel_id=1, source_target_pairs={{0,2},{2,0},{4,6},{6,4},{1,3},{3,1},{5,7},{7,5},{8,10},{10,8},{12,... | collective-permute-start | bytes 1572872 | tf_op jit(solution)/shard_map/ppermute | solution.py:547
  164.0 19.9 %collective-permute-start.39 = (bf16[128,2048]{1,0:T(8,128)(2,1)S(1)}, bf16[128,2048]{1,0:T(8,128)(2,1)S(1)}, u32[]{:S(2)}, u32[]{:S(2)}) collective-permute-start(bf16[128,2048]{1,0:T(8,128)(2,1)S(1)} %get-tuple-element.50), channel_id=1, source_target_pairs={{0,4},{2,6},{4,0},{6,2},{1,5},{3,7},{5,1},{7,3},{8,12},{10,14},{12... | collective-permute-start | bytes 1572872 | tf_op jit(solution)/shard_map/ppermute | solution.py:547
  178.6 15.3 %collective-permute-start.46 = (bf16[128,2048]{1,0:T(8,128)(2,1)S(1)}, bf16[128,2048]{1,0:T(8,128)(2,1)S(1)}, u32[]{:S(2)}, u32[]{:S(2)}) collective-permute-start(bf16[128,2048]{1,0:T(8,128)(2,1)S(1)} %get-tuple-element.53), channel_id=1, source_target_pairs={{0,2},{2,0},{4,6},{6,4},{1,3},{3,1},{5,7},{7,5},{8,10},{10,8},{12,... | collective-permute-start | bytes 1572872 | tf_op jit(solution)/shard_map/ppermute | solution.py:547
  180.1 15.1 %collective-permute-start.47 = (bf16[128,2048]{1,0:T(8,128)(2,1)S(1)}, bf16[128,2048]{1,0:T(8,128)(2,1)S(1)}, u32[]{:S(2)}, u32[]{:S(2)}) collective-permute-start(bf16[128,2048]{1,0:T(8,128)(2,1)S(1)} %get-tuple-element.54), channel_id=1, source_target_pairs={{0,4},{2,6},{4,0},{6,2},{1,5},{3,7},{5,1},{7,3},{8,12},{10,14},{12... | collective-permute-start | bytes 1572872 | tf_op jit(solution)/shard_map/ppermute | solution.py:547
  182.7 17.8 %collective-permute-start.40 = (bf16[128,1024]{1,0:T(8,128)(2,1)S(1)}, bf16[128,1024]{1,0:T(8,128)(2,1)S(1)}, u32[]{:S(2)}, u32[]{:S(2)}) collective-permute-start(bf16[128,1024]{1,0:T(8,128)(2,1)S(1)} %add_convert_fusion.3), channel_id=1, source_target_pairs={{0,4},{2,6},{4,0},{6,2},{1,5},{3,7},{5,1},{7,3},{8,12},{10,14},{12... | collective-permute-start | bytes 786440 | tf_op jit(solution)/shard_map/ppermute | solution.py:547
  184.0 16.5 %collective-permute-start.41 = (bf16[128,1024]{1,0:T(8,128)(2,1)S(1)}, bf16[128,1024]{1,0:T(8,128)(2,1)S(1)}, u32[]{:S(2)}, u32[]{:S(2)}) collective-permute-start(bf16[128,1024]{1,0:T(8,128)(2,1)S(1)} %add_convert_fusion.2), channel_id=1, source_target_pairs={{0,2},{2,0},{4,6},{6,4},{1,3},{3,1},{5,7},{7,5},{8,10},{10,8},{12,... | collective-permute-start | bytes 786440 | tf_op jit(solution)/shard_map/ppermute | solution.py:547
  (38 other events, 560.9 us)

commit v2 on v1

--- a/solution.py
+++ b/solution.py
@@ -115,13 +115,14 @@
     return (states.astype(jnp.float32) + summed).astype(jnp.bfloat16)
 
 
-def call(kernel, out_shape, in_specs, out_specs, scratch, mib, flops, *args):
+def call(kernel, out_shape, in_specs, out_specs, scratch, mib, flops, *args, aliases=()):
     return pl.pallas_call(
         kernel,
         out_shape=out_shape,
         in_specs=in_specs,
         out_specs=out_specs,
         scratch_shapes=scratch,
+        input_output_aliases=dict(aliases),
         compiler_params=pltpu.CompilerParams(vmem_limit_bytes=mib * 1024 * 1024),
         cost_estimate=pl.CostEstimate(
             flops=flops,
@@ -186,6 +187,18 @@
         copies.append(pltpu.make_async_copy(weights.at[:, cols], part, sems.at[i]))
     for c in copies:
         c.start()
+    for c in copies:
+        c.wait()
+
+
+def halves_kernel(states, *rest):
+    outs, sems = rest[:-1], rest[-1]
+    rows = outs[0].shape[0]
+    copies = []
+    for i, out in enumerate(outs):
+        part = states.at[pl.ds(i * rows, rows), :]
+        copies.append(pltpu.make_async_copy(part, out, sems.at[i]))
+        copies[-1].start()
     for c in copies:
         c.wait()
 
@@ -317,14 +330,15 @@
         c.wait()
 
 
-def load_pieces(n_span, first, pieces, held, sems):
+def load_pieces(n_span, first, pieces, held, sems, begin=0, total=None):
     z = lax.axis_index("span").astype(jnp.int32)
     g = lax.axis_index("group").astype(jnp.int32)
     x, y = square_place()
     rows = pieces[0].shape[0]
     copies = []
-    split = (len(pieces) - 2) // (2 * (n_span - 1))
-    for i, piece in enumerate(pieces):
+    total = total or len(pieces)
+    split = (total - 2) // (2 * (n_span - 1))
+    for i, piece in enumerate(pieces, begin):
         if i < 2:
             r, other, cols = 0, i, slice(None)
             piece = piece.at[:, pl.ds(first, held.shape[1])]
@@ -340,7 +354,7 @@
         spot = lax.rem(z + (n_span - r), n_span) * 2 + (g ^ other)
         start = pl.multiple_of(spot * rows, rows)
         copies.append(
-            pltpu.make_async_copy(piece, held.at[pl.ds(start, rows), cols], sems.at[i])
+            pltpu.make_async_copy(piece, held.at[pl.ds(start, rows), cols], sems.at[i - begin])
         )
     return copies
 
@@ -349,12 +363,17 @@
     return min(r, n_span - 2) % 2
 
 
-def self_kernel(n_span, assign, owners, places, store, r1, r2, r3, *rest):
-    pieces = rest[: 2 * n_span]
-    source, within, held, triple, scores, weights, sem_s, sem_w = rest[2 * n_span :]
+def early_weights_kernel(n_span, first, total, *rest):
+    pieces, (held, sem_w) = rest[:-2], rest[-2:]
+    copies = load_pieces(n_span, first, pieces, held, sem_w, total=total)
+    for c in copies:
+        c.start()
+    for c in copies:
+        c.wait()
+
+
+def source_kernel(assign, owners, places, store, r1, r2, r3, source, sem_s):
     me = head_index()
-    per = 2 * NEIGHBOURS
-    copies = load_pieces(n_span, 0, pieces, held, sem_w)
     mine = neighbours_of(assign, owners, places, me)
     for j, (owner, place) in enumerate(mine):
         at = source.at[pl.ds(j * RETRIEVED, RETRIEVED), :]
@@ -367,11 +386,16 @@
             def _():
                 pltpu.make_async_copy(ref.at[place if k == 0 else nth], at, sem_s.at[j]).start()
 
-    for c in copies:
-        c.start()
-    for j in range(per):
+    for j in range(len(mine)):
         at = source.at[pl.ds(j * RETRIEVED, RETRIEVED), :]
         pltpu.make_async_copy(r1.at[0], at, sem_s.at[j]).wait()
+
+
+def self_kernel(n_span, source, early, own, other, within, held, triple, scores, weights, sem_w):
+    total = 2 * n_span
+    copies = load_pieces(n_span, 0, (own, other), held, sem_w, begin=total - 2, total=total)
+    for c in copies:
+        c.start()
     for c in copies:
         c.wait()
     breadth = source.shape[1]
@@ -379,24 +403,24 @@
         cols = slice(c * breadth, (c + 1) * breadth)
         triple[:, cols] = dot(source[...], held[:, cols]).astype(jnp.bfloat16)
     units = []
-    for j in range(per):
+    for j in range(source.shape[0] // RETRIEVED):
         rows = slice(j * RETRIEVED, (j + 1) * RETRIEVED)
         for c in range(0, breadth, HEAD_DIM):
             units.append(unit(triple, rows, c, triple, rows, breadth + c, 2 * breadth + c, within))
     attend_many(units, scores, weights)
 
 
-def cross_kernel(n_span, first, source, within, own, from_x, from_y, last_y, last_x, *rest):
-    pieces = rest[: 4 * n_span - 2]
-    middle, across, held, context, asking, scores, weights, sem_w = rest[4 * n_span - 2 :]
-    copies = load_pieces(n_span, first, pieces, held, sem_w)
+def cross_kernel(n_span, total, source, within, own, from_x, from_y, last_y, last_x, *rest):
+    pieces = rest[1:5]
+    middle, across, held, context, asking, scores, weights, sem_w = rest[5:]
+    copies = load_pieces(n_span, 0, pieces, held, sem_w, begin=total - 4, total=total)
     for c in copies:
         c.start()
     breadth = source.shape[1]
     for i, (near, far) in enumerate(((from_x, last_y), (from_y, last_x))):
         at = slice(i * SPAN_LEN, (i + 1) * SPAN_LEN)
-        total = own[at, :].astype(jnp.float32) + near[:SPAN_LEN, :].astype(jnp.float32)
-        context[at, :] = (total + far[...].astype(jnp.float32)).astype(jnp.bfloat16)
+        sums = own[at, :].astype(jnp.float32) + near[:SPAN_LEN, :].astype(jnp.float32)
+        context[at, :] = (sums + far[...].astype(jnp.float32)).astype(jnp.bfloat16)
     for c in copies:
         c.wait()
     middle[...] = (
@@ -413,21 +437,22 @@
     attend_many(units, scores, weights)
 
 
-def encoded_kernel(n_span, first, middle, across, *rest):
-    pieces = rest[: 2 * n_span]
-    outs, held, sem_w = rest[2 * n_span : -2], rest[-2], rest[-1]
-    copies = load_pieces(n_span, first, pieces, held, sem_w)
+def encoded_kernel(n_span, middle, across, early, own, other, *rest):
+    outs, held, sem_w = rest[:-2], rest[-2], rest[-1]
+    total = 2 * n_span
+    copies = load_pieces(n_span, 0, (own, other), held, sem_w, begin=total - 2, total=total)
     for c in copies:
         c.start()
     for c in copies:
         c.wait()
     span_rows = NEIGHBOURS * RETRIEVED
-    total = middle[...].astype(jnp.float32) + dot(across[...], held[...])
     for s, out in enumerate(outs):
-        out[...] = total[s * span_rows : (s + 1) * span_rows, :].astype(jnp.bfloat16)
-
-
-def query_kernel(own, from_x, from_y, d0, d1, w, out, held, total, sems):
+        rows = slice(s * span_rows, (s + 1) * span_rows)
+        result = middle[rows, :].astype(jnp.float32) + dot(across[rows, :], held[...])
+        out[...] = result.astype(jnp.bfloat16)
+
+
+def query_kernel(own, x0, x1, y0, y1, d0, d1, w, out, held, total, sems):
     me = head_index()
     width = own.shape[1]
     half = d0.shape[0]
@@ -441,12 +466,10 @@
         c.start()
     copies[0].wait()
     total[...] = dot(own[...], held[0])
-    for k, from_k in enumerate((from_x, from_y)):
+    for k, (first, second) in enumerate(((x0, x1), (y0, y1), (d0, d1))):
         copies[k + 1].wait()
-        total[...] += dot(from_k[...], held[k + 1])
-    copies[3].wait()
-    total[:half, :] += dot(d0[...], held[3])
-    total[half:, :] += dot(d1[...], held[3])
+        total[:half, :] += dot(first[...], held[k + 1])
+        total[half:, :] += dot(second[...], held[k + 1])
     out[...] = total[...].astype(jnp.bfloat16)
 
 
@@ -517,22 +540,49 @@
             out[one:, cols] = first if swapped else second
 
 
-def final_kernel(assign, states, *rest):
-    terms, out = rest[:-1], rest[-1]
+def put_rows(assign, chunk, block, out, sems):
+    me = head_index()
+    copies = []
+    for s, (relation, i) in enumerate(chunk):
+        start = pl.multiple_of(assign[(me ^ relation) * 2 + i] * SPAN_LEN, SPAN_LEN)
+        rows = block.at[pl.ds(s * SPAN_LEN, SPAN_LEN), :]
+        copies.append(pltpu.make_async_copy(rows, out.at[pl.ds(start, SPAN_LEN), :], sems.at[s]))
+        copies[-1].start()
+    return copies
+
+
+def almost_kernel(assign, states, *rest):
+    kept, near, last = rest[:4], rest[4:8], rest[8:10]
+    out, partial, block, sems = rest[10:]
     me = head_index()
     width = out.shape[1]
-    for c, chunk in enumerate(CHUNKS):
-        for s, (relation, i) in enumerate(chunk):
+    for c in (1, 0):
+        for s, (relation, i) in enumerate(CHUNKS[c]):
             side, row = s // 2, (s % 2) * SPAN_LEN
-            near = slice(row, row + SPAN_LEN)
-            span = assign[(me ^ relation) * 2 + i]
-            at = pl.ds(pl.multiple_of(span * SPAN_LEN, SPAN_LEN), SPAN_LEN)
-            kept, arrived = terms[6 * c + side], terms[6 * c + 2 + side]
-            last = terms[6 * (1 - c) + 4 + side]
-            total = kept[near, :width].astype(jnp.float32)
-            total = total + arrived[near, :width].astype(jnp.float32)
-            total = total + last[near, :].astype(jnp.float32)
-            out[at, :] = (states[at, :].astype(jnp.float32) + total).astype(jnp.bfloat16)
+            part = slice(row, row + SPAN_LEN)
+            start = pl.multiple_of(assign[(me ^ relation) * 2 + i] * SPAN_LEN, SPAN_LEN)
+            total = kept[2 * c + side][part, :width].astype(jnp.float32)
+            total = total + near[2 * c + side][part, :width].astype(jnp.float32)
+            total = total + states[pl.ds(start, SPAN_LEN), :].astype(jnp.float32)
+            rows = slice(s * SPAN_LEN, (s + 1) * SPAN_LEN)
+            if c == 0:
+                partial[rows, :] = total
+            else:
+                total = total + last[side][part, :].astype(jnp.float32)
+                block[rows, :] = total.astype(jnp.bfloat16)
+        if c == 1:
+            copies = put_rows(assign, CHUNKS[c], block, out, sems)
+    for c in copies:
+        c.wait()
+
+
+def final_kernel(assign, partial, last_y, last_x, before, out, block, sems):
+    half = last_y.shape[0]
+    for side, last in enumerate((last_y, last_x)):
+        rows = slice(side * half, (side + 1) * half)
+        block[rows, :] = (partial[rows, :] + last[...].astype(jnp.float32)).astype(jnp.bfloat16)
+    for c in put_rows(assign, CHUNKS[0], block, out, sems):
+        c.wait()
 
 
 def shape(*dims):
@@ -577,7 +627,7 @@
         [HBM],
         [VMEM] * 3,
         [pltpu.SemaphoreType.DMA((3,))],
-        8,
+        60,
         2 * 10**9,
         encoder_weights,
     )
@@ -630,7 +680,7 @@
             pltpu.SemaphoreType.DMA((3 * most,)),
             pltpu.SemaphoreType.DMA((3 * most,)),
         ],
-        8,
+        60,
         4 * 10**9,
         assign,
         owners,
@@ -647,7 +697,7 @@
         [SMEM, VMEM, VMEM],
         [HBM] * 5,
         [pltpu.VMEM((tokens, width_c), bf16), pltpu.SemaphoreType.DMA((8,))],
-        16,
+        54,
         2 * tokens * feat * width_c,
         assign,
         states,
@@ -660,66 +710,106 @@
     context = [own_c, from_x, from_y, last_y, last_x]
 
     half_t = tokens // 2
-    states_x, states_y = to(1, states), to(2, states)
-    d0, d1 = to(2, states_x[:half_t]), to(1, states_y[half_t:])
-
-    source, within = call(
-        functools.partial(self_kernel, n_span),
-        [shape(per * RETRIEVED, ENC_WIDTH)] * 2,
-        [SMEM] * 3 + [HBM] * (4 + n_pieces[0]),
+    s0, s1 = call(
+        halves_kernel,
+        [shape(half_t, feat)] * 2,
+        [HBM],
         [VMEM] * 2,
-        [
-            pltpu.VMEM((ENC_WIDTH, widths[0]), bf16),
-            pltpu.VMEM((per * RETRIEVED, widths[0]), bf16),
-            pltpu.VMEM((per * ENC_WIDTH, RETRIEVED), jnp.float32),
-            pltpu.VMEM((per * ENC_WIDTH, RETRIEVED), bf16),
-            pltpu.SemaphoreType.DMA((per,)),
-            pltpu.SemaphoreType.DMA((n_pieces[0],)),
-        ],
-        20,
-        4 * per * RETRIEVED * ENC_WIDTH * widths[0],
+        [pltpu.SemaphoreType.DMA((2,))],
+        60,
+        2 * 10**9,
+        states,
+    )
+    x0, y1 = to(1, s0), to(2, s1)
+    x1, y0 = to(1, s1), to(2, s0)
+    d0, d1 = to(2, x0), to(1, y1)
+
+    held = []
+    for i, n_last in enumerate((2, 4, 2)):
+        n_early = n_pieces[i] - n_last
+        held.append(
+            call(
+                functools.partial(early_weights_kernel, n_span, starts[i], n_pieces[i]),
+                pltpu.VMEM((ENC_WIDTH, widths[i]), bf16),
+                [HBM] * n_early,
+                VMEM,
+                [pltpu.SemaphoreType.DMA((n_early,))],
+                16,
+                2 * 10**9,
+                *parts[i][:n_early],
+            )
+        )
+    source = call(
+        source_kernel,
+        pltpu.VMEM((per * RETRIEVED, ENC_WIDTH), bf16),
+        [SMEM] * 3 + [HBM] * 4,
+        VMEM,
+        [pltpu.SemaphoreType.DMA((per,))],
+        16,
+        2 * 10**9,
         assign,
         owners,
         slots,
         store,
         *raw,
-        *parts[0],
-    )
-    span_rows = NEIGHBOURS * RETRIEVED
-    middle, across = call(
-        functools.partial(cross_kernel, n_span, starts[1]),
-        [shape(per * RETRIEVED, ENC_WIDTH)] * 2,
-        [VMEM] * 7 + [HBM] * n_pieces[1],
+    )
+    within, _ = call(
+        functools.partial(self_kernel, n_span),
+        [
+            pltpu.VMEM((per * RETRIEVED, ENC_WIDTH), bf16),
+            pltpu.VMEM((ENC_WIDTH, widths[0]), bf16),
+        ],
+        [VMEM] * 2 + [HBM] * 2,
         [VMEM] * 2,
         [
-            pltpu.VMEM((ENC_WIDTH, widths[1]), bf16),
+            pltpu.VMEM((per * RETRIEVED, widths[0]), bf16),
+            pltpu.VMEM((per * ENC_WIDTH, RETRIEVED), jnp.float32),
+            pltpu.VMEM((per * ENC_WIDTH, RETRIEVED), bf16),
+            pltpu.SemaphoreType.DMA((2,)),
+        ],
+        20,
+        4 * per * RETRIEVED * ENC_WIDTH * widths[0],
+        source,
+        held[0],
+        *parts[0][-2:],
+        aliases={1: 1}.items(),
+    )
+    span_rows = NEIGHBOURS * RETRIEVED
+    rows_e = per * RETRIEVED
+    middle, across, _ = call(
+        functools.partial(cross_kernel, n_span, n_pieces[1]),
+        [pltpu.VMEM((rows_e, ENC_WIDTH), bf16)] * 2 + [pltpu.VMEM((ENC_WIDTH, widths[1]), bf16)],
+        [VMEM] * 8 + [HBM] * 4,
+        [VMEM] * 3,
+        [
             pltpu.VMEM((rows_c, width_c), bf16),
-            pltpu.VMEM((per * RETRIEVED, ENC_WIDTH), bf16),
+            pltpu.VMEM((rows_e, ENC_WIDTH), bf16),
             pltpu.VMEM((per * ENC_WIDTH, SPAN_LEN), jnp.float32),
             pltpu.VMEM((per * ENC_WIDTH, SPAN_LEN), bf16),
-            pltpu.SemaphoreType.DMA((n_pieces[1],)),
+            pltpu.SemaphoreType.DMA((4,)),
         ],
         20,
-        4 * per * RETRIEVED * ENC_WIDTH * widths[1],
+        4 * rows_e * ENC_WIDTH * widths[1],
         source,
         within,
         *context,
-        *parts[1],
-    )
-    enc = call(
-        functools.partial(encoded_kernel, n_span, starts[2]),
-        [shape(span_rows, ENC_WIDTH)] * own_spans,
-        [VMEM] * 2 + [HBM] * n_pieces[2],
-        [VMEM] * own_spans,
-        [
-            pltpu.VMEM((ENC_WIDTH, widths[2]), bf16),
-            pltpu.SemaphoreType.DMA((n_pieces[2],)),
-        ],
+        held[1],
+        *parts[1][-4:],
+        aliases={7: 2}.items(),
+    )
+    *enc, _ = call(
+        functools.partial(encoded_kernel, n_span),
+        [shape(span_rows, ENC_WIDTH)] * own_spans + [pltpu.VMEM((ENC_WIDTH, widths[2]), bf16)],
+        [VMEM] * 3 + [HBM] * 2,
+        [VMEM] * (own_spans + 1),
+        [pltpu.SemaphoreType.DMA((2,))],
         16,
-        4 * per * RETRIEVED * ENC_WIDTH * widths[2],
+        4 * rows_e * ENC_WIDTH * widths[2],
         middle,
         across,
-        *parts[2],
+        held[2],
+        *parts[2][-2:],
+        aliases={2: own_spans}.items(),
     )
     first = own_spans // 2
     x = [to(1, e) for e in enc]
@@ -730,7 +820,7 @@
     queries = call(
         query_kernel,
         shape(tokens, local),
-        [VMEM] * 5 + [HBM],
+        [VMEM] * 7 + [HBM],
         VMEM,
         [
             pltpu.VMEM((4, feat, local), bf16),
@@ -740,8 +830,10 @@
         24,
         8 * tokens * feat * local,
         states,
-        states_x,
-        states_y,
+        x0,
+        x1,
+        y0,
+        y1,
         d0,
         d1,
         query_weight,
@@ -799,18 +891,39 @@
         near_x, near_y = to(1, to_x), to(2, to_y)
         last_y = to(2, add(keep_a[:, feat:], near_x[:, feat:]))
         last_x = to(1, add(keep_b[:, feat:], near_y[:, feat:]))
-        terms += [keep_a, keep_b, near_x, near_y, last_y, last_x]
-    return call(
-        final_kernel,
-        shape(tokens, feat),
-        [SMEM] + [VMEM] * 13,
-        VMEM,
-        [],
+        terms.append(((keep_a, keep_b), (near_x, near_y), (last_y, last_x)))
+    (keep_1, near_1, last_1), (keep_2, near_2, last_2) = terms
+    half_rows = tokens // 2
+    rows_scratch = [pltpu.VMEM((half_rows, feat), bf16), pltpu.SemaphoreType.DMA((4,))]
+    before, partial = call(
+        almost_kernel,
+        [shape(tokens, feat), pltpu.VMEM((half_rows, feat), jnp.float32)],
+        [SMEM] + [VMEM] * 11,
+        [HBM, VMEM],
+        rows_scratch,
         16,
         17 * tokens * feat,
         assign,
         states,
-        *terms,
+        *keep_1,
+        *keep_2,
+        *near_1,
+        *near_2,
+        *last_1,
+    )
+    return call(
+        final_kernel,
+        shape(tokens, feat),
+        [SMEM] + [VMEM] * 3 + [HBM],
+        HBM,
+        rows_scratch,
+        16,
+        4 * tokens * feat,
+        assign,
+        partial,
+        *last_2,
+        before,
+        aliases={4: 0}.items(),
     )
 
 

time: 207 us -> 200 us (0.966)
  waiting for transfers between devices: 109 us -> 85.6 us
  Pallas kernels: 53.3 us -> 61.5 us
  starting transfers between devices: 34.7 us -> 42.5 us
  local copies, waits for them, and re-layouts: 9.28 us -> 6.43 us
    ppermute x10, waiting for transfers between devices: 52.8 us -> 24.7 us  [ring(): lax.ppermute(value, 'span', [(i, (i + 1) % n_span) for i in range(n_span)])]
    ppermute x27 -> x29, starting transfers between devices: 26.1 us -> 34.4 us  [to(): return lax.ppermute(value, 'head', [(i, i ^ k) for i in range(4)])]
    pallas_call x11 -> x17, Pallas kernels: 51.7 us -> 59.8 us  [call(): pl.pallas_call(kernel, out_shape=out_shape, in_specs=in_specs, out_specs=...]
    ppermute x27 -> x29, waiting for transfers between devices: 54.8 us -> 60.9 us  [to(): return lax.ppermute(value, 'head', [(i, i ^ k) for i in range(4)])]
    unnamed x41 -> x45, local copies, waits for them, and re-layouts: 9.21 us -> 6.43 us
  transfers between devices with their start and end apart: 50 -> 52, of which waited for: 17 -> 21; matrix products, arithmetic and copies ran while one was open for 1% -> 2% of each run, Pallas kernels for 24% -> 29%
where the time goes in v2:
time: 200 us; the launch traced here: 199 us
  waiting for transfers between devices  85.6 us (43%)
  Pallas kernels  61.5 us (31%)
  starting transfers between devices  42.5 us (21%)
  local copies, waits for them, and re-layouts  6.43 us (3%)
  other arithmetic  2.45 us (1%)
    ppermute x29, waiting for transfers between devices, to(): return lax.ppermute(value, 'head', [(i, i ^ k) for i in range(4)])  60.9 us
    pallas_call x17, Pallas kernels, call(): pl.pallas_call(kernel, out_shape=out_shape, in_specs=in_specs, out_specs=...  59.8 us
    ppermute x29, starting transfers between devices, to(): return lax.ppermute(value, 'head', [(i, i ^ k) for i in range(4)])  34.4 us
    ppermute x10, waiting for transfers between devices, ring(): lax.ppermute(value, 'span', [(i, (i + 1) % n_span) for i in range(n_span)])  24.7 us
    ppermute x10, starting transfers between devices, ring(): lax.ppermute(value, 'span', [(i, (i + 1) % n_span) for i in range(n_span)])  6.59 us
    unnamed x45, local copies, waits for them, and re-layouts  6.43 us
  transfers between devices with their start and end apart: 52, of which 21 were waited for; matrix products, arithmetic and copies ran while one was open for 2% of the time, Pallas kernels for 29%

profile of v2, /device:TPU:0, one launch (start us, length us, event | category | flops | bytes accessed | tf_op | source)
XLA Modules:
  0.0 199.2 jit_solution(12868601496335507078)
XLA Ops:
  0.0 2.1 %shard_map.104 = (bf16[112,2688]{1,0:T(8,128)(2,1)}, bf16[112,896]{1,0:T(8,128)(2,1)}, bf16[112,896]{1,0:T(8,128)(2,1)}) custom-call(bf16[112,5376]{1,0:T(8,128)(2,1)} %rest_0_.5), custom_call_target="tpu_custom_call" | custom-call | flops 2000000000 | bytes 1204224 | tf_op jit(solution)/shard_map/pallas_call | solution.py:119
  2.2 3.1 %collective-permute-start.20 = (bf16[112,896]{1,0:T(8,128)(2,1)}, bf16[112,896]{1,0:T(8,128)(2,1)S(1)}, u32[]{:S(2)}, u32[]{:S(2)}) collective-permute-start(bf16[112,896]{1,0:T(8,128)(2,1)} %get-tuple-element.45), channel_id=1, source_target_pairs={{0,8},{8,16},{16,24},{24,0},{1,9},{9,17},{17,25},{25,1},{2,10},{10... | collective-permute-start | bytes 602120 | tf_op jit(solution)/shard_map/ppermute | solution.py:638
  10.1 3.2 %collective-permute-done.20.rest_2_ = bf16[112,896]{1,0:T(8,128)(2,1)S(1)} collective-permute-done((bf16[112,896]{1,0:T(8,128)(2,1)}, bf16[112,896]{1,0:T(8,128)(2,1)S(1)}, u32[]{:S(2)}, u32[]{:S(2)}) %collective-permute-start.20) | collective-permute-done | bytes 200736 | tf_op jit(solution)/shard_map/ppermute | solution.py:638
  15.1 2.6 %collective-permute-done.32.rest_2_ = bf16[112,896]{1,0:T(8,128)(2,1)S(1)} collective-permute-done((bf16[112,896]{1,0:T(8,128)(2,1)}, bf16[112,896]{1,0:T(8,128)(2,1)S(1)}, u32[]{:S(2)}, u32[]{:S(2)}) %collective-permute-start.32) | collective-permute-done | bytes 200736 | tf_op jit(solution)/shard_map/ppermute | solution.py:638
  17.6 3.4 %shard_map.102 = (bf16[2,128,896]{2,1,0:T(8,128)(2,1)}, bf16[2,128,896]{2,1,0:T(8,128)(2,1)}, bf16[2,128,896]{2,1,0:T(8,128)(2,1)}) custom-call(s32[8]{0:T(128)} %plan.1.assign, s32[2,8]{1,0:T(2,128)} %bitcast.11, s32[2,8]{1,0:T(2,128)} %bitcast.17, bf16[8,128,896]{2,1,0:T(8,128)(2,1)} %bitcast.15), custom_call_target="tpu_custom_call" | custom-call | flops 4000000000 | bytes 1835088 | tf_op jit(solution)/shard_map/pallas_call | solution.py:119
  24.8 6.1 %shard_map.107 = (bf16[128,1792]{1,0:T(8,128)(2,1)}, bf16[128,1792]{1,0:T(8,128)(2,1)}, bf16[128,1792]{1,0:T(8,128)(2,1)}, bf16[64,1792]{1,0:T(8,128)(2,1)}, bf16[64,1792]{1,0:T(8,128)(2,1)}) custom-call(s32[8]{0:T(128)} %plan.1.assign, bf16[512,1024]{1,0:T(8,128)(2,1)} %states.3, bf16[1024,1792]{1,0:T(8,128)(2,1)} %w.3), custom_call_target="tpu_custom_call" | custom-call | flops 1879048192 | bytes 4718608 | tf_op jit(solution)/shard_map/pallas_call | solution.py:119
  30.8 3.3 %collective-permute-done.34.rest_4_ = bf16[112,896]{1,0:T(8,128)(2,1)} collective-permute-done((bf16[112,896]{1,0:T(8,128)(2,1)S(1)}, bf16[112,896]{1,0:T(8,128)(2,1)}, u32[]{:S(2)}, u32[]{:S(2)}) %collective-permute-start.34) | collective-permute-done | bytes 200736 | tf_op jit(solution)/shard_map/ppermute | solution.py:638
  35.7 2.2 %shard_map.100 = (bf16[256,1024]{1,0:T(8,128)(2,1)}, bf16[256,1024]{1,0:T(8,128)(2,1)}) custom-call(bf16[512,1024]{1,0:T(8,128)(2,1)} %states.3), custom_call_target="tpu_custom_call" | custom-call | flops 2000000000 | bytes 1048576 | tf_op jit(solution)/shard_map/pallas_call | solution.py:119
  39.2 5.4 %collective-permute-done.7.r2 = bf16[2,128,896]{2,1,0:T(8,128)(2,1)S(1)} collective-permute-done((bf16[2,128,896]{2,1,0:T(8,128)(2,1)}, bf16[2,128,896]{2,1,0:T(8,128)(2,1)S(1)}, u32[]{:S(2)}, u32[]{:S(2)}) %collective-permute-start.7) | collective-permute-done | bytes 458784 | tf_op jit(solution)/shard_map/ppermute | solution.py:597
  45.3 2.4 %collective-permute-start.17 = (bf16[128,1792]{1,0:T(8,128)(2,1)}, bf16[128,1792]{1,0:T(8,128)(2,1)}, u32[]{:S(2)}, u32[]{:S(2)}) collective-permute-start(bf16[128,1792]{1,0:T(8,128)(2,1)} %get-tuple-element.42), channel_id=1, source_target_pairs={{0,4},{2,6},{4,0},{6,2},{1,5},{3,7},{5,1},{7,3},{8,12},{10,14},{12... | collective-permute-start | bytes 1376264 | tf_op jit(solution)/shard_map/ppermute | solution.py:597
  47.8 6.6 %collective-permute-done.16.from_x = bf16[128,1792]{1,0:T(8,128)(2,1)S(1)} collective-permute-done((bf16[128,1792]{1,0:T(8,128)(2,1)}, bf16[128,1792]{1,0:T(8,128)(2,1)S(1)}, u32[]{:S(2)}, u32[]{:S(2)}) %collective-permute-start.16) | collective-permute-done | bytes 458784 | tf_op jit(solution)/shard_map/ppermute | solution.py:597
  54.5 4.9 %collective-permute-done.17.from_y = bf16[128,1792]{1,0:T(8,128)(2,1)} collective-permute-done((bf16[128,1792]{1,0:T(8,128)(2,1)}, bf16[128,1792]{1,0:T(8,128)(2,1)}, u32[]{:S(2)}, u32[]{:S(2)}) %collective-permute-start.17) | collective-permute-done | bytes 458784 | tf_op jit(solution)/shard_map/ppermute | solution.py:597
  59.4 5.8 %collective-permute-done.x0 = bf16[256,1024]{1,0:T(8,128)(2,1)} collective-permute-done((bf16[256,1024]{1,0:T(8,128)(2,1)}, bf16[256,1024]{1,0:T(8,128)(2,1)}, u32[]{:S(2)}, u32[]{:S(2)}) %collective-permute-start) | collective-permute-done | bytes 524320 | tf_op jit(solution)/shard_map/ppermute | solution.py:597
  65.2 4.4 %collective-permute-done.3.y1 = bf16[256,1024]{1,0:T(8,128)(2,1)} collective-permute-done((bf16[256,1024]{1,0:T(8,128)(2,1)}, bf16[256,1024]{1,0:T(8,128)(2,1)}, u32[]{:S(2)}, u32[]{:S(2)}) %collective-permute-start.3) | collective-permute-done | bytes 524320 | tf_op jit(solution)/shard_map/ppermute | solution.py:597
  69.7 3.7 %collective-permute-done.24.rest_6_ = bf16[112,896]{1,0:T(8,128)(2,1)S(1)} collective-permute-done((bf16[112,896]{1,0:T(8,128)(2,1)S(1)}, bf16[112,896]{1,0:T(8,128)(2,1)S(1)}, u32[]{:S(2)}, u32[]{:S(2)}) %collective-permute-start.24) | collective-permute-done | bytes 200736 | tf_op jit(solution)/shard_map/ppermute | solution.py:638
  75.0 4.5 %collective-permute-done.36.own = bf16[112,896]{1,0:T(8,128)(2,1)S(1)} collective-permute-done((bf16[112,896]{1,0:T(8,128)(2,1)}, bf16[112,896]{1,0:T(8,128)(2,1)S(1)}, u32[]{:S(2)}, u32[]{:S(2)}) %collective-permute-start.36) | collective-permute-done | bytes 200736 | tf_op jit(solution)/shard_map/ppermute | solution.py:638
  80.7 4.9 %collective-permute-done.26.rest_8_ = bf16[112,896]{1,0:T(8,128)(2,1)S(1)} collective-permute-done((bf16[112,896]{1,0:T(8,128)(2,1)S(1)}, bf16[112,896]{1,0:T(8,128)(2,1)S(1)}, u32[]{:S(2)}, u32[]{:S(2)}) %collective-permute-start.26) | collective-permute-done | bytes 200736 | tf_op jit(solution)/shard_map/ppermute | solution.py:597
  85.6 6.8 %collective-permute-done.14.own = bf16[112,2688]{1,0:T(8,128)(2,1)S(1)} collective-permute-done((bf16[112,2688]{1,0:T(8,128)(2,1)S(1)}, bf16[112,2688]{1,0:T(8,128)(2,1)S(1)}, u32[]{:S(2)}, u32[]{:S(2)}) %collective-permute-start.14) | collective-permute-done | bytes 602144 | tf_op jit(solution)/shard_map/ppermute | solution.py:638
  104.5 3.0 %collective-permute-done.18.last_y = bf16[64,1792]{1,0:T(8,128)(2,1)S(1)} collective-permute-done((bf16[64,1792]{1,0:T(8,128)(2,1)S(1)}, bf16[64,1792]{1,0:T(8,128)(2,1)S(1)}, u32[]{:S(2)}, u32[]{:S(2)}) %collective-permute-start.18) | collective-permute-done | bytes 229408 | tf_op jit(solution)/shard_map/ppermute | solution.py:597
  113.1 4.8 %shard_map.106 = (bf16[512,896]{1,0:T(8,128)(2,1)S(1)}, bf16[896,2688]{1,0:T(8,128)(2,1)S(1)}) custom-call(bf16[512,896]{1,0:T(8,128)(2,1)S(1)} %shard_map.103.source, bf16[896,2688]{1,0:T(8,128)(2,1)S(1)} %shard_map.105.early, bf16[112,2688]{1,0:T(8,128)(2,1)S(1)} %collective-permute-done.14.own, ...), custom_call_target="tpu_custom_call", output_to_operand_aliasing={{1}: (1, {})} | custom-call | flops 4932501504 | bytes 6938624 | tf_op jit(solution)/shard_map/pallas_call | solution.py:119
  118.5 4.7 %shard_map.109 = (bf16[512,896]{1,0:T(8,128)(2,1)S(1)}, bf16[512,896]{1,0:T(8,128)(2,1)S(1)}, bf16[896,1792]{1,0:T(8,128)(2,1)S(1)}) custom-call(bf16[512,896]{1,0:T(8,128)(2,1)S(1)} %shard_map.103.source, bf16[512,896]{1,0:T(8,128)(2,1)S(1)} %get-tuple-element.39.within, bf16[128,1792]{1,0:T(8,128)(2,1)S(1)} %copy-done.14, ...), custom_call_target="tpu_custom_call", output_to_operand_aliasing={{2}: (7, {})} | custom-call | flops 3288334336 | bytes 7684096 | tf_op jit(solution)/shard_map/pallas_call | solution.py:119
  128.7 6.7 %collective-permute-done.4.d0 = bf16[256,1024]{1,0:T(8,128)(2,1)S(1)} collective-permute-done((bf16[256,1024]{1,0:T(8,128)(2,1)}, bf16[256,1024]{1,0:T(8,128)(2,1)S(1)}, u32[]{:S(2)}, u32[]{:S(2)}) %collective-permute-start.4) | collective-permute-done | bytes 524320 | tf_op jit(solution)/shard_map/ppermute | solution.py:597
  135.4 6.7 %shard_map.101.queries = bf16[512,1024]{1,0:T(8,128)(2,1)S(1)} custom-call(bf16[512,1024]{1,0:T(8,128)(2,1)S(1)} %copy-done.1, bf16[256,1024]{1,0:T(8,128)(2,1)} %collective-permute-done.x0, bf16[256,1024]{1,0:T(8,128)(2,1)S(1)} %collective-permute-done.1.x1, bf16[256,1024]{1,0:T(8,128)(2,1)S(1)} %collective-permute-done.2.y0, ...), custom_call_target="tpu_custom_call" | custom-call | flops 4294967296 | bytes 12582912 | tf_op jit(solution)/shard_map/pallas_call | solution.py:119
  146.9 9.7 %shard_map.112 = (bf16[128,2048]{1,0:T(8,128)(2,1)S(1)}, bf16[128,2048]{1,0:T(8,128)(2,1)S(1)}, bf16[128,2048]{1,0:T(8,128)(2,1)S(1)}, bf16[128,2048]{1,0:T(8,128)(2,1)S(1)}) custom-call(s32[8]{0:T(128)S(1)} %copy-done.2, bf16[512,1024]{1,0:T(8,128)(2,1)S(1)} %shard_map.101.queries, bf16[256,896]{1,0:T(8,128)(2,1)S(1)} %get-tuple-element.49.rest_0_, ...), custom_call_target="tpu_custom_call" | custom-call | flops 7516192768 | bytes 14942224 | tf_op jit(solution)/shard_map/pallas_call | solution.py:119
  159.0 4.1 %shard_map.113.rest_2_ = bf16[128,1024]{1,0:T(8,128)(2,1)S(1)} custom-call(s32[8]{0:T(128)S(1)} %copy-done.2, bf16[512,1024]{1,0:T(8,128)(2,1)S(1)} %shard_map.101.queries, bf16[256,896]{1,0:T(8,128)(2,1)S(1)} %collective-permute-done.42.rest_0_, bf16[256,896]{1,0:T(8,128)(2,1)S(1)} %collective-permute-done.43.rest_1_, bf16[896,2048]{1,0:T(8,128)(2,1)S(1)} %bitcast.6), custom_call_target="tpu_custom_call" | custom-call | flops 3758096384 | bytes 5636112 | tf_op jit(solution)/shard_map/pallas_call | solution.py:119
  163.2 2.2 %collective-permute-done.40.rest_0_ = bf16[256,896]{1,0:T(8,128)(2,1)S(1)} collective-permute-done((bf16[256,896]{1,0:T(8,128)(2,1)S(1)}, bf16[256,896]{1,0:T(8,128)(2,1)S(1)}, u32[]{:S(2)}, u32[]{:S(2)}) %collective-permute-start.40) | collective-permute-done | bytes 458784 | tf_op jit(solution)/shard_map/ppermute | solution.py:597
  167.4 6.7 %shard_map.114 = (bf16[128,2048]{1,0:T(8,128)(2,1)S(1)}, bf16[128,2048]{1,0:T(8,128)(2,1)S(1)}, bf16[128,2048]{1,0:T(8,128)(2,1)S(1)}, bf16[128,2048]{1,0:T(8,128)(2,1)S(1)}) custom-call(s32[8]{0:T(128)S(1)} %copy-done.2, bf16[512,1024]{1,0:T(8,128)(2,1)S(1)} %shard_map.101.queries, bf16[256,896]{1,0:T(8,128)(2,1)S(1)} %collective-permute-done.40.rest_0_, ...), custom_call_target="tpu_custom_call" | custom-call | flops 3758096384 | bytes 14286864 | tf_op jit(solution)/shard_map/pallas_call | solution.py:119
  175.9 2.1 %collective-permute-done.44.rest_4_ = bf16[128,2048]{1,0:T(8,128)(2,1)S(1)} collective-permute-done((bf16[128,2048]{1,0:T(8,128)(2,1)S(1)}, bf16[128,2048]{1,0:T(8,128)(2,1)S(1)}, u32[]{:S(2)}, u32[]{:S(2)}) %collective-permute-start.44) | collective-permute-done | bytes 524320 | tf_op jit(solution)/shard_map/ppermute | solution.py:597
  178.2 2.4 %collective-permute-start.49 = (bf16[128,1024]{1,0:T(8,128)(2,1)S(1)}, bf16[128,1024]{1,0:T(8,128)(2,1)S(1)}, u32[]{:S(2)}, u32[]{:S(2)}) collective-permute-start(bf16[128,1024]{1,0:T(8,128)(2,1)S(1)} %add_convert_fusion.2), channel_id=1, source_target_pairs={{0,2},{2,0},{4,6},{6,4},{1,3},{3,1},{5,7},{7,5},{8,10},{10,8},{12,... | collective-permute-start | bytes 786440 | tf_op jit(solution)/shard_map/ppermute | solution.py:597
  180.6 8.6 %collective-permute-done.46.rest_6_ = bf16[128,2048]{1,0:T(8,128)(2,1)S(1)} collective-permute-done((bf16[128,2048]{1,0:T(8,128)(2,1)S(1)}, bf16[128,2048]{1,0:T(8,128)(2,1)S(1)}, u32[]{:S(2)}, u32[]{:S(2)}) %collective-permute-start.46) | collective-permute-done | bytes 524320 | tf_op jit(solution)/shard_map/ppermute | solution.py:597
  189.4 2.4 %collective-permute-start.51 = (bf16[128,1024]{1,0:T(8,128)(2,1)S(1)}, bf16[128,1024]{1,0:T(8,128)(2,1)S(1)}, u32[]{:S(2)}, u32[]{:S(2)}) collective-permute-start(bf16[128,1024]{1,0:T(8,128)(2,1)S(1)} %add_convert_fusion), channel_id=1, source_target_pairs={{0,2},{2,0},{4,6},{6,4},{1,3},{3,1},{5,7},{7,5},{8,10},{10,8},{12,... | collective-permute-start | bytes 786440 | tf_op jit(solution)/shard_map/ppermute | solution.py:597
  191.8 2.8 %collective-permute-done.48.rest_8_ = bf16[128,1024]{1,0:T(8,128)(2,1)S(1)} collective-permute-done((bf16[128,1024]{1,0:T(8,128)(2,1)S(1)}, bf16[128,1024]{1,0:T(8,128)(2,1)S(1)}, u32[]{:S(2)}, u32[]{:S(2)}) %collective-permute-start.48) | collective-permute-done | bytes 262176 | tf_op jit(solution)/shard_map/ppermute | solution.py:597
  (144 shorter events, 56.2 us)
Async XLA Ops:
  6.8 40.9 %collective-permute-start.10 = (bf16[112,2688]{1,0:T(8,128)(2,1)}, bf16[112,2688]{1,0:T(8,128)(2,1)S(1)}, u32[]{:S(2)}, u32[]{:S(2)}) collective-permute-start(bf16[112,2688]{1,0:T(8,128)(2,1)} %get-tuple-element.38), channel_id=1, source_target_pairs={{0,8},{8,16},{16,24},{24,0},{1,9},{9,17},{17,25},{25,1},{2,10},{10... | collective-permute-start | bytes 1806344 | tf_op jit(solution)/shard_map/ppermute | solution.py:638
  21.1 16.8 %collective-permute-start.6 = (bf16[2,128,896]{2,1,0:T(8,128)(2,1)}, bf16[2,128,896]{2,1,0:T(8,128)(2,1)S(1)}, u32[]{:S(2)}, u32[]{:S(2)}) collective-permute-start(bf16[2,128,896]{2,1,0:T(8,128)(2,1)} %get-tuple-element.35), channel_id=1, source_target_pairs={{0,2},{2,0},{4,6},{6,4},{1,3},{3,1},{5,7},{7,5},{8,10},{10,8},{12,... | collective-permute-start | bytes 1376264 | tf_op jit(solution)/shard_map/ppermute | solution.py:597
  22.8 21.7 %collective-permute-start.7 = (bf16[2,128,896]{2,1,0:T(8,128)(2,1)}, bf16[2,128,896]{2,1,0:T(8,128)(2,1)S(1)}, u32[]{:S(2)}, u32[]{:S(2)}) collective-permute-start(bf16[2,128,896]{2,1,0:T(8,128)(2,1)} %get-tuple-element.36), channel_id=1, source_target_pairs={{0,4},{2,6},{4,0},{6,2},{1,5},{3,7},{5,1},{7,3},{8,12},{10,14},{12... | collective-permute-start | bytes 1376264 | tf_op jit(solution)/shard_map/ppermute | solution.py:597
  24.2 23.5 %collective-permute-start.8 = (bf16[2,128,896]{2,1,0:T(8,128)(2,1)}, bf16[2,128,896]{2,1,0:T(8,128)(2,1)}, u32[]{:S(2)}, u32[]{:S(2)}) collective-permute-start(bf16[2,128,896]{2,1,0:T(8,128)(2,1)} %get-tuple-element.37), channel_id=1, source_target_pairs={{0,6},{2,4},{4,2},{6,0},{1,7},{3,5},{5,3},{7,1},{8,14},{10,12},{12... | collective-permute-start | bytes 1376264 | tf_op jit(solution)/shard_map/ppermute | solution.py:597
  34.1 20.4 %collective-permute-start.16 = (bf16[128,1792]{1,0:T(8,128)(2,1)}, bf16[128,1792]{1,0:T(8,128)(2,1)S(1)}, u32[]{:S(2)}, u32[]{:S(2)}) collective-permute-start(bf16[128,1792]{1,0:T(8,128)(2,1)} %get-tuple-element.41), channel_id=1, source_target_pairs={{0,2},{2,0},{4,6},{6,4},{1,3},{3,1},{5,7},{7,5},{8,10},{10,8},{12,... | collective-permute-start | bytes 1376264 | tf_op jit(solution)/shard_map/ppermute | solution.py:597
  38.7 26.5 %collective-permute-start = (bf16[256,1024]{1,0:T(8,128)(2,1)}, bf16[256,1024]{1,0:T(8,128)(2,1)}, u32[]{:S(2)}, u32[]{:S(2)}) collective-permute-start(bf16[256,1024]{1,0:T(8,128)(2,1)} %get-tuple-element.33), channel_id=1, source_target_pairs={{0,2},{2,0},{4,6},{6,4},{1,3},{3,1},{5,7},{7,5},{8,10},{10,8},{12,... | collective-permute-start | bytes 1572872 | tf_op jit(solution)/shard_map/ppermute | solution.py:597
  45.3 14.1 %collective-permute-start.17 = (bf16[128,1792]{1,0:T(8,128)(2,1)}, bf16[128,1792]{1,0:T(8,128)(2,1)}, u32[]{:S(2)}, u32[]{:S(2)}) collective-permute-start(bf16[128,1792]{1,0:T(8,128)(2,1)} %get-tuple-element.42), channel_id=1, source_target_pairs={{0,4},{2,6},{4,0},{6,2},{1,5},{3,7},{5,1},{7,3},{8,12},{10,14},{12... | collective-permute-start | bytes 1376264 | tf_op jit(solution)/shard_map/ppermute | solution.py:597
  47.7 25.7 %collective-permute-start.12 = (bf16[112,2688]{1,0:T(8,128)(2,1)S(1)}, bf16[112,2688]{1,0:T(8,128)(2,1)S(1)}, u32[]{:S(2)}, u32[]{:S(2)}) collective-permute-start(bf16[112,2688]{1,0:T(8,128)(2,1)S(1)} %collective-permute-done.10.rest_2_), channel_id=1, source_target_pairs={{0,8},{8,16},{16,24},{24,0},{1,9},{9,17},{17,25},{25,1},{2,10},{10... | collective-permute-start | bytes 1806344 | tf_op jit(solution)/shard_map/ppermute | solution.py:638
  47.7 21.9 %collective-permute-start.3 = (bf16[256,1024]{1,0:T(8,128)(2,1)}, bf16[256,1024]{1,0:T(8,128)(2,1)}, u32[]{:S(2)}, u32[]{:S(2)}) collective-permute-start(bf16[256,1024]{1,0:T(8,128)(2,1)} %get-tuple-element.34), channel_id=1, source_target_pairs={{0,4},{2,6},{4,0},{6,2},{1,5},{3,7},{5,1},{7,3},{8,12},{10,14},{12... | collective-permute-start | bytes 1572872 | tf_op jit(solution)/shard_map/ppermute | solution.py:597
  54.5 31.1 %collective-permute-start.9 = (bf16[112,5376]{1,0:T(8,128)(2,1)S(1)}, bf16[112,5376]{1,0:T(8,128)(2,1)S(1)}, u32[]{:S(2)}, u32[]{:S(2)}) collective-permute-start(bf16[112,5376]{1,0:T(8,128)(2,1)S(1)} %copy-done), channel_id=1, source_target_pairs={{0,1},{1,0},{2,3},{3,2},{4,5},{5,4},{6,7},{7,6},{8,9},{9,8},{10,11... | collective-permute-start | bytes 3612680 | tf_op jit(solution)/shard_map/ppermute | solution.py:641
  73.4 19.0 %collective-permute-start.14 = (bf16[112,2688]{1,0:T(8,128)(2,1)S(1)}, bf16[112,2688]{1,0:T(8,128)(2,1)S(1)}, u32[]{:S(2)}, u32[]{:S(2)}) collective-permute-start(bf16[112,2688]{1,0:T(8,128)(2,1)S(1)} %collective-permute-done.12.rest_4_), channel_id=1, source_target_pairs={{0,8},{8,16},{16,24},{24,0},{1,9},{9,17},{17,25},{25,1},{2,10},{10... | collective-permute-start | bytes 1806344 | tf_op jit(solution)/shard_map/ppermute | solution.py:638
  74.4 28.6 %collective-permute-start.11 = (bf16[112,2688]{1,0:T(8,128)(2,1)S(1)}, bf16[112,2688]{1,0:T(8,128)(2,1)S(1)}, u32[]{:S(2)}, u32[]{:S(2)}) collective-permute-start(bf16[112,2688]{1,0:T(8,128)(2,1)S(1)} %collective-permute-done.10.rest_2_), channel_id=1, source_target_pairs={{0,1},{1,0},{2,3},{3,2},{4,5},{5,4},{6,7},{7,6},{8,9},{9,8},{10,11... | collective-permute-start | bytes 1806344 | tf_op jit(solution)/shard_map/ppermute | solution.py:641
  79.5 23.5 %collective-permute-start.13 = (bf16[112,2688]{1,0:T(8,128)(2,1)S(1)}, bf16[112,2688]{1,0:T(8,128)(2,1)S(1)}, u32[]{:S(2)}, u32[]{:S(2)}) collective-permute-start(bf16[112,2688]{1,0:T(8,128)(2,1)S(1)} %collective-permute-done.12.rest_4_), channel_id=1, source_target_pairs={{0,1},{1,0},{2,3},{3,2},{4,5},{5,4},{6,7},{7,6},{8,9},{9,8},{10,11... | collective-permute-start | bytes 1806344 | tf_op jit(solution)/shard_map/ppermute | solution.py:641
  85.6 13.9 %collective-permute-start.28 = (bf16[112,896]{1,0:T(8,128)(2,1)S(1)}, bf16[112,896]{1,0:T(8,128)(2,1)S(1)}, u32[]{:S(2)}, u32[]{:S(2)}) collective-permute-start(bf16[112,896]{1,0:T(8,128)(2,1)S(1)} %collective-permute-done.24.rest_6_), channel_id=1, source_target_pairs={{0,8},{8,16},{16,24},{24,0},{1,9},{9,17},{17,25},{25,1},{2,10},{10... | collective-permute-start | bytes 602120 | tf_op jit(solution)/shard_map/ppermute | solution.py:638
  85.6 15.5 %collective-permute-start.27 = (bf16[112,896]{1,0:T(8,128)(2,1)S(1)}, bf16[112,896]{1,0:T(8,128)(2,1)S(1)}, u32[]{:S(2)}, u32[]{:S(2)}) collective-permute-start(bf16[112,896]{1,0:T(8,128)(2,1)S(1)} %collective-permute-done.26.rest_8_), channel_id=1, source_target_pairs={{0,1},{1,0},{2,3},{3,2},{4,5},{5,4},{6,7},{7,6},{8,9},{9,8},{10,11... | collective-permute-start | bytes 602120 | tf_op jit(solution)/shard_map/ppermute | solution.py:641
  92.4 20.7 %collective-permute-start.15 = (bf16[112,2688]{1,0:T(8,128)(2,1)S(1)}, bf16[112,2688]{1,0:T(8,128)(2,1)S(1)}, u32[]{:S(2)}, u32[]{:S(2)}) collective-permute-start(bf16[112,2688]{1,0:T(8,128)(2,1)S(1)} %collective-permute-done.14.own), channel_id=1, source_target_pairs={{0,1},{1,0},{2,3},{3,2},{4,5},{5,4},{6,7},{7,6},{8,9},{9,8},{10,11... | collective-permute-start | bytes 1806344 | tf_op jit(solution)/shard_map/ppermute | solution.py:641
  107.6 18.4 %collective-permute-start.1 = (bf16[256,1024]{1,0:T(8,128)(2,1)S(1)}, bf16[256,1024]{1,0:T(8,128)(2,1)S(1)}, u32[]{:S(2)}, u32[]{:S(2)}) collective-permute-start(bf16[256,1024]{1,0:T(8,128)(2,1)S(1)} %copy-done.17), channel_id=1, source_target_pairs={{0,2},{2,0},{4,6},{6,4},{1,3},{3,1},{5,7},{7,5},{8,10},{10,8},{12,... | collective-permute-start | bytes 1572872 | tf_op jit(solution)/shard_map/ppermute | solution.py:597
  109.4 19.3 %collective-permute-start.2 = (bf16[256,1024]{1,0:T(8,128)(2,1)S(1)}, bf16[256,1024]{1,0:T(8,128)(2,1)S(1)}, u32[]{:S(2)}, u32[]{:S(2)}) collective-permute-start(bf16[256,1024]{1,0:T(8,128)(2,1)S(1)} %copy-done.16), channel_id=1, source_target_pairs={{0,4},{2,6},{4,0},{6,2},{1,5},{3,7},{5,1},{7,3},{8,12},{10,14},{12... | collective-permute-start | bytes 1572872 | tf_op jit(solution)/shard_map/ppermute | solution.py:597
  111.4 24.0 %collective-permute-start.4 = (bf16[256,1024]{1,0:T(8,128)(2,1)}, bf16[256,1024]{1,0:T(8,128)(2,1)S(1)}, u32[]{:S(2)}, u32[]{:S(2)}) collective-permute-start(bf16[256,1024]{1,0:T(8,128)(2,1)} %collective-permute-done.x0), channel_id=1, source_target_pairs={{0,4},{2,6},{4,0},{6,2},{1,5},{3,7},{5,1},{7,3},{8,12},{10,14},{12... | collective-permute-start | bytes 1572872 | tf_op jit(solution)/shard_map/ppermute | solution.py:597
  112.0 23.4 %collective-permute-start.5 = (bf16[256,1024]{1,0:T(8,128)(2,1)}, bf16[256,1024]{1,0:T(8,128)(2,1)S(1)}, u32[]{:S(2)}, u32[]{:S(2)}) collective-permute-start(bf16[256,1024]{1,0:T(8,128)(2,1)} %collective-permute-done.3.y1), channel_id=1, source_target_pairs={{0,2},{2,0},{4,6},{6,4},{1,3},{3,1},{5,7},{7,5},{8,10},{10,8},{12,... | collective-permute-start | bytes 1572872 | tf_op jit(solution)/shard_map/ppermute | solution.py:597
  125.0 19.3 %collective-permute-start.38 = (bf16[256,896]{1,0:T(8,128)(2,1)S(1)}, bf16[256,896]{1,0:T(8,128)(2,1)S(1)}, u32[]{:S(2)}, u32[]{:S(2)}) collective-permute-start(bf16[256,896]{1,0:T(8,128)(2,1)S(1)} %get-tuple-element.49.rest_0_), channel_id=1, source_target_pairs={{0,2},{2,0},{4,6},{6,4},{1,3},{3,1},{5,7},{7,5},{8,10},{10,8},{12,... | collective-permute-start | bytes 1376264 | tf_op jit(solution)/shard_map/ppermute | solution.py:597
  125.9 20.0 %collective-permute-start.39 = (bf16[256,896]{1,0:T(8,128)(2,1)S(1)}, bf16[256,896]{1,0:T(8,128)(2,1)S(1)}, u32[]{:S(2)}, u32[]{:S(2)}) collective-permute-start(bf16[256,896]{1,0:T(8,128)(2,1)S(1)} %get-tuple-element.50.rest_2_), channel_id=1, source_target_pairs={{0,4},{2,6},{4,0},{6,2},{1,5},{3,7},{5,1},{7,3},{8,12},{10,14},{12... | collective-permute-start | bytes 1376264 | tf_op jit(solution)/shard_map/ppermute | solution.py:597
  142.1 15.6 %collective-permute-start.42 = (bf16[256,896]{1,0:T(8,128)(2,1)S(1)}, bf16[256,896]{1,0:T(8,128)(2,1)S(1)}, u32[]{:S(2)}, u32[]{:S(2)}) collective-permute-start(bf16[256,896]{1,0:T(8,128)(2,1)S(1)} %get-tuple-element.49.rest_0_), channel_id=1, source_target_pairs={{0,4},{2,6},{4,0},{6,2},{1,5},{3,7},{5,1},{7,3},{8,12},{10,14},{12... | collective-permute-start | bytes 1376264 | tf_op jit(solution)/shard_map/ppermute | solution.py:597
  144.2 14.9 %collective-permute-start.43 = (bf16[256,896]{1,0:T(8,128)(2,1)S(1)}, bf16[256,896]{1,0:T(8,128)(2,1)S(1)}, u32[]{:S(2)}, u32[]{:S(2)}) collective-permute-start(bf16[256,896]{1,0:T(8,128)(2,1)S(1)} %get-tuple-element.50.rest_2_), channel_id=1, source_target_pairs={{0,2},{2,0},{4,6},{6,4},{1,3},{3,1},{5,7},{7,5},{8,10},{10,8},{12,... | collective-permute-start | bytes 1376264 | tf_op jit(solution)/shard_map/ppermute | solution.py:597
  144.3 21.1 %collective-permute-start.40 = (bf16[256,896]{1,0:T(8,128)(2,1)S(1)}, bf16[256,896]{1,0:T(8,128)(2,1)S(1)}, u32[]{:S(2)}, u32[]{:S(2)}) collective-permute-start(bf16[256,896]{1,0:T(8,128)(2,1)S(1)} %collective-permute-done.38.rest_1_), channel_id=1, source_target_pairs={{0,4},{2,6},{4,0},{6,2},{1,5},{3,7},{5,1},{7,3},{8,12},{10,14},{12... | collective-permute-start | bytes 1376264 | tf_op jit(solution)/shard_map/ppermute | solution.py:597
  145.9 21.5 %collective-permute-start.41 = (bf16[256,896]{1,0:T(8,128)(2,1)S(1)}, bf16[256,896]{1,0:T(8,128)(2,1)S(1)}, u32[]{:S(2)}, u32[]{:S(2)}) collective-permute-start(bf16[256,896]{1,0:T(8,128)(2,1)S(1)} %collective-permute-done.39.rest_3_), channel_id=1, source_target_pairs={{0,2},{2,0},{4,6},{6,4},{1,3},{3,1},{5,7},{7,5},{8,10},{10,8},{12,... | collective-permute-start | bytes 1376264 | tf_op jit(solution)/shard_map/ppermute | solution.py:597
  156.6 21.3 %collective-permute-start.44 = (bf16[128,2048]{1,0:T(8,128)(2,1)S(1)}, bf16[128,2048]{1,0:T(8,128)(2,1)S(1)}, u32[]{:S(2)}, u32[]{:S(2)}) collective-permute-start(bf16[128,2048]{1,0:T(8,128)(2,1)S(1)} %get-tuple-element.55), channel_id=1, source_target_pairs={{0,2},{2,0},{4,6},{6,4},{1,3},{3,1},{5,7},{7,5},{8,10},{10,8},{12,... | collective-permute-start | bytes 1572872 | tf_op jit(solution)/shard_map/ppermute | solution.py:597
  157.7 20.4 %collective-permute-start.45 = (bf16[128,2048]{1,0:T(8,128)(2,1)S(1)}, bf16[128,2048]{1,0:T(8,128)(2,1)S(1)}, u32[]{:S(2)}, u32[]{:S(2)}) collective-permute-start(bf16[128,2048]{1,0:T(8,128)(2,1)S(1)} %get-tuple-element.56), channel_id=1, source_target_pairs={{0,4},{2,6},{4,0},{6,2},{1,5},{3,7},{5,1},{7,3},{8,12},{10,14},{12... | collective-permute-start | bytes 1572872 | tf_op jit(solution)/shard_map/ppermute | solution.py:597
  174.1 15.1 %collective-permute-start.46 = (bf16[128,2048]{1,0:T(8,128)(2,1)S(1)}, bf16[128,2048]{1,0:T(8,128)(2,1)S(1)}, u32[]{:S(2)}, u32[]{:S(2)}) collective-permute-start(bf16[128,2048]{1,0:T(8,128)(2,1)S(1)} %get-tuple-element.57), channel_id=1, source_target_pairs={{0,2},{2,0},{4,6},{6,4},{1,3},{3,1},{5,7},{7,5},{8,10},{10,8},{12,... | collective-permute-start | bytes 1572872 | tf_op jit(solution)/shard_map/ppermute | solution.py:597
  174.2 15.1 %collective-permute-start.47 = (bf16[128,2048]{1,0:T(8,128)(2,1)S(1)}, bf16[128,2048]{1,0:T(8,128)(2,1)S(1)}, u32[]{:S(2)}, u32[]{:S(2)}) collective-permute-start(bf16[128,2048]{1,0:T(8,128)(2,1)S(1)} %get-tuple-element.58), channel_id=1, source_target_pairs={{0,4},{2,6},{4,0},{6,2},{1,5},{3,7},{5,1},{7,3},{8,12},{10,14},{12... | collective-permute-start | bytes 1572872 | tf_op jit(solution)/shard_map/ppermute | solution.py:597
  178.0 16.6 %collective-permute-start.48 = (bf16[128,1024]{1,0:T(8,128)(2,1)S(1)}, bf16[128,1024]{1,0:T(8,128)(2,1)S(1)}, u32[]{:S(2)}, u32[]{:S(2)}) collective-permute-start(bf16[128,1024]{1,0:T(8,128)(2,1)S(1)} %add_convert_fusion.3), channel_id=1, source_target_pairs={{0,4},{2,6},{4,0},{6,2},{1,5},{3,7},{5,1},{7,3},{8,12},{10,14},{12... | collective-permute-start | bytes 786440 | tf_op jit(solution)/shard_map/ppermute | solution.py:597
  178.2 16.4 %collective-permute-start.49 = (bf16[128,1024]{1,0:T(8,128)(2,1)S(1)}, bf16[128,1024]{1,0:T(8,128)(2,1)S(1)}, u32[]{:S(2)}, u32[]{:S(2)}) collective-permute-start(bf16[128,1024]{1,0:T(8,128)(2,1)S(1)} %add_convert_fusion.2), channel_id=1, source_target_pairs={{0,2},{2,0},{4,6},{6,4},{1,3},{3,1},{5,7},{7,5},{8,10},{10,8},{12,... | collective-permute-start | bytes 786440 | tf_op jit(solution)/shard_map/ppermute | solution.py:597
  (42 other events, 521.8 us)

commit v3 on v2

--- a/solution.py
+++ b/solution.py
@@ -410,17 +410,20 @@
     attend_many(units, scores, weights)
 
 
-def cross_kernel(n_span, total, source, within, own, from_x, from_y, last_y, last_x, *rest):
-    pieces = rest[1:5]
-    middle, across, held, context, asking, scores, weights, sem_w = rest[5:]
-    copies = load_pieces(n_span, 0, pieces, held, sem_w, begin=total - 4, total=total)
-    for c in copies:
-        c.start()
-    breadth = source.shape[1]
+def sums_kernel(own, from_x, from_y, last_y, last_x, context):
     for i, (near, far) in enumerate(((from_x, last_y), (from_y, last_x))):
         at = slice(i * SPAN_LEN, (i + 1) * SPAN_LEN)
         sums = own[at, :].astype(jnp.float32) + near[:SPAN_LEN, :].astype(jnp.float32)
         context[at, :] = (sums + far[...].astype(jnp.float32)).astype(jnp.bfloat16)
+
+
+def cross_kernel(n_span, total, source, within, context, *rest):
+    pieces = rest[1:5]
+    middle, across, held, asking, scores, weights, sem_w = rest[5:]
+    copies = load_pieces(n_span, 0, pieces, held, sem_w, begin=total - 4, total=total)
+    for c in copies:
+        c.start()
+    breadth = source.shape[1]
     for c in copies:
         c.wait()
     middle[...] = (
@@ -707,7 +710,20 @@
     last_y = add(for_y, from_x[SPAN_LEN:])
     last_x = add(for_x, from_y[SPAN_LEN:])
     last_y, last_x = to(2, last_y), to(1, last_x)
-    context = [own_c, from_x, from_y, last_y, last_x]
+    context = call(
+        sums_kernel,
+        pltpu.VMEM((rows_c, width_c), bf16),
+        [VMEM] * 5,
+        VMEM,
+        [],
+        16,
+        10**9,
+        own_c,
+        from_x,
+        from_y,
+        last_y,
+        last_x,
+    )
 
     half_t = tokens // 2
     s0, s1 = call(
@@ -779,10 +795,9 @@
     middle, across, _ = call(
         functools.partial(cross_kernel, n_span, n_pieces[1]),
         [pltpu.VMEM((rows_e, ENC_WIDTH), bf16)] * 2 + [pltpu.VMEM((ENC_WIDTH, widths[1]), bf16)],
-        [VMEM] * 8 + [HBM] * 4,
+        [VMEM] * 4 + [HBM] * 4,
         [VMEM] * 3,
         [
-            pltpu.VMEM((rows_c, width_c), bf16),
             pltpu.VMEM((rows_e, ENC_WIDTH), bf16),
             pltpu.VMEM((per * ENC_WIDTH, SPAN_LEN), jnp.float32),
             pltpu.VMEM((per * ENC_WIDTH, SPAN_LEN), bf16),
@@ -792,10 +807,10 @@
         4 * rows_e * ENC_WIDTH * widths[1],
         source,
         within,
-        *context,
+        context,
         held[1],
         *parts[1][-4:],
-        aliases={7: 2}.items(),
+        aliases={3: 2}.items(),
     )
     *enc, _ = call(
         functools.partial(encoded_kernel, n_span),

time: 200 us -> 205 us (1.025)
  starting transfers between devices: 42.5 us -> 48.5 us
  waiting for transfers between devices: 85.6 us -> 89.8 us
  local copies, waits for them, and re-layouts: 6.43 us -> 3.53 us
  Pallas kernels: 61.5 us -> 59.4 us
    ppermute x29, waiting for transfers between devices: 60.9 us -> 68.1 us  [to(): return lax.ppermute(value, 'head', [(i, i ^ k) for i in range(4)])]
    ppermute x10, starting transfers between devices: 6.59 us -> 10.3 us  [ring(): lax.ppermute(value, 'span', [(i, (i + 1) % n_span) for i in range(n_span)])]
    ppermute x10, waiting for transfers between devices: 24.7 us -> 21.7 us  [ring(): lax.ppermute(value, 'span', [(i, (i + 1) % n_span) for i in range(n_span)])]
    unnamed x45 -> x41, local copies, waits for them, and re-layouts: 6.43 us -> 3.53 us
    pallas_call x17 -> x18, Pallas kernels: 59.8 us -> 57.7 us  [call(): pl.pallas_call(kernel, out_shape=out_shape, in_specs=in_specs, out_specs=...]
  transfers between devices with their start and end apart: 52 -> 52, of which waited for: 21 -> 17; matrix products, arithmetic and copies ran while one was open for 2% -> 2% of each run, Pallas kernels for 29% -> 27%
where the time goes in v3:
time: 205 us; the launch traced here: 204 us
  waiting for transfers between devices  89.8 us (44%)
  Pallas kernels  59.4 us (29%)
  starting transfers between devices  48.5 us (24%)
  local copies, waits for them, and re-layouts  3.53 us (2%)
  other arithmetic  2.36 us (1%)
    ppermute x29, waiting for transfers between devices, to(): return lax.ppermute(value, 'head', [(i, i ^ k) for i in range(4)])  68.1 us
    pallas_call x18, Pallas kernels, call(): pl.pallas_call(kernel, out_shape=out_shape, in_specs=in_specs, out_specs=...  57.7 us
    ppermute x29, starting transfers between devices, to(): return lax.ppermute(value, 'head', [(i, i ^ k) for i in range(4)])  36.4 us
    ppermute x10, waiting for transfers between devices, ring(): lax.ppermute(value, 'span', [(i, (i + 1) % n_span) for i in range(n_span)])  21.7 us
    ppermute x10, starting transfers between devices, ring(): lax.ppermute(value, 'span', [(i, (i + 1) % n_span) for i in range(n_span)])  10.3 us
  transfers between devices with their start and end apart: 52, of which 17 were waited for; matrix products, arithmetic and copies ran while one was open for 2% of the time, Pallas kernels for 27%

profile of v3, /device:TPU:0, one launch (start us, length us, event | category | flops | bytes accessed | tf_op | source)
XLA Modules:
  0.0 204.2 jit_solution(679713827831875914)
XLA Ops:
  0.0 2.1 %shard_map.104 = (bf16[112,2688]{1,0:T(8,128)(2,1)}, bf16[112,896]{1,0:T(8,128)(2,1)}, bf16[112,896]{1,0:T(8,128)(2,1)}) custom-call(bf16[112,5376]{1,0:T(8,128)(2,1)} %rest_0_.5), custom_call_target="tpu_custom_call" | custom-call | flops 2000000000 | bytes 1204224 | tf_op jit(solution)/shard_map/pallas_call | solution.py:119
  2.1 3.1 %collective-permute-start.20 = (bf16[112,896]{1,0:T(8,128)(2,1)}, bf16[112,896]{1,0:T(8,128)(2,1)S(1)}, u32[]{:S(2)}, u32[]{:S(2)}) collective-permute-start(bf16[112,896]{1,0:T(8,128)(2,1)} %get-tuple-element.45), channel_id=1, source_target_pairs={{0,8},{8,16},{16,24},{24,0},{1,9},{9,17},{17,25},{25,1},{2,10},{10... | collective-permute-start | bytes 602120 | tf_op jit(solution)/shard_map/ppermute | solution.py:641
  10.1 3.2 %collective-permute-done.20.rest_2_ = bf16[112,896]{1,0:T(8,128)(2,1)S(1)} collective-permute-done((bf16[112,896]{1,0:T(8,128)(2,1)}, bf16[112,896]{1,0:T(8,128)(2,1)S(1)}, u32[]{:S(2)}, u32[]{:S(2)}) %collective-permute-start.20) | collective-permute-done | bytes 200736 | tf_op jit(solution)/shard_map/ppermute | solution.py:641
  13.3 3.5 %shard_map.102 = (bf16[2,128,896]{2,1,0:T(8,128)(2,1)}, bf16[2,128,896]{2,1,0:T(8,128)(2,1)}, bf16[2,128,896]{2,1,0:T(8,128)(2,1)}) custom-call(s32[8]{0:T(128)} %plan.1.assign, s32[2,8]{1,0:T(2,128)} %bitcast.11, s32[2,8]{1,0:T(2,128)} %bitcast.17, bf16[8,128,896]{2,1,0:T(8,128)(2,1)} %bitcast.15), custom_call_target="tpu_custom_call" | custom-call | flops 4000000000 | bytes 1835088 | tf_op jit(solution)/shard_map/pallas_call | solution.py:119
  16.8 1.7 collective-permute-start.6
  19.6 10.1 %collective-permute-done.32.rest_2_ = bf16[112,896]{1,0:T(8,128)(2,1)S(1)} collective-permute-done((bf16[112,896]{1,0:T(8,128)(2,1)}, bf16[112,896]{1,0:T(8,128)(2,1)S(1)}, u32[]{:S(2)}, u32[]{:S(2)}) %collective-permute-start.32) | collective-permute-done | bytes 200736 | tf_op jit(solution)/shard_map/ppermute | solution.py:641
  29.8 6.1 %shard_map.107 = (bf16[128,1792]{1,0:T(8,128)(2,1)}, bf16[128,1792]{1,0:T(8,128)(2,1)}, bf16[128,1792]{1,0:T(8,128)(2,1)}, bf16[64,1792]{1,0:T(8,128)(2,1)}, bf16[64,1792]{1,0:T(8,128)(2,1)}) custom-call(s32[8]{0:T(128)} %plan.1.assign, bf16[512,1024]{1,0:T(8,128)(2,1)} %states.3, bf16[1024,1792]{1,0:T(8,128)(2,1)} %w.3), custom_call_target="tpu_custom_call" | custom-call | flops 1879048192 | bytes 4718608 | tf_op jit(solution)/shard_map/pallas_call | solution.py:119
  40.5 2.3 %shard_map.100 = (bf16[256,1024]{1,0:T(8,128)(2,1)}, bf16[256,1024]{1,0:T(8,128)(2,1)}) custom-call(bf16[512,1024]{1,0:T(8,128)(2,1)} %states.3), custom_call_target="tpu_custom_call" | custom-call | flops 2000000000 | bytes 1048576 | tf_op jit(solution)/shard_map/pallas_call | solution.py:119
  45.3 13.5 %collective-permute-done.7.r2 = bf16[2,128,896]{2,1,0:T(8,128)(2,1)S(1)} collective-permute-done((bf16[2,128,896]{2,1,0:T(8,128)(2,1)}, bf16[2,128,896]{2,1,0:T(8,128)(2,1)S(1)}, u32[]{:S(2)}, u32[]{:S(2)}) %collective-permute-start.7) | collective-permute-done | bytes 458784 | tf_op jit(solution)/shard_map/ppermute | solution.py:600
  62.6 9.4 %collective-permute-done.17.from_y = bf16[128,1792]{1,0:T(8,128)(2,1)S(1)} collective-permute-done((bf16[128,1792]{1,0:T(8,128)(2,1)}, bf16[128,1792]{1,0:T(8,128)(2,1)S(1)}, u32[]{:S(2)}, u32[]{:S(2)}) %collective-permute-start.17) | collective-permute-done | bytes 458784 | tf_op jit(solution)/shard_map/ppermute | solution.py:600
  77.2 4.3 %collective-permute-done.24.rest_6_ = bf16[112,896]{1,0:T(8,128)(2,1)S(1)} collective-permute-done((bf16[112,896]{1,0:T(8,128)(2,1)S(1)}, bf16[112,896]{1,0:T(8,128)(2,1)S(1)}, u32[]{:S(2)}, u32[]{:S(2)}) %collective-permute-start.24) | collective-permute-done | bytes 200736 | tf_op jit(solution)/shard_map/ppermute | solution.py:641
  83.6 5.3 %collective-permute-done.19.last_x = bf16[64,1792]{1,0:T(8,128)(2,1)S(1)} collective-permute-done((bf16[64,1792]{1,0:T(8,128)(2,1)S(1)}, bf16[64,1792]{1,0:T(8,128)(2,1)S(1)}, u32[]{:S(2)}, u32[]{:S(2)}) %collective-permute-start.19) | collective-permute-done | bytes 229408 | tf_op jit(solution)/shard_map/ppermute | solution.py:600
  89.4 2.4 %collective-permute-done.26.rest_8_ = bf16[112,896]{1,0:T(8,128)(2,1)S(1)} collective-permute-done((bf16[112,896]{1,0:T(8,128)(2,1)S(1)}, bf16[112,896]{1,0:T(8,128)(2,1)S(1)}, u32[]{:S(2)}, u32[]{:S(2)}) %collective-permute-start.26) | collective-permute-done | bytes 200736 | tf_op jit(solution)/shard_map/ppermute | solution.py:600
  93.3 1.9 shard_map.103.source
  95.3 4.1 %collective-permute-done.28.rest_1_ = bf16[112,896]{1,0:T(8,128)(2,1)S(1)} collective-permute-done((bf16[112,896]{1,0:T(8,128)(2,1)S(1)}, bf16[112,896]{1,0:T(8,128)(2,1)S(1)}, u32[]{:S(2)}, u32[]{:S(2)}) %collective-permute-start.28) | collective-permute-done | bytes 200736 | tf_op jit(solution)/shard_map/ppermute | solution.py:641
  100.1 1.8 collective-permute-start.3
  105.0 9.0 %collective-permute-done.3.y1 = bf16[256,1024]{1,0:T(8,128)(2,1)S(1)} collective-permute-done((bf16[256,1024]{1,0:T(8,128)(2,1)S(1)}, bf16[256,1024]{1,0:T(8,128)(2,1)S(1)}, u32[]{:S(2)}, u32[]{:S(2)}) %collective-permute-start.3) | collective-permute-done | bytes 524320 | tf_op jit(solution)/shard_map/ppermute | solution.py:600
  118.0 4.8 %shard_map.106 = (bf16[512,896]{1,0:T(8,128)(2,1)S(1)}, bf16[896,2688]{1,0:T(8,128)(2,1)S(1)}) custom-call(bf16[512,896]{1,0:T(8,128)(2,1)S(1)} %shard_map.103.source, bf16[896,2688]{1,0:T(8,128)(2,1)S(1)} %shard_map.105.early, bf16[112,2688]{1,0:T(8,128)(2,1)S(1)} %collective-permute-done.14.own, ...), custom_call_target="tpu_custom_call", output_to_operand_aliasing={{1}: (1, {})} | custom-call | flops 4932501504 | bytes 6938624 | tf_op jit(solution)/shard_map/pallas_call | solution.py:119
  123.4 3.3 %shard_map.110 = (bf16[512,896]{1,0:T(8,128)(2,1)S(1)}, bf16[512,896]{1,0:T(8,128)(2,1)S(1)}, bf16[896,1792]{1,0:T(8,128)(2,1)S(1)}) custom-call(bf16[512,896]{1,0:T(8,128)(2,1)S(1)} %shard_map.103.source, bf16[512,896]{1,0:T(8,128)(2,1)S(1)} %get-tuple-element.39.within, bf16[128,1792]{1,0:T(8,128)(2,1)S(1)} %shard_map.108.context, ...), custom_call_target="tpu_custom_call", output_to_operand_aliasing={{2}: (3, {})} | custom-call | flops 3288334336 | bytes 6307840 | tf_op jit(solution)/shard_map/pallas_call | solution.py:119
  126.8 1.8 shard_map.112
  130.1 1.7 collective-permute-start.39
  133.2 8.3 %collective-permute-done.4.d0 = bf16[256,1024]{1,0:T(8,128)(2,1)S(1)} collective-permute-done((bf16[256,1024]{1,0:T(8,128)(2,1)S(1)}, bf16[256,1024]{1,0:T(8,128)(2,1)S(1)}, u32[]{:S(2)}, u32[]{:S(2)}) %collective-permute-start.4) | collective-permute-done | bytes 524320 | tf_op jit(solution)/shard_map/ppermute | solution.py:600
  141.5 5.5 %shard_map.101.queries = bf16[512,1024]{1,0:T(8,128)(2,1)S(1)} custom-call(bf16[512,1024]{1,0:T(8,128)(2,1)S(1)} %copy-done.1, bf16[256,1024]{1,0:T(8,128)(2,1)S(1)} %collective-permute-done.x0, bf16[256,1024]{1,0:T(8,128)(2,1)S(1)} %collective-permute-done.1.x1, bf16[256,1024]{1,0:T(8,128)(2,1)S(1)} %collective-permute-done.2.y0, ...), custom_call_target="tpu_custom_call" | custom-call | flops 4294967296 | bytes 12582912 | tf_op jit(solution)/shard_map/pallas_call | solution.py:119
  147.0 1.8 collective-permute-start.42
  149.3 2.2 %collective-permute-start.40 = (bf16[256,896]{1,0:T(8,128)(2,1)S(1)}, bf16[256,896]{1,0:T(8,128)(2,1)S(1)}, u32[]{:S(2)}, u32[]{:S(2)}) collective-permute-start(bf16[256,896]{1,0:T(8,128)(2,1)S(1)} %collective-permute-done.38.rest_1_), channel_id=1, source_target_pairs={{0,4},{2,6},{4,0},{6,2},{1,5},{3,7},{5,1},{7,3},{8,12},{10,14},{12... | collective-permute-start | bytes 1376264 | tf_op jit(solution)/shard_map/ppermute | solution.py:600
  153.0 9.7 %shard_map.113 = (bf16[128,2048]{1,0:T(8,128)(2,1)S(1)}, bf16[128,2048]{1,0:T(8,128)(2,1)S(1)}, bf16[128,2048]{1,0:T(8,128)(2,1)S(1)}, bf16[128,2048]{1,0:T(8,128)(2,1)S(1)}) custom-call(s32[8]{0:T(128)S(1)} %copy-done.2, bf16[512,1024]{1,0:T(8,128)(2,1)S(1)} %shard_map.101.queries, bf16[256,896]{1,0:T(8,128)(2,1)S(1)} %get-tuple-element.49.rest_0_, ...), custom_call_target="tpu_custom_call" | custom-call | flops 7516192768 | bytes 14942224 | tf_op jit(solution)/shard_map/pallas_call | solution.py:119
  164.8 4.1 %shard_map.114.rest_2_ = bf16[128,1024]{1,0:T(8,128)(2,1)S(1)} custom-call(s32[8]{0:T(128)S(1)} %copy-done.2, bf16[512,1024]{1,0:T(8,128)(2,1)S(1)} %shard_map.101.queries, bf16[256,896]{1,0:T(8,128)(2,1)S(1)} %collective-permute-done.42.rest_0_, bf16[256,896]{1,0:T(8,128)(2,1)S(1)} %collective-permute-done.43.rest_1_, bf16[896,2048]{1,0:T(8,128)(2,1)S(1)} %bitcast.6), custom_call_target="tpu_custom_call" | custom-call | flops 3758096384 | bytes 5636112 | tf_op jit(solution)/shard_map/pallas_call | solution.py:119
  169.0 2.0 collective-permute-done.40.rest_0_
  172.0 6.7 %shard_map.115 = (bf16[128,2048]{1,0:T(8,128)(2,1)S(1)}, bf16[128,2048]{1,0:T(8,128)(2,1)S(1)}, bf16[128,2048]{1,0:T(8,128)(2,1)S(1)}, bf16[128,2048]{1,0:T(8,128)(2,1)S(1)}) custom-call(s32[8]{0:T(128)S(1)} %copy-done.2, bf16[512,1024]{1,0:T(8,128)(2,1)S(1)} %shard_map.101.queries, bf16[256,896]{1,0:T(8,128)(2,1)S(1)} %collective-permute-done.40.rest_0_, ...), custom_call_target="tpu_custom_call" | custom-call | flops 3758096384 | bytes 14286864 | tf_op jit(solution)/shard_map/pallas_call | solution.py:119
  181.6 1.8 collective-permute-start.48
  184.4 9.2 %collective-permute-done.46.rest_6_ = bf16[128,2048]{1,0:T(8,128)(2,1)S(1)} collective-permute-done((bf16[128,2048]{1,0:T(8,128)(2,1)S(1)}, bf16[128,2048]{1,0:T(8,128)(2,1)S(1)}, u32[]{:S(2)}, u32[]{:S(2)}) %collective-permute-start.46) | collective-permute-done | bytes 524320 | tf_op jit(solution)/shard_map/ppermute | solution.py:600
  195.7 4.0 %collective-permute-done.48.rest_8_ = bf16[128,1024]{1,0:T(8,128)(2,1)S(1)} collective-permute-done((bf16[128,1024]{1,0:T(8,128)(2,1)S(1)}, bf16[128,1024]{1,0:T(8,128)(2,1)S(1)}, u32[]{:S(2)}, u32[]{:S(2)}) %collective-permute-start.48) | collective-permute-done | bytes 262176 | tf_op jit(solution)/shard_map/ppermute | solution.py:600
  (141 shorter events, 52.9 us)
Async XLA Ops:
  5.3 38.8 %collective-permute-start.10 = (bf16[112,2688]{1,0:T(8,128)(2,1)}, bf16[112,2688]{1,0:T(8,128)(2,1)S(1)}, u32[]{:S(2)}, u32[]{:S(2)}) collective-permute-start(bf16[112,2688]{1,0:T(8,128)(2,1)} %get-tuple-element.38), channel_id=1, source_target_pairs={{0,8},{8,16},{16,24},{24,0},{1,9},{9,17},{17,25},{25,1},{2,10},{10... | collective-permute-start | bytes 1806344 | tf_op jit(solution)/shard_map/ppermute | solution.py:641
  6.8 22.9 %collective-permute-start.32 = (bf16[112,896]{1,0:T(8,128)(2,1)}, bf16[112,896]{1,0:T(8,128)(2,1)S(1)}, u32[]{:S(2)}, u32[]{:S(2)}) collective-permute-start(bf16[112,896]{1,0:T(8,128)(2,1)} %get-tuple-element.48), channel_id=1, source_target_pairs={{0,8},{8,16},{16,24},{24,0},{1,9},{9,17},{17,25},{25,1},{2,10},{10... | collective-permute-start | bytes 602120 | tf_op jit(solution)/shard_map/ppermute | solution.py:641
  13.3 16.4 %collective-permute-start.21 = (bf16[112,896]{1,0:T(8,128)(2,1)S(1)}, bf16[112,896]{1,0:T(8,128)(2,1)S(1)}, u32[]{:S(2)}, u32[]{:S(2)}) collective-permute-start(bf16[112,896]{1,0:T(8,128)(2,1)S(1)} %collective-permute-done.20.rest_2_), channel_id=1, source_target_pairs={{0,1},{1,0},{2,3},{3,2},{4,5},{5,4},{6,7},{7,6},{8,9},{9,8},{10,11... | collective-permute-start | bytes 602120 | tf_op jit(solution)/shard_map/ppermute | solution.py:644
  16.8 26.0 %collective-permute-start.6 = (bf16[2,128,896]{2,1,0:T(8,128)(2,1)}, bf16[2,128,896]{2,1,0:T(8,128)(2,1)S(1)}, u32[]{:S(2)}, u32[]{:S(2)}) collective-permute-start(bf16[2,128,896]{2,1,0:T(8,128)(2,1)} %get-tuple-element.35), channel_id=1, source_target_pairs={{0,2},{2,0},{4,6},{6,4},{1,3},{3,1},{5,7},{7,5},{8,10},{10,8},{12,... | collective-permute-start | bytes 1376264 | tf_op jit(solution)/shard_map/ppermute | solution.py:600
  18.5 17.3 %collective-permute-start.22 = (bf16[112,896]{1,0:T(8,128)(2,1)S(1)}, bf16[112,896]{1,0:T(8,128)(2,1)S(1)}, u32[]{:S(2)}, u32[]{:S(2)}) collective-permute-start(bf16[112,896]{1,0:T(8,128)(2,1)S(1)} %collective-permute-done.20.rest_2_), channel_id=1, source_target_pairs={{0,4},{2,6},{4,0},{6,2},{1,5},{3,7},{5,1},{7,3},{8,12},{10,14},{12... | collective-permute-start | bytes 602120 | tf_op jit(solution)/shard_map/ppermute | solution.py:600
  35.9 23.0 %collective-permute-start.7 = (bf16[2,128,896]{2,1,0:T(8,128)(2,1)}, bf16[2,128,896]{2,1,0:T(8,128)(2,1)S(1)}, u32[]{:S(2)}, u32[]{:S(2)}) collective-permute-start(bf16[2,128,896]{2,1,0:T(8,128)(2,1)} %get-tuple-element.36), channel_id=1, source_target_pairs={{0,4},{2,6},{4,0},{6,2},{1,5},{3,7},{5,1},{7,3},{8,12},{10,14},{12... | collective-permute-start | bytes 1376264 | tf_op jit(solution)/shard_map/ppermute | solution.py:600
  38.2 20.7 %collective-permute-start.8 = (bf16[2,128,896]{2,1,0:T(8,128)(2,1)}, bf16[2,128,896]{2,1,0:T(8,128)(2,1)S(1)}, u32[]{:S(2)}, u32[]{:S(2)}) collective-permute-start(bf16[2,128,896]{2,1,0:T(8,128)(2,1)} %get-tuple-element.37), channel_id=1, source_target_pairs={{0,6},{2,4},{4,2},{6,0},{1,7},{3,5},{5,3},{7,1},{8,14},{10,12},{12... | collective-permute-start | bytes 1376264 | tf_op jit(solution)/shard_map/ppermute | solution.py:600
  39.6 22.0 %collective-permute-start.16 = (bf16[128,1792]{1,0:T(8,128)(2,1)}, bf16[128,1792]{1,0:T(8,128)(2,1)S(1)}, u32[]{:S(2)}, u32[]{:S(2)}) collective-permute-start(bf16[128,1792]{1,0:T(8,128)(2,1)} %get-tuple-element.41), channel_id=1, source_target_pairs={{0,2},{2,0},{4,6},{6,4},{1,3},{3,1},{5,7},{7,5},{8,10},{10,8},{12,... | collective-permute-start | bytes 1376264 | tf_op jit(solution)/shard_map/ppermute | solution.py:600
  42.8 30.1 %collective-permute-start = (bf16[256,1024]{1,0:T(8,128)(2,1)}, bf16[256,1024]{1,0:T(8,128)(2,1)S(1)}, u32[]{:S(2)}, u32[]{:S(2)}) collective-permute-start(bf16[256,1024]{1,0:T(8,128)(2,1)} %get-tuple-element.33), channel_id=1, source_target_pairs={{0,2},{2,0},{4,6},{6,4},{1,3},{3,1},{5,7},{7,5},{8,10},{10,8},{12,... | collective-permute-start | bytes 1572872 | tf_op jit(solution)/shard_map/ppermute | solution.py:600
  44.1 30.5 %collective-permute-start.12 = (bf16[112,2688]{1,0:T(8,128)(2,1)S(1)}, bf16[112,2688]{1,0:T(8,128)(2,1)S(1)}, u32[]{:S(2)}, u32[]{:S(2)}) collective-permute-start(bf16[112,2688]{1,0:T(8,128)(2,1)S(1)} %collective-permute-done.10.rest_2_), channel_id=1, source_target_pairs={{0,8},{8,16},{16,24},{24,0},{1,9},{9,17},{17,25},{25,1},{2,10},{10... | collective-permute-start | bytes 1806344 | tf_op jit(solution)/shard_map/ppermute | solution.py:641
  58.9 41.1 %collective-permute-start.9 = (bf16[112,5376]{1,0:T(8,128)(2,1)S(1)}, bf16[112,5376]{1,0:T(8,128)(2,1)S(1)}, u32[]{:S(2)}, u32[]{:S(2)}) collective-permute-start(bf16[112,5376]{1,0:T(8,128)(2,1)S(1)} %copy-done), channel_id=1, source_target_pairs={{0,1},{1,0},{2,3},{3,2},{4,5},{5,4},{6,7},{7,6},{8,9},{9,8},{10,11... | collective-permute-start | bytes 3612680 | tf_op jit(solution)/shard_map/ppermute | solution.py:644
  74.6 24.8 %collective-permute-start.14 = (bf16[112,2688]{1,0:T(8,128)(2,1)S(1)}, bf16[112,2688]{1,0:T(8,128)(2,1)S(1)}, u32[]{:S(2)}, u32[]{:S(2)}) collective-permute-start(bf16[112,2688]{1,0:T(8,128)(2,1)S(1)} %collective-permute-done.12.rest_4_), channel_id=1, source_target_pairs={{0,8},{8,16},{16,24},{24,0},{1,9},{9,17},{17,25},{25,1},{2,10},{10... | collective-permute-start | bytes 1806344 | tf_op jit(solution)/shard_map/ppermute | solution.py:641
  88.9 14.5 %collective-permute-start.11 = (bf16[112,2688]{1,0:T(8,128)(2,1)S(1)}, bf16[112,2688]{1,0:T(8,128)(2,1)S(1)}, u32[]{:S(2)}, u32[]{:S(2)}) collective-permute-start(bf16[112,2688]{1,0:T(8,128)(2,1)S(1)} %collective-permute-done.10.rest_2_), channel_id=1, source_target_pairs={{0,1},{1,0},{2,3},{3,2},{4,5},{5,4},{6,7},{7,6},{8,9},{9,8},{10,11... | collective-permute-start | bytes 1806344 | tf_op jit(solution)/shard_map/ppermute | solution.py:644
  88.9 14.8 %collective-permute-start.13 = (bf16[112,2688]{1,0:T(8,128)(2,1)S(1)}, bf16[112,2688]{1,0:T(8,128)(2,1)S(1)}, u32[]{:S(2)}, u32[]{:S(2)}) collective-permute-start(bf16[112,2688]{1,0:T(8,128)(2,1)S(1)} %collective-permute-done.12.rest_4_), channel_id=1, source_target_pairs={{0,1},{1,0},{2,3},{3,2},{4,5},{5,4},{6,7},{7,6},{8,9},{9,8},{10,11... | collective-permute-start | bytes 1806344 | tf_op jit(solution)/shard_map/ppermute | solution.py:644
  99.3 18.7 %collective-permute-start.15 = (bf16[112,2688]{1,0:T(8,128)(2,1)S(1)}, bf16[112,2688]{1,0:T(8,128)(2,1)S(1)}, u32[]{:S(2)}, u32[]{:S(2)}) collective-permute-start(bf16[112,2688]{1,0:T(8,128)(2,1)S(1)} %collective-permute-done.14.own), channel_id=1, source_target_pairs={{0,1},{1,0},{2,3},{3,2},{4,5},{5,4},{6,7},{7,6},{8,9},{9,8},{10,11... | collective-permute-start | bytes 1806344 | tf_op jit(solution)/shard_map/ppermute | solution.py:644
  103.5 14.0 %collective-permute-start.30 = (bf16[112,896]{1,0:T(8,128)(2,1)S(1)}, bf16[112,896]{1,0:T(8,128)(2,1)S(1)}, u32[]{:S(2)}, u32[]{:S(2)}) collective-permute-start(bf16[112,896]{1,0:T(8,128)(2,1)S(1)} %collective-permute-done.26.rest_8_), channel_id=1, source_target_pairs={{0,8},{8,16},{16,24},{24,0},{1,9},{9,17},{17,25},{25,1},{2,10},{10... | collective-permute-start | bytes 602120 | tf_op jit(solution)/shard_map/ppermute | solution.py:641
  114.0 16.2 %collective-permute-start.1 = (bf16[256,1024]{1,0:T(8,128)(2,1)S(1)}, bf16[256,1024]{1,0:T(8,128)(2,1)S(1)}, u32[]{:S(2)}, u32[]{:S(2)}) collective-permute-start(bf16[256,1024]{1,0:T(8,128)(2,1)S(1)} %copy-done.15), channel_id=1, source_target_pairs={{0,2},{2,0},{4,6},{6,4},{1,3},{3,1},{5,7},{7,5},{8,10},{10,8},{12,... | collective-permute-start | bytes 1572872 | tf_op jit(solution)/shard_map/ppermute | solution.py:600
  115.5 17.7 %collective-permute-start.2 = (bf16[256,1024]{1,0:T(8,128)(2,1)S(1)}, bf16[256,1024]{1,0:T(8,128)(2,1)S(1)}, u32[]{:S(2)}, u32[]{:S(2)}) collective-permute-start(bf16[256,1024]{1,0:T(8,128)(2,1)S(1)} %copy-done.14), channel_id=1, source_target_pairs={{0,4},{2,6},{4,0},{6,2},{1,5},{3,7},{5,1},{7,3},{8,12},{10,14},{12... | collective-permute-start | bytes 1572872 | tf_op jit(solution)/shard_map/ppermute | solution.py:600
  117.2 24.3 %collective-permute-start.4 = (bf16[256,1024]{1,0:T(8,128)(2,1)S(1)}, bf16[256,1024]{1,0:T(8,128)(2,1)S(1)}, u32[]{:S(2)}, u32[]{:S(2)}) collective-permute-start(bf16[256,1024]{1,0:T(8,128)(2,1)S(1)} %collective-permute-done.x0), channel_id=1, source_target_pairs={{0,4},{2,6},{4,0},{6,2},{1,5},{3,7},{5,1},{7,3},{8,12},{10,14},{12... | collective-permute-start | bytes 1572872 | tf_op jit(solution)/shard_map/ppermute | solution.py:600
  117.5 24.0 %collective-permute-start.5 = (bf16[256,1024]{1,0:T(8,128)(2,1)S(1)}, bf16[256,1024]{1,0:T(8,128)(2,1)S(1)}, u32[]{:S(2)}, u32[]{:S(2)}) collective-permute-start(bf16[256,1024]{1,0:T(8,128)(2,1)S(1)} %collective-permute-done.3.y1), channel_id=1, source_target_pairs={{0,2},{2,0},{4,6},{6,4},{1,3},{3,1},{5,7},{7,5},{8,10},{10,8},{12,... | collective-permute-start | bytes 1572872 | tf_op jit(solution)/shard_map/ppermute | solution.py:600
  128.6 20.8 %collective-permute-start.38 = (bf16[256,896]{1,0:T(8,128)(2,1)S(1)}, bf16[256,896]{1,0:T(8,128)(2,1)S(1)}, u32[]{:S(2)}, u32[]{:S(2)}) collective-permute-start(bf16[256,896]{1,0:T(8,128)(2,1)S(1)} %get-tuple-element.49.rest_0_), channel_id=1, source_target_pairs={{0,2},{2,0},{4,6},{6,4},{1,3},{3,1},{5,7},{7,5},{8,10},{10,8},{12,... | collective-permute-start | bytes 1376264 | tf_op jit(solution)/shard_map/ppermute | solution.py:600
  130.1 21.4 %collective-permute-start.39 = (bf16[256,896]{1,0:T(8,128)(2,1)S(1)}, bf16[256,896]{1,0:T(8,128)(2,1)S(1)}, u32[]{:S(2)}, u32[]{:S(2)}) collective-permute-start(bf16[256,896]{1,0:T(8,128)(2,1)S(1)} %get-tuple-element.50.rest_2_), channel_id=1, source_target_pairs={{0,4},{2,6},{4,0},{6,2},{1,5},{3,7},{5,1},{7,3},{8,12},{10,14},{12... | collective-permute-start | bytes 1376264 | tf_op jit(solution)/shard_map/ppermute | solution.py:600
  147.0 16.3 %collective-permute-start.42 = (bf16[256,896]{1,0:T(8,128)(2,1)S(1)}, bf16[256,896]{1,0:T(8,128)(2,1)S(1)}, u32[]{:S(2)}, u32[]{:S(2)}) collective-permute-start(bf16[256,896]{1,0:T(8,128)(2,1)S(1)} %get-tuple-element.49.rest_0_), channel_id=1, source_target_pairs={{0,4},{2,6},{4,0},{6,2},{1,5},{3,7},{5,1},{7,3},{8,12},{10,14},{12... | collective-permute-start | bytes 1376264 | tf_op jit(solution)/shard_map/ppermute | solution.py:600
  148.8 16.0 %collective-permute-start.43 = (bf16[256,896]{1,0:T(8,128)(2,1)S(1)}, bf16[256,896]{1,0:T(8,128)(2,1)S(1)}, u32[]{:S(2)}, u32[]{:S(2)}) collective-permute-start(bf16[256,896]{1,0:T(8,128)(2,1)S(1)} %get-tuple-element.50.rest_2_), channel_id=1, source_target_pairs={{0,2},{2,0},{4,6},{6,4},{1,3},{3,1},{5,7},{7,5},{8,10},{10,8},{12,... | collective-permute-start | bytes 1376264 | tf_op jit(solution)/shard_map/ppermute | solution.py:600
  149.3 21.6 %collective-permute-start.40 = (bf16[256,896]{1,0:T(8,128)(2,1)S(1)}, bf16[256,896]{1,0:T(8,128)(2,1)S(1)}, u32[]{:S(2)}, u32[]{:S(2)}) collective-permute-start(bf16[256,896]{1,0:T(8,128)(2,1)S(1)} %collective-permute-done.38.rest_1_), channel_id=1, source_target_pairs={{0,4},{2,6},{4,0},{6,2},{1,5},{3,7},{5,1},{7,3},{8,12},{10,14},{12... | collective-permute-start | bytes 1376264 | tf_op jit(solution)/shard_map/ppermute | solution.py:600
  151.5 20.5 %collective-permute-start.41 = (bf16[256,896]{1,0:T(8,128)(2,1)S(1)}, bf16[256,896]{1,0:T(8,128)(2,1)S(1)}, u32[]{:S(2)}, u32[]{:S(2)}) collective-permute-start(bf16[256,896]{1,0:T(8,128)(2,1)S(1)} %collective-permute-done.39.rest_3_), channel_id=1, source_target_pairs={{0,2},{2,0},{4,6},{6,4},{1,3},{3,1},{5,7},{7,5},{8,10},{10,8},{12,... | collective-permute-start | bytes 1376264 | tf_op jit(solution)/shard_map/ppermute | solution.py:600
  162.7 18.8 %collective-permute-start.44 = (bf16[128,2048]{1,0:T(8,128)(2,1)S(1)}, bf16[128,2048]{1,0:T(8,128)(2,1)S(1)}, u32[]{:S(2)}, u32[]{:S(2)}) collective-permute-start(bf16[128,2048]{1,0:T(8,128)(2,1)S(1)} %get-tuple-element.55), channel_id=1, source_target_pairs={{0,2},{2,0},{4,6},{6,4},{1,3},{3,1},{5,7},{7,5},{8,10},{10,8},{12,... | collective-permute-start | bytes 1572872 | tf_op jit(solution)/shard_map/ppermute | solution.py:600
  163.3 20.1 %collective-permute-start.45 = (bf16[128,2048]{1,0:T(8,128)(2,1)S(1)}, bf16[128,2048]{1,0:T(8,128)(2,1)S(1)}, u32[]{:S(2)}, u32[]{:S(2)}) collective-permute-start(bf16[128,2048]{1,0:T(8,128)(2,1)S(1)} %get-tuple-element.56), channel_id=1, source_target_pairs={{0,4},{2,6},{4,0},{6,2},{1,5},{3,7},{5,1},{7,3},{8,12},{10,14},{12... | collective-permute-start | bytes 1572872 | tf_op jit(solution)/shard_map/ppermute | solution.py:600
  178.7 14.9 %collective-permute-start.46 = (bf16[128,2048]{1,0:T(8,128)(2,1)S(1)}, bf16[128,2048]{1,0:T(8,128)(2,1)S(1)}, u32[]{:S(2)}, u32[]{:S(2)}) collective-permute-start(bf16[128,2048]{1,0:T(8,128)(2,1)S(1)} %get-tuple-element.57), channel_id=1, source_target_pairs={{0,2},{2,0},{4,6},{6,4},{1,3},{3,1},{5,7},{7,5},{8,10},{10,8},{12,... | collective-permute-start | bytes 1572872 | tf_op jit(solution)/shard_map/ppermute | solution.py:600
  179.3 15.3 %collective-permute-start.47 = (bf16[128,2048]{1,0:T(8,128)(2,1)S(1)}, bf16[128,2048]{1,0:T(8,128)(2,1)S(1)}, u32[]{:S(2)}, u32[]{:S(2)}) collective-permute-start(bf16[128,2048]{1,0:T(8,128)(2,1)S(1)} %get-tuple-element.58), channel_id=1, source_target_pairs={{0,4},{2,6},{4,0},{6,2},{1,5},{3,7},{5,1},{7,3},{8,12},{10,14},{12... | collective-permute-start | bytes 1572872 | tf_op jit(solution)/shard_map/ppermute | solution.py:600
  181.6 18.1 %collective-permute-start.48 = (bf16[128,1024]{1,0:T(8,128)(2,1)S(1)}, bf16[128,1024]{1,0:T(8,128)(2,1)S(1)}, u32[]{:S(2)}, u32[]{:S(2)}) collective-permute-start(bf16[128,1024]{1,0:T(8,128)(2,1)S(1)} %add_convert_fusion.3), channel_id=1, source_target_pairs={{0,4},{2,6},{4,0},{6,2},{1,5},{3,7},{5,1},{7,3},{8,12},{10,14},{12... | collective-permute-start | bytes 786440 | tf_op jit(solution)/shard_map/ppermute | solution.py:600
  183.5 16.3 %collective-permute-start.49 = (bf16[128,1024]{1,0:T(8,128)(2,1)S(1)}, bf16[128,1024]{1,0:T(8,128)(2,1)S(1)}, u32[]{:S(2)}, u32[]{:S(2)}) collective-permute-start(bf16[128,1024]{1,0:T(8,128)(2,1)S(1)} %add_convert_fusion.2), channel_id=1, source_target_pairs={{0,2},{2,0},{4,6},{6,4},{1,3},{3,1},{5,7},{7,5},{8,10},{10,8},{12,... | collective-permute-start | bytes 786440 | tf_op jit(solution)/shard_map/ppermute | solution.py:600
  (40 other events, 521.3 us)
